TPU v7x, 512 devices: a whole 4x8x8 slice. The times are simulated.
512 devices in a mesh: gx: 16 (over y, core), gy: 4 (over x), gz: 8 (over z).
Axes of the slice: x: 4, y: 8, z: 8, core: 2. Of those that a mesh axis runs over, the one named last changes fastest.
Arguments:
- fractions: float32 [3, 16, 8, 16, 128], P(None, 'gx', 'gy', 'gz'), may hold values from 0 to 1
- polarizability: float32 [16, 8, 16, 128], P('gx', 'gy', 'gz'), may hold values from 0.5 to 2
- occupancy: int32 [16, 8, 16, 128], P('gx', 'gy', 'gz'), may hold values 0 or 1
- pair_mask: int32 [16, 8, 16, 27], P('gx', 'gy', 'gz'), may hold values from 0 to 1, as said below
- perm_field: float32 [6, 16, 8, 16, 128], P(None, 'gx', 'gy', 'gz'), may hold values from -6 to 6
- history: float32 [6, 6, 16, 8, 16, 128], P(None, None, 'gx', 'gy', 'gz'), may hold values from -12 to 12
Outputs:
- induced: float32 [6, 16, 8, 16, 128], P(None, 'gx', 'gy', 'gz')
- change: float32 [], replicated
Inputs may be any that keep to these rules, and one draw needn't show every extreme that they name: pair_mask[t, k] equals pair_mask at tile t + offset(k) for the opposite offset 26 - k (periodic); pair_mask[t, 13] (the tile itself) is 1.
All inputs are finite; a program needn't handle non-finite values. No bound on the sum of `occupancy` on one device may be relied on, other than what follows from the above.
Results may differ from a plain program's by a relative error of at most 0.0003.
Values sent between devices are 32-bit elements; how exact they have to be, the bound alone decides.
No kernel may reach another device: no remote copies, remote signals or barrier semaphores. Data moves between devices by JAX's collectives and lax.ppermute only.
A program may use at most 64 MiB of HBM per device.

v0:
```python
import functools

import jax
import jax.numpy as jnp
from jax import lax
from jax.sharding import Mesh
from jax.sharding import PartitionSpec as P

GX_GY_GZ = ("gx_0", "gx_1", "gy", "gz")
GX = ("gx_0", "gx_1")


CELL_EDGE = 10.0
SOFTENING = 0.3
THOLE_DAMP = 0.39
RELAXATION = 0.7


def with_halo(cells, sides, width):
    for axis, dim in sides:
        count = lax.axis_size(axis)
        head = lax.slice_in_dim(cells, 0, width, axis=dim)
        tail = lax.slice_in_dim(cells, cells.shape[dim] - width, cells.shape[dim], axis=dim)
        cells = jnp.concatenate(
            [
                lax.ppermute(tail, axis, [(i, (i + 1) % count) for i in range(count)]),
                cells,
                lax.ppermute(head, axis, [((i + 1) % count, i) for i in range(count)]),
            ],
            axis=dim,
        )
    return cells


def one_axis_at_a_time(shard, axes):
    return functools.reduce(lax.psum, axes, shard)


def pair_field(target, source, moment, offset_vec, itself, allowed):
    displace = [
        (offset_vec[axis_num] + source[axis_num][:, None, :] - target[axis_num][:, :, None])
        * CELL_EDGE
        for axis_num in range(3)
    ]
    dist_sq = (
        displace[0] * displace[0]
        + displace[1] * displace[1]
        + displace[2] * displace[2]
        + SOFTENING
    )
    inv_cube = lax.rsqrt(dist_sq) / dist_sq
    thole_arg = (
        dist_sq * jnp.sqrt(dist_sq) * lax.rsqrt(target[3][:, :, None] * source[3][:, None, :])
    )
    damping = jnp.exp(-THOLE_DAMP * thole_arg)
    lambda_three = 1.0 - damping
    lambda_five = 1.0 - (1.0 + THOLE_DAMP * thole_arg) * damping
    slots = target.shape[-1]
    self_pair = jnp.logical_and(itself, jnp.eye(slots, dtype=bool))
    weight = jnp.where(self_pair, 0.0, allowed[:, None, None])
    radial = 3.0 * lambda_five * inv_cube / dist_sq * weight
    direct = lambda_three * inv_cube * weight
    fields = []
    for which_set in range(moment.shape[0] // 3):
        parts = [moment[3 * which_set + axis_num][:, None, :] for axis_num in range(3)]
        project = displace[0] * parts[0] + displace[1] * parts[1] + displace[2] * parts[2]
        for axis_num in range(3):
            fields.append(
                jnp.sum(radial * project * displace[axis_num] - direct * parts[axis_num], axis=-1)
            )
    return jnp.stack(fields)


def slab_field(geometry_pad, moment_pad, allowed_slab, slab_index):
    width_y = geometry_pad.shape[2] - 2
    width_z = geometry_pad.shape[3] - 2
    slots = geometry_pad.shape[4]
    rows = moment_pad.shape[0]
    zero = jnp.zeros((), jnp.int32)
    one = jnp.ones((), jnp.int32)
    first_x = (jnp.asarray(slab_index) + 1).astype(jnp.int32)
    target = lax.dynamic_slice(
        geometry_pad, (zero, first_x, one, one, zero), (4, 1, width_y, width_z, slots)
    ).reshape(4, width_y * width_z, slots)

    def offset_step(offset, summed):
        offset = jnp.asarray(offset).astype(jnp.int32)
        along_x = offset // 9 - 1
        along_y = offset // 3 % 3 - 1
        along_z = offset % 3 - 1
        starts = (zero, first_x + along_x, one + along_y, one + along_z, zero)
        source = lax.dynamic_slice(geometry_pad, starts, (4, 1, width_y, width_z, slots)).reshape(
            4, width_y * width_z, slots
        )
        moment = lax.dynamic_slice(moment_pad, starts, (rows, 1, width_y, width_z, slots)).reshape(
            rows, width_y * width_z, slots
        )
        allowed = (
            lax.dynamic_index_in_dim(allowed_slab, offset, 2, keepdims=False)
            .reshape(-1)
            .astype(jnp.float32)
        )
        offset_vec = jnp.stack([along_x, along_y, along_z]).astype(jnp.float32)
        return summed + pair_field(target, source, moment, offset_vec, offset == 13, allowed)

    summed = lax.fori_loop(
        0, 27, offset_step, jnp.zeros((rows, width_y * width_z, slots), jnp.float32)
    )
    return summed.reshape(rows, width_y, width_z, slots)


def device_field(geometry_pad, moment_pad, pair_mask):
    slabs = [slab_field(geometry_pad, moment_pad, pair_mask[0], 0)]
    return jnp.stack(slabs, 1)


def share_dipoles(dipoles):
    return with_halo(dipoles, ((GX, 1), ("gy", 2), ("gz", 3)), 1)


def global_gram(local_gram):
    return one_axis_at_a_time(local_gram, GX_GY_GZ)


def fit_coefficients(gram_matrix):
    past_count = gram_matrix.shape[0] - 1
    gram_past = gram_matrix[:past_count, :past_count]
    gram_next = gram_matrix[:past_count, past_count]
    ridge_term = 0.001 * jnp.trace(gram_past) / past_count + 1.0
    factor = jnp.linalg.cholesky(gram_past + ridge_term * jnp.eye(past_count, dtype=jnp.float32))
    return jax.scipy.linalg.cho_solve((factor, True), gram_next)


def on_device(fractions, polarizability, occupancy, pair_mask, perm_field, history):
    filled = occupancy.astype(jnp.float32)
    geometry = jnp.concatenate([fractions, polarizability[None]], 0)
    masked = history * filled
    past_sets = masked.shape[0]
    flat_hist = masked.reshape(past_sets, -1)
    local_gram = jnp.dot(flat_hist, flat_hist.T, precision=lax.Precision.HIGHEST)
    scaled = RELAXATION * filled * polarizability
    later = masked[1:]
    stacked = jnp.concatenate([geometry, later.reshape((-1,) + later.shape[2:])], 0)
    ghosts = with_halo(stacked, ((GX, 1), ("gy", 2), ("gz", 3)), 1)
    coeffs = fit_coefficients(global_gram(local_gram))
    geometry_pad = ghosts[:4]
    later_pad = ghosts[4:].reshape((past_sets - 1, 6) + ghosts.shape[1:])
    predicted_pad = jnp.tensordot(coeffs, later_pad, axes=1, precision=lax.Precision.HIGHEST)
    predicted = predicted_pad[:, 1:-1, 1:-1, 1:-1, :]
    field_one = device_field(geometry_pad, predicted_pad, pair_mask)
    dipole_one = (1.0 - RELAXATION) * predicted + scaled * (perm_field + field_one)
    field_two = device_field(geometry_pad, share_dipoles(dipole_one), pair_mask)
    induced = (1.0 - RELAXATION) * dipole_one + scaled * (perm_field + field_two)
    update = induced - dipole_one
    totals = (
        one_axis_at_a_time(jnp.sum(update * update), GX_GY_GZ),
        one_axis_at_a_time(jnp.sum(induced * induced), GX_GY_GZ),
    )
    change = jnp.sqrt(totals[0] / (totals[1] + 1.0))
    return (induced, change)


def solution(mesh):
    split = Mesh(
        mesh.devices.reshape(8, 2, mesh.shape["gy"], mesh.shape["gz"]), ("gx_0", "gx_1", "gy", "gz")
    )
    placed = (
        P(None, GX, "gy", "gz", None),
        P(GX, "gy", "gz", None),
        P(GX, "gy", "gz", None),
        P(GX, "gy", "gz", None),
        P(None, GX, "gy", "gz", None),
        P(None, None, GX, "gy", "gz", None),
    )
    return jax.shard_map(
        on_device,
        mesh=split,
        in_specs=placed,
        out_specs=(P(None, GX, "gy", "gz", None), P()),
        check_vma=False,
    )
```

profile of v0, /device:TPU:1, one launch (start us, length us, event | category | flops | bytes accessed | tf_op | source)
XLA Modules:
  0.0 427.0 jit_solution(18372942800853096347)
XLA Ops:
  3.0 2.7 collective-permute-start
  5.7 4.2 collective-permute-start.1
  11.1 13.4 %psum.84 = f32[6,6]{0,1:T(8,128)S(1)} all-reduce(f32[6,6]{0,1:T(8,128)S(1)} %convolution_bitcast_fusion), channel_id=1, replica_groups=mesh['gx_0'=8,'gx_1'=2,'gy'=4,'gz'=8] {'gx_0'}, use_global_device_ids=true, to_apply=%region_0.0 | all-reduce | flops 36 | bytes 288 | tf_op jit(solution)/shard_map/psum | solution.py:36
  24.5 5.9 %psum.85 = f32[6,6]{0,1:T(8,128)S(1)} all-reduce(f32[6,6]{0,1:T(8,128)S(1)} %psum.84), channel_id=1, replica_groups=mesh['gx_0'=8,'gx_1'=2,'gy'=4,'gz'=8] {'gx_1'}, use_global_device_ids=true, to_apply=%region_1.0 | all-reduce | flops 36 | bytes 288 | tf_op jit(solution)/shard_map/psum | solution.py:36
  30.3 6.1 %psum.86 = f32[6,6]{0,1:T(8,128)S(1)} all-reduce(f32[6,6]{0,1:T(8,128)S(1)} %psum.85), channel_id=1, replica_groups=mesh['gx_0'=8,'gx_1'=2,'gy'=4,'gz'=8] {'gy'}, use_global_device_ids=true, to_apply=%region_2.0 | all-reduce | flops 36 | bytes 288 | tf_op jit(solution)/shard_map/psum | solution.py:36
  36.4 18.7 %psum.87 = f32[6,6]{0,1:T(8,128)S(1)} all-reduce(f32[6,6]{0,1:T(8,128)S(1)} %psum.86), channel_id=1, replica_groups=mesh['gx_0'=8,'gx_1'=2,'gy'=4,'gz'=8] {'gz'}, use_global_device_ids=true, to_apply=%region_3.0 | all-reduce | flops 36 | bytes 288 | tf_op jit(solution)/shard_map/psum | solution.py:36
  62.8 4.6 %collective-permute-start.3 = (f32[34,3,1,2,128]{4,3,2,1,0:T(2,128)S(1)}, f32[34,3,1,2,128]{4,3,2,1,0:T(2,128)S(1)}, u32[]{:S(2)}, u32[]{:S(2)}) collective-permute-start(f32[34,3,1,2,128]{4,3,2,1,0:T(2,128)S(1)} %get-tuple-element.668), channel_id=1, source_target_pairs={{8,0},{16,8},{24,16},{0,24},{9,1},{17,9},{25,17},{1,25},{10,2},{18... | collective-permute-start | bytes 313352 | tf_op jit(solution)/shard_map/ppermute | solution.py:28
  71.5 4.6 %collective-permute-start.5 = (f32[34,3,4,1,128]{4,3,2,1,0:T(1,128)S(1)}, f32[34,3,4,1,128]{4,3,2,1,0:T(1,128)S(1)}, u32[]{:S(2)}, u32[]{:S(2)}) collective-permute-start(f32[34,3,4,1,128]{4,3,2,1,0:T(1,128)S(1)} %get-tuple-element.666), channel_id=1, source_target_pairs={{1,0},{2,1},{3,2},{4,3},{5,4},{6,5},{7,6},{0,7},{9,8},{10,9},{11,1... | collective-permute-start | bytes 626696 | tf_op jit(solution)/shard_map/ppermute | solution.py:28
  81.9 133.7 %while.38 = (s32[]{:T(128)}, f32[6,4,128]{2,1,0:T(4,128)S(1)}, f32[4,3,4,4,128]{4,3,2,1,0:T(4,128)S(1)}, f32[4,4,128]{2,1,0:T(4,128)S(1)}, s32[2,2,27]{1,0,2:T(2...) while((s32[]{:T(128)}, f32[6,4,128]{2,1,0:T(4,128)S(1)}, ...), condition=%wide.region_14.15_spmd.clone, body=%wide.region_7.14_spmd.clone.sunk | while | flops 6200890 | bytes 262953 | solution.py:106
  82.7 1.9 constant_dynamic-slice_fusion.24
  87.6 1.9 constant_dynamic-slice_fusion.24
  92.6 1.9 constant_dynamic-slice_fusion.24
  97.5 1.9 constant_dynamic-slice_fusion.24
  102.5 1.9 constant_dynamic-slice_fusion.24
  107.5 1.9 constant_dynamic-slice_fusion.24
  112.4 1.9 constant_dynamic-slice_fusion.24
  117.4 1.9 constant_dynamic-slice_fusion.24
  122.3 1.9 constant_dynamic-slice_fusion.24
  127.3 1.9 constant_dynamic-slice_fusion.24
  132.2 1.9 constant_dynamic-slice_fusion.24
  137.2 1.9 constant_dynamic-slice_fusion.24
  142.1 1.9 constant_dynamic-slice_fusion.24
  147.1 1.9 constant_dynamic-slice_fusion.24
  152.0 1.9 constant_dynamic-slice_fusion.24
  157.0 1.9 constant_dynamic-slice_fusion.24
  161.9 1.9 constant_dynamic-slice_fusion.24
  166.9 1.9 constant_dynamic-slice_fusion.24
  171.8 1.9 constant_dynamic-slice_fusion.24
  176.8 1.9 constant_dynamic-slice_fusion.24
  181.8 1.9 constant_dynamic-slice_fusion.24
  186.7 1.9 constant_dynamic-slice_fusion.24
  191.7 1.9 constant_dynamic-slice_fusion.24
  196.6 1.9 constant_dynamic-slice_fusion.24
  201.6 1.9 constant_dynamic-slice_fusion.24
  206.5 1.9 constant_dynamic-slice_fusion.24
  211.5 1.9 constant_dynamic-slice_fusion.24
  215.6 8.8 %collective-permute-start.6 = (f32[6,1,2,2,128]{4,3,2,1,0:T(2,128)S(1)}, f32[6,1,2,2,128]{4,3,2,1,0:T(2,128)S(1)}, u32[]{:S(2)}, u32[]{:S(2)}) collective-permute-start(f32[6,1,2,2,128]{4,3,2,1,0:T(2,128)S(1)} %fusion.75), channel_id=1, source_target_pairs={{0,32},{32,64},{64,96},{96,128},{128,160},{160,192},{192,224},{224... | collective-permute-start | bytes 36872 | tf_op jit(solution)/shard_map/ppermute | solution.py:26
  225.3 2.6 collective-permute-done.7
  229.9 5.2 %collective-permute-start.9 = (f32[6,3,1,2,128]{4,3,2,1,0:T(2,128)S(1)}, f32[6,3,1,2,128]{4,3,2,1,0:T(2,128)S(1)}, u32[]{:S(2)}, u32[]{:S(2)}) collective-permute-start(f32[6,3,1,2,128]{4,3,2,1,0:T(2,128)S(1)} %get-tuple-element.672), channel_id=1, source_target_pairs={{8,0},{16,8},{24,16},{0,24},{9,1},{17,9},{25,17},{1,25},{10,2},{18... | collective-permute-start | bytes 55304 | tf_op jit(solution)/shard_map/ppermute | solution.py:28
  238.0 5.3 %collective-permute-start.11 = (f32[6,3,4,1,128]{4,3,2,1,0:T(1,128)S(1)}, f32[6,3,4,1,128]{4,3,2,1,0:T(1,128)S(1)}, u32[]{:S(2)}, u32[]{:S(2)}) collective-permute-start(f32[6,3,4,1,128]{4,3,2,1,0:T(1,128)S(1)} %get-tuple-element.670), channel_id=1, source_target_pairs={{1,0},{2,1},{3,2},{4,3},{5,4},{6,5},{7,6},{0,7},{9,8},{10,9},{11,1... | collective-permute-start | bytes 110600 | tf_op jit(solution)/shard_map/ppermute | solution.py:28
  244.5 133.6 %while.39 = (s32[]{:T(128)}, f32[6,4,128]{2,1,0:T(4,128)S(1)}, f32[4,3,4,4,128]{4,3,2,1,0:T(4,128)S(1)}, f32[4,4,128]{2,1,0:T(4,128)S(1)}, s32[2,2,27]{1,0,2:T(2...) while((s32[]{:T(128)}, f32[6,4,128]{2,1,0:T(4,128)S(1)}, ...), condition=%wide.region_22.23_spmd.clone, body=%wide.region_15.22_spmd.clone.sunk | while | flops 6200890 | bytes 262953 | solution.py:106
  245.3 1.9 constant_dynamic-slice_fusion.25
  250.3 1.9 constant_dynamic-slice_fusion.25
  255.2 1.9 constant_dynamic-slice_fusion.25
  260.2 1.9 constant_dynamic-slice_fusion.25
  265.1 1.9 constant_dynamic-slice_fusion.25
  270.1 1.9 constant_dynamic-slice_fusion.25
  275.0 1.9 constant_dynamic-slice_fusion.25
  279.9 1.9 constant_dynamic-slice_fusion.25
  284.9 1.9 constant_dynamic-slice_fusion.25
  289.8 1.9 constant_dynamic-slice_fusion.25
  294.8 1.9 constant_dynamic-slice_fusion.25
  299.7 1.9 constant_dynamic-slice_fusion.25
  304.7 1.9 constant_dynamic-slice_fusion.25
  309.6 1.9 constant_dynamic-slice_fusion.25
  314.6 1.9 constant_dynamic-slice_fusion.25
  319.5 1.9 constant_dynamic-slice_fusion.25
  324.5 1.9 constant_dynamic-slice_fusion.25
  329.4 1.9 constant_dynamic-slice_fusion.25
  334.4 1.9 constant_dynamic-slice_fusion.25
  379.3 14.4 %all-reduce.1 = (f32[]{:T(128)}, f32[]{:T(128)}) all-reduce(f32[]{:T(128)} %get-tuple-element.589, f32[]{:T(128)} %get-tuple-element.588), channel_id=1, replica_groups=mesh['gx_0'=8,'gx_1'=2,'gy'=4,'gz'=8] {'gx_0'}, use_global_device_ids=true, to_apply=%region_24.25 | all-reduce | flops 2 | bytes 16 | tf_op jit(solution)/shard_map/psum | solution.py:36
  393.7 6.2 %all-reduce.3 = (f32[]{:T(128)}, f32[]{:T(128)}) all-reduce(f32[]{:T(128)} %get-tuple-element.616, f32[]{:T(128)} %get-tuple-element.617), channel_id=1, replica_groups=mesh['gx_0'=8,'gx_1'=2,'gy'=4,'gz'=8] {'gx_1'}, use_global_device_ids=true, to_apply=%region_25.26 | all-reduce | flops 2 | bytes 16 | tf_op jit(solution)/shard_map/psum | solution.py:36
  400.0 9.9 %all-reduce.2 = (f32[]{:T(128)}, f32[]{:T(128)}) all-reduce(f32[]{:T(128)} %get-tuple-element.620, f32[]{:T(128)} %get-tuple-element.621), channel_id=1, replica_groups=mesh['gx_0'=8,'gx_1'=2,'gy'=4,'gz'=8] {'gy'}, use_global_device_ids=true, to_apply=%region_26.27 | all-reduce | flops 2 | bytes 16 | tf_op jit(solution)/shard_map/psum | solution.py:36
  409.9 14.8 %all-reduce = (f32[]{:T(128)}, f32[]{:T(128)}) all-reduce(f32[]{:T(128)} %get-tuple-element.618, f32[]{:T(128)} %get-tuple-element.619), channel_id=1, replica_groups=mesh['gx_0'=8,'gx_1'=2,'gy'=4,'gz'=8] {'gz'}, use_global_device_ids=true, to_apply=%region_27.28 | all-reduce | flops 2 | bytes 16 | tf_op jit(solution)/shard_map/psum | solution.py:36
  (1208 shorter events, 196.8 us)
Async XLA Ops:
  0.6 66.8 %copy-start.2 = (f32[1,2,2,128]{3,2,1,0:T(2,128)S(1)}, f32[1,2,2,128]{3,2,1,0:T(2,128)}, u32[]{:S(2)}) copy-start(f32[1,2,2,128]{3,2,1,0:T(2,128)} %param.11) | copy-start | bytes 6148
  0.6 66.8 %copy-start.1 = (f32[3,1,2,2,128]{4,3,2,1,0:T(2,128)S(1)}, f32[3,1,2,2,128]{4,3,2,1,0:T(2,128)}, u32[]{:S(2)}) copy-start(f32[3,1,2,2,128]{4,3,2,1,0:T(2,128)} %param.10) | copy-start | bytes 18436
  3.0 57.0 %collective-permute-start = (f32[34,1,2,2,128]{4,3,2,1,0:T(2,128)S(1)}, f32[34,1,2,2,128]{4,3,2,1,0:T(2,128)S(1)}, u32[]{:S(2)}, u32[]{:S(2)}) collective-permute-start(f32[34,1,2,2,128]{4,3,2,1,0:T(2,128)S(1)} %pad_maximum_fusion.5), channel_id=1, source_target_pairs={{0,32},{32,64},{64,96},{96,128},{128,160},{160,192},{192,224},{224... | collective-permute-start | bytes 208904 | tf_op jit(solution)/shard_map/ppermute | solution.py:26
  5.7 54.3 %collective-permute-start.1 = (f32[34,1,2,2,128]{4,3,2,1,0:T(2,128)S(1)}, f32[34,1,2,2,128]{4,3,2,1,0:T(2,128)S(1)}, u32[]{:S(2)}, u32[]{:S(2)}) collective-permute-start(f32[34,1,2,2,128]{4,3,2,1,0:T(2,128)S(1)} %pad_maximum_fusion.5), channel_id=1, source_target_pairs={{32,0},{64,32},{96,64},{128,96},{160,128},{192,160},{224,192},{256... | collective-permute-start | bytes 208904 | tf_op jit(solution)/shard_map/ppermute | solution.py:28
  60.9 6.6 %collective-permute-start.2 = (f32[34,3,1,2,128]{4,3,2,1,0:T(2,128)S(1)}, f32[34,3,1,2,128]{4,3,2,1,0:T(2,128)S(1)}, u32[]{:S(2)}, u32[]{:S(2)}) collective-permute-start(f32[34,3,1,2,128]{4,3,2,1,0:T(2,128)S(1)} %get-tuple-element.667), channel_id=1, source_target_pairs={{0,8},{8,16},{16,24},{24,0},{1,9},{9,17},{17,25},{25,1},{2,10},{10... | collective-permute-start | bytes 313352 | tf_op jit(solution)/shard_map/ppermute | solution.py:26
  62.8 6.3 %collective-permute-start.3 = (f32[34,3,1,2,128]{4,3,2,1,0:T(2,128)S(1)}, f32[34,3,1,2,128]{4,3,2,1,0:T(2,128)S(1)}, u32[]{:S(2)}, u32[]{:S(2)}) collective-permute-start(f32[34,3,1,2,128]{4,3,2,1,0:T(2,128)S(1)} %get-tuple-element.668), channel_id=1, source_target_pairs={{8,0},{16,8},{24,16},{0,24},{9,1},{17,9},{25,17},{1,25},{10,2},{18... | collective-permute-start | bytes 313352 | tf_op jit(solution)/shard_map/ppermute | solution.py:28
  67.5 8.7 %copy-start.4 = (s32[1,2,2,128]{3,2,1,0:T(2,128)S(1)}, s32[1,2,2,128]{3,2,1,0:T(2,128)}, u32[]{:S(2)}) copy-start(s32[1,2,2,128]{3,2,1,0:T(2,128)} %param.12) | copy-start | bytes 6148
  69.6 7.8 %collective-permute-start.4 = (f32[34,3,4,1,128]{4,3,2,1,0:T(1,128)S(1)}, f32[34,3,4,1,128]{4,3,2,1,0:T(1,128)S(1)}, u32[]{:S(2)}, u32[]{:S(2)}) collective-permute-start(f32[34,3,4,1,128]{4,3,2,1,0:T(1,128)S(1)} %get-tuple-element.665), channel_id=1, source_target_pairs={{0,1},{1,2},{2,3},{3,4},{4,5},{5,6},{6,7},{7,0},{8,9},{9,10},{10,1... | collective-permute-start | bytes 626696 | tf_op jit(solution)/shard_map/ppermute | solution.py:26
  71.5 7.3 %collective-permute-start.5 = (f32[34,3,4,1,128]{4,3,2,1,0:T(1,128)S(1)}, f32[34,3,4,1,128]{4,3,2,1,0:T(1,128)S(1)}, u32[]{:S(2)}, u32[]{:S(2)}) collective-permute-start(f32[34,3,4,1,128]{4,3,2,1,0:T(1,128)S(1)} %get-tuple-element.666), channel_id=1, source_target_pairs={{1,0},{2,1},{3,2},{4,3},{5,4},{6,5},{7,6},{0,7},{9,8},{10,9},{11,1... | collective-permute-start | bytes 626696 | tf_op jit(solution)/shard_map/ppermute | solution.py:28
  79.4 0.9 copy-start
  80.3 1.5 slice-start
  81.8 133.8 %copy-start.3 = (f32[6,1,2,2,128]{4,3,2,1,0:T(2,128)S(1)}, f32[6,1,2,2,128]{4,3,2,1,0:T(2,128)}, u32[]{:S(2)}) copy-start(f32[6,1,2,2,128]{4,3,2,1,0:T(2,128)} %param.14) | copy-start | bytes 36868
  215.6 9.7 %collective-permute-start.6 = (f32[6,1,2,2,128]{4,3,2,1,0:T(2,128)S(1)}, f32[6,1,2,2,128]{4,3,2,1,0:T(2,128)S(1)}, u32[]{:S(2)}, u32[]{:S(2)}) collective-permute-start(f32[6,1,2,2,128]{4,3,2,1,0:T(2,128)S(1)} %fusion.75), channel_id=1, source_target_pairs={{0,32},{32,64},{64,96},{96,128},{128,160},{160,192},{192,224},{224... | collective-permute-start | bytes 36872 | tf_op jit(solution)/shard_map/ppermute | solution.py:26
  224.5 3.4 collective-permute-start.7
  227.9 7.2 %collective-permute-start.8 = (f32[6,3,1,2,128]{4,3,2,1,0:T(2,128)S(1)}, f32[6,3,1,2,128]{4,3,2,1,0:T(2,128)S(1)}, u32[]{:S(2)}, u32[]{:S(2)}) collective-permute-start(f32[6,3,1,2,128]{4,3,2,1,0:T(2,128)S(1)} %get-tuple-element.671), channel_id=1, source_target_pairs={{0,8},{8,16},{16,24},{24,0},{1,9},{9,17},{17,25},{25,1},{2,10},{10... | collective-permute-start | bytes 55304 | tf_op jit(solution)/shard_map/ppermute | solution.py:26
  229.9 6.1 %collective-permute-start.9 = (f32[6,3,1,2,128]{4,3,2,1,0:T(2,128)S(1)}, f32[6,3,1,2,128]{4,3,2,1,0:T(2,128)S(1)}, u32[]{:S(2)}, u32[]{:S(2)}) collective-permute-start(f32[6,3,1,2,128]{4,3,2,1,0:T(2,128)S(1)} %get-tuple-element.672), channel_id=1, source_target_pairs={{8,0},{16,8},{24,16},{0,24},{9,1},{17,9},{25,17},{1,25},{10,2},{18... | collective-permute-start | bytes 55304 | tf_op jit(solution)/shard_map/ppermute | solution.py:28
  236.1 7.3 %collective-permute-start.10 = (f32[6,3,4,1,128]{4,3,2,1,0:T(1,128)S(1)}, f32[6,3,4,1,128]{4,3,2,1,0:T(1,128)S(1)}, u32[]{:S(2)}, u32[]{:S(2)}) collective-permute-start(f32[6,3,4,1,128]{4,3,2,1,0:T(1,128)S(1)} %get-tuple-element.669), channel_id=1, source_target_pairs={{0,1},{1,2},{2,3},{3,4},{4,5},{5,6},{6,7},{7,0},{8,9},{9,10},{10,1... | collective-permute-start | bytes 110600 | tf_op jit(solution)/shard_map/ppermute | solution.py:26
  238.0 6.4 %collective-permute-start.11 = (f32[6,3,4,1,128]{4,3,2,1,0:T(1,128)S(1)}, f32[6,3,4,1,128]{4,3,2,1,0:T(1,128)S(1)}, u32[]{:S(2)}, u32[]{:S(2)}) collective-permute-start(f32[6,3,4,1,128]{4,3,2,1,0:T(1,128)S(1)} %get-tuple-element.670), channel_id=1, source_target_pairs={{1,0},{2,1},{3,2},{4,3},{5,4},{6,5},{7,6},{0,7},{9,8},{10,9},{11,1... | collective-permute-start | bytes 110600 | tf_op jit(solution)/shard_map/ppermute | solution.py:28
where the time goes:
time: 433 us; the launch traced here: 427 us
  other arithmetic  223 us (52%)
  blocking collectives  89.3 us (21%)
  local copies, waits for them, and re-layouts  45.7 us (11%)
  starting transfers between devices  43.1 us (10%)
  loops' own time  10.2 us (2%)
  waiting for transfers between devices  9.63 us (2%)
    slice x54, other arithmetic, pair_field(): moment[3 * which_set + axis_num][:, None, :]  104 us
    reduce_sum x108, other arithmetic, pair_field(): jnp.sum(radial * project * displace[axis_num] - direct * parts[axis_num],...  102 us
    psum x8, blocking collectives, one_axis_at_a_time(): return functools.reduce(lax.psum, axes, shard)  89.3 us
    slice x54, local copies, waits for them, and re-layouts, pair_field(): offset_vec[axis_num] + source[axis_num][:, None, :]  36 us
    ppermute x6, starting transfers between devices, with_halo(): lax.ppermute(head, axis, [((i + 1) % count, i) for i in range(count)])  23.9 us
    ppermute x6, starting transfers between devices, with_halo(): lax.ppermute(tail, axis, [(i, (i + 1) % count) for i in range(count)])  19.2 us
    another operation x2, loops' own time, slab_field(): lax.fori_loop(0, 27, offset_step, jnp.zeros((rows, width_y * width_z, slo...  10.2 us
  transfers between devices with their start and end apart: 12, of which 8 were waited for; matrix products, arithmetic and copies ran while one was open for 1% of the time, Pallas kernels for 0%

commit v1 on v0

v1 whole, which is shorter than its diff:
```python
import functools

import jax
import jax.numpy as jnp
from jax import lax
from jax.experimental import pallas as pl
from jax.experimental.pallas import tpu as pltpu

ALL = ("gx", "gy", "gz")
CELL_EDGE = 10.0
SOFTENING = 0.3
THOLE_DAMP = 0.39
RELAXATION = 0.7
LN2 = 0.6931471805599453

SLOTS = 128
NX, NY, NZ = 3, 4, 4
TILES = NX * NY * NZ
OWN = 4
OFFSETS = 27
TERMS = 48
A_ROWS = 96
B_ROWS = 24
BATCH = 8
PAIRS = OWN + OWN * (OFFSETS - 1)
GRAM = tuple((a, b) for a in range(6) for b in range(a + 1))


def source_tile(tile, offset):
    x = offset // 9
    y = tile // 2 + offset // 3 % 3
    z = tile % 2 + offset % 3
    return (x * NY + y) * NZ + z


OWN_TILES = tuple(source_tile(t, 13) for t in range(OWN))


def split3(value):
    high = value.astype(jnp.bfloat16).astype(jnp.float32)
    rest = value - high
    middle = rest.astype(jnp.bfloat16).astype(jnp.float32)
    return high, middle, rest - middle


def positions(geo):
    tile = lax.broadcasted_iota(jnp.int32, (TILES, SLOTS), 0)
    x = (tile // (NY * NZ)).astype(jnp.float32)
    y = (tile // NZ % NY).astype(jnp.float32)
    z = (tile % NZ).astype(jnp.float32)
    return (
        (geo[0] + (x - 1.5)) * CELL_EDGE,
        (geo[1] + (y - 2.0)) * CELL_EDGE,
        (geo[2] + (z - 2.0)) * CELL_EDGE,
    )


def scale_of(polar):
    factor = (THOLE_DAMP / LN2) ** (1.0 / 3.0)
    return factor * jnp.exp(jnp.log(polar) * (-1.0 / 3.0))


def own_rows(value):
    return [value[t : t + 1] for t in OWN_TILES]


def pair_kernel(mask_ref, geo_ref, list_ref, count_ref, pair_ref, q_ref, qt_ref, p_ref):
    geo = [geo_ref[a] for a in range(4)]
    r = positions(geo)
    a = scale_of(geo[3])
    norm = r[0] * r[0] + r[1] * r[1] + r[2] * r[2]
    sources = [a, a * (norm + SOFTENING), a * r[0], a * r[1], a * r[2]]
    targets = [a * norm, a, -2.0 * a * r[0], -2.0 * a * r[1], -2.0 * a * r[2]]
    row = 0
    for source, target in zip(sources, targets):
        source_parts = split3(source)
        target_parts = split3(target)
        for s in range(3):
            for t in range(3):
                q_ref[0:TILES, row, :] = source_parts[s]
                for own in range(OWN):
                    p_ref[own, row : row + 1, :] = target_parts[t][
                        OWN_TILES[own] : OWN_TILES[own] + 1
                    ]
                row += 1
    zero = jnp.zeros((TILES, SLOTS), jnp.float32)
    for rest in range(row, TERMS):
        q_ref[0:TILES, rest, :] = zero
        for own in range(OWN):
            p_ref[own, rest : rest + 1, :] = zero[0:1]

    def flip(n, carry):
        qt_ref[n] = q_ref[n].T.astype(jnp.bfloat16)
        return carry

    lax.fori_loop(0, TILES, flip, 0)
    qt_ref[TILES] = qt_ref[0]

    count = jnp.int32(OWN)
    for t in range(OWN):
        list_ref[t] = OWN_TILES[t] * OWN + t
    for t in range(OWN):
        for k in range(OFFSETS):
            if k == 13:
                continue
            list_ref[count] = source_tile(t, k) * OWN + t
            count = count + (mask_ref[t * OFFSETS + k] != 0).astype(jnp.int32)
    for extra in range(BATCH):
        list_ref[count + extra] = TILES * OWN
    count_ref[0] = count

    def pair(slot, keep):
        entry = list_ref[slot]
        n = entry // OWN
        t = entry % OWN
        dist = jnp.dot(
            qt_ref[n], p_ref[t].astype(jnp.bfloat16), preferred_element_type=jnp.float32
        )
        inv = lax.rsqrt(dist)
        arg = dist * (dist * inv)
        damp = jnp.exp2(-arg)
        inv2 = inv * inv
        direct = (1.0 - damp) * (inv2 * inv)
        radial = inv2 * (direct - LN2 * damp)
        if keep is not None:
            direct = jnp.where(keep, direct, 0.0)
            radial = jnp.where(keep, radial, 0.0)
        for part, value in enumerate((radial, direct)):
            high = value.astype(jnp.bfloat16)
            low = (value - high.astype(jnp.float32)).astype(jnp.bfloat16)
            base = part * 2 * SLOTS
            pair_ref[slot, base : base + SLOTS, :] = high
            pair_ref[slot, base + SLOTS : base + 2 * SLOTS, :] = low

    keep = lax.broadcasted_iota(jnp.int32, (SLOTS, SLOTS), 0) != lax.broadcasted_iota(
        jnp.int32, (SLOTS, SLOTS), 1
    )
    for slot in range(OWN):
        pair(slot, keep)

    def batch(b, carry):
        for u in range(BATCH):
            pair(OWN + b * BATCH + u, None)
        return carry

    lax.fori_loop(0, (count - OWN + BATCH - 1) // BATCH, batch, 0)


def build_pairs(mask, geo):
    return pl.pallas_call(
        pair_kernel,
        name="build_pairs",
        in_specs=[
            pl.BlockSpec(memory_space=pltpu.SMEM),
            pl.BlockSpec(memory_space=pltpu.VMEM),
        ],
        out_specs=[
            pl.BlockSpec(memory_space=pltpu.SMEM),
            pl.BlockSpec(memory_space=pltpu.SMEM),
            pl.BlockSpec(memory_space=pltpu.VMEM),
        ],
        out_shape=[
            jax.ShapeDtypeStruct((PAIRS + BATCH,), jnp.int32),
            jax.ShapeDtypeStruct((1,), jnp.int32),
            jax.ShapeDtypeStruct((PAIRS, 4 * SLOTS, SLOTS), jnp.bfloat16),
        ],
        scratch_shapes=[
            pltpu.VMEM((TILES, TERMS, SLOTS), jnp.float32),
            pltpu.VMEM((TILES + 1, SLOTS, TERMS), jnp.bfloat16),
            pltpu.VMEM((OWN, TERMS, SLOTS), jnp.float32),
        ],
        compiler_params=pltpu.CompilerParams(vmem_limit_bytes=24 * 1024 * 1024),
    )(mask, geo)


def apply_pairs(list_ref, count_ref, geo_ref, pair_ref, moment, a_ref, b_ref, sum_a, sum_b):
    geo = [geo_ref[a] for a in range(4)]
    r = positions(geo)
    a = scale_of(geo[3])
    root = jnp.sqrt(a)
    scale_b = a * root
    scale_a = scale_b * a
    for kind in range(2):
        m = [moment[3 * kind + c] * scale_a for c in range(3)]
        g = r[0] * m[0] + r[1] * m[1] + r[2] * m[2]
        values = [g] + [r[c] * g for c in range(3)] + m
        values += [r[c] * m[d] for c in range(3) for d in range(3)]
        for index, value in enumerate(values):
            for s, part in enumerate(split3(value)):
                a_ref[0:TILES, 32 * s + 16 * kind + index, :] = part
    for c in range(6):
        for s, part in enumerate(split3(moment[c] * scale_b)):
            b_ref[0:TILES, 8 * s + c, :] = part
    zero = jnp.zeros((TILES, SLOTS), jnp.float32)
    for s in range(3):
        for c in (6, 7):
            b_ref[0:TILES, 8 * s + c, :] = zero
    a_ref[TILES] = jnp.zeros((A_ROWS, SLOTS), jnp.float32)
    b_ref[TILES] = jnp.zeros((B_ROWS, SLOTS), jnp.float32)

    def product(slot):
        entry = list_ref[slot]
        n = entry // OWN
        left = a_ref[n].astype(jnp.bfloat16)
        part_a = jnp.dot(
            jnp.concatenate([left, left], axis=1),
            pair_ref[slot, 0 : 2 * SLOTS, :],
            preferred_element_type=jnp.float32,
        )
        left = b_ref[n].astype(jnp.bfloat16)
        part_b = jnp.dot(
            jnp.concatenate([left, left], axis=1),
            pair_ref[slot, 2 * SLOTS : 4 * SLOTS, :],
            preferred_element_type=jnp.float32,
        )
        return entry % OWN, part_a, part_b

    for slot in range(OWN):
        t, part_a, part_b = product(slot)
        sum_a[slot] = part_a
        sum_b[slot] = part_b

    def batch(b, carry):
        for u in range(BATCH):
            t, part_a, part_b = product(OWN + b * BATCH + u)
            sum_a[t] += part_a
            sum_b[t] += part_b
        return carry

    lax.fori_loop(0, (count_ref[0] - OWN + BATCH - 1) // BATCH, batch, 0)

    own_r = [jnp.concatenate(own_rows(r[c]), 0) for c in range(3)]
    own_a = 3.0 * jnp.concatenate(own_rows(scale_a), 0)
    own_b = jnp.concatenate(own_rows(scale_b), 0)

    def total_a(kind, index):
        row = 16 * kind + index
        return sum_a[:, row, :] + sum_a[:, 32 + row, :] + sum_a[:, 64 + row, :]

    def total_b(row):
        return sum_b[:, row, :] + sum_b[:, 8 + row, :] + sum_b[:, 16 + row, :]

    fields = []
    for kind in range(2):
        g = total_a(kind, 0)
        m = [total_a(kind, 4 + c) for c in range(3)]
        dot = own_r[0] * m[0] + own_r[1] * m[1] + own_r[2] * m[2] - g
        for c in range(3):
            cross = sum(own_r[d] * total_a(kind, 7 + 3 * c + d) for d in range(3))
            radial = total_a(kind, 1 + c) - cross + own_r[c] * dot
            fields.append(own_a * radial - own_b * total_b(3 * kind + c))
    return fields


def own_part(value):
    return jnp.concatenate(own_rows(value), 0)


def solve(gram):
    count = 5
    matrix = [[gram[max(a, b), min(a, b)] for b in range(count)] for a in range(count)]
    right = [gram[count, a] for a in range(count)]
    trace = matrix[0][0]
    for a in range(1, count):
        trace = trace + matrix[a][a]
    ridge = 0.001 * trace / count + 1.0
    for a in range(count):
        matrix[a][a] = matrix[a][a] + ridge
    for c in range(count):
        for a in range(c + 1, count):
            ratio = matrix[a][c] / matrix[c][c]
            for b in range(c + 1, a + 1):
                matrix[a][b] = matrix[a][b] - ratio * matrix[b][c]
            right[a] = right[a] - ratio * right[c]
    result = [None] * count
    for a in reversed(range(count)):
        rest = right[a]
        for b in range(a + 1, count):
            rest = rest - matrix[b][a] * result[b]
        result[a] = rest / matrix[a][a]
    return result


def gram_kernel(history_ref, occupancy_ref, out_ref):
    filled = occupancy_ref[...].astype(jnp.float32)
    masked = [
        [history_ref[h, c] * filled for c in range(6)] for h in range(6)
    ]
    lane = lax.broadcasted_iota(jnp.int32, (1, SLOTS), 1)
    row = jnp.zeros((1, SLOTS), jnp.float32)
    for index, (a, b) in enumerate(GRAM):
        product = masked[a][0] * masked[b][0]
        for c in range(1, 6):
            product = product + masked[a][c] * masked[b][c]
        total = jnp.sum(jnp.sum(product, axis=0, keepdims=True), axis=1, keepdims=True)
        row = jnp.where(lane == index, total, row)
    out_ref[...] = jnp.broadcast_to(row[None], out_ref.shape)


def vmem_spec():
    return pl.BlockSpec(memory_space=pltpu.VMEM)


def smem_spec():
    return pl.BlockSpec(memory_space=pltpu.SMEM)


def local_gram(history, occupancy, copies):
    return pl.pallas_call(
        gram_kernel,
        name="local_gram",
        in_specs=[vmem_spec(), vmem_spec()],
        out_specs=vmem_spec(),
        out_shape=jax.ShapeDtypeStruct((copies, 1, SLOTS), jnp.float32),
    )(history, occupancy)


def sum_kernel(parts_ref, out_ref):
    total = jnp.sum(parts_ref[...], axis=0, keepdims=True)
    out_ref[...] = jnp.broadcast_to(total, out_ref.shape)


def sum_parts(parts, copies):
    return pl.pallas_call(
        sum_kernel,
        name="sum_parts",
        in_specs=[vmem_spec()],
        out_specs=vmem_spec(),
        out_shape=jax.ShapeDtypeStruct((copies, 1, SLOTS), jnp.float32),
    )(parts)


SCRATCH = [
    pltpu.VMEM((TILES + 1, A_ROWS, SLOTS), jnp.float32),
    pltpu.VMEM((TILES + 1, B_ROWS, SLOTS), jnp.float32),
    pltpu.VMEM((OWN, A_ROWS, SLOTS), jnp.float32),
    pltpu.VMEM((OWN, B_ROWS, SLOTS), jnp.float32),
]


def first_kernel(
    list_ref, count_ref, gram_ref, geo_ref, later_ref, occupancy_ref, perm_ref, pair_ref,
    out_ref, a_ref, b_ref, sum_a, sum_b,
):
    total = jnp.sum(gram_ref[...], axis=0)
    gram = {ab: total[0:1, i : i + 1] for i, ab in enumerate(GRAM)}
    coeffs = solve(gram)
    moment = []
    for c in range(6):
        value = coeffs[0] * later_ref[c]
        for h in range(1, 5):
            value = value + coeffs[h] * later_ref[6 * h + c]
        moment.append(value)
    fields = apply_pairs(
        list_ref, count_ref, geo_ref, pair_ref, moment, a_ref, b_ref, sum_a, sum_b
    )
    scaled = RELAXATION * occupancy_ref[...].astype(jnp.float32) * own_part(geo_ref[3])
    for c in range(6):
        out_ref[c] = (1.0 - RELAXATION) * own_part(moment[c]) + scaled * (
            perm_ref[c] + fields[c]
        )


def second_kernel(
    list_ref, count_ref, geo_ref, dipole_ref, occupancy_ref, perm_ref, pair_ref,
    out_ref, size_ref, a_ref, b_ref, sum_a, sum_b,
):
    moment = [dipole_ref[c] for c in range(6)]
    fields = apply_pairs(
        list_ref, count_ref, geo_ref, pair_ref, moment, a_ref, b_ref, sum_a, sum_b
    )
    scaled = RELAXATION * occupancy_ref[...].astype(jnp.float32) * own_part(geo_ref[3])
    moved = jnp.zeros((OWN, SLOTS), jnp.float32)
    size = jnp.zeros((OWN, SLOTS), jnp.float32)
    for c in range(6):
        old = own_part(moment[c])
        new = (1.0 - RELAXATION) * old + scaled * (perm_ref[c] + fields[c])
        out_ref[c] = new
        moved = moved + (new - old) * (new - old)
        size = size + new * new
    lane = lax.broadcasted_iota(jnp.int32, (1, SLOTS), 1)
    row = jnp.zeros((1, SLOTS), jnp.float32)
    for index, value in enumerate((moved, size)):
        total = jnp.sum(jnp.sum(value, axis=0, keepdims=True), axis=1, keepdims=True)
        row = jnp.where(lane == index, total, row)
    size_ref[...] = jnp.broadcast_to(row[None], size_ref.shape)


FIELD_PARAMS = pltpu.CompilerParams(vmem_limit_bytes=24 * 1024 * 1024)


def first_field(pair_list, count, gram, geo, later, occupancy, perm, pairs):
    return pl.pallas_call(
        first_kernel,
        name="first_field",
        in_specs=[smem_spec(), smem_spec()] + [vmem_spec()] * 6,
        out_specs=vmem_spec(),
        out_shape=jax.ShapeDtypeStruct((6, OWN, SLOTS), jnp.float32),
        scratch_shapes=SCRATCH,
        compiler_params=FIELD_PARAMS,
    )(pair_list, count, gram, geo, later, occupancy, perm, pairs)


def second_field(pair_list, count, geo, dipoles, occupancy, perm, pairs, copies):
    return pl.pallas_call(
        second_kernel,
        name="second_field",
        in_specs=[smem_spec(), smem_spec()] + [vmem_spec()] * 5,
        out_specs=[vmem_spec(), vmem_spec()],
        out_shape=[
            jax.ShapeDtypeStruct((6, OWN, SLOTS), jnp.float32),
            jax.ShapeDtypeStruct((copies, 1, SLOTS), jnp.float32),
        ],
        scratch_shapes=SCRATCH,
        compiler_params=FIELD_PARAMS,
    )(pair_list, count, geo, dipoles, occupancy, perm, pairs)


def with_halo(cells, sides):
    for axis, dim in sides:
        count = lax.axis_size(axis)
        head = lax.slice_in_dim(cells, 0, 1, axis=dim)
        tail = lax.slice_in_dim(cells, cells.shape[dim] - 1, cells.shape[dim], axis=dim)
        cells = jnp.concatenate(
            [
                lax.ppermute(tail, axis, [(i, (i + 1) % count) for i in range(count)]),
                cells,
                lax.ppermute(head, axis, [((i + 1) % count, i) for i in range(count)]),
            ],
            axis=dim,
        )
    return cells


SIDES = (("gx", 1), ("gy", 2), ("gz", 3))


def exchange(parts, axes):
    return lax.all_to_all(parts, axes, 0, 0)


def on_device(fractions, polarizability, occupancy, pair_mask, perm_field, history):
    plane = lax.axis_size("gy") * lax.axis_size("gz")
    line = lax.axis_size("gx")
    history = history.reshape(6, 6, OWN, SLOTS)
    occupancy = occupancy.reshape(OWN, SLOTS)
    perm = perm_field.reshape(6, OWN, SLOTS)

    filled = occupancy.astype(jnp.float32)
    later = (history[1:] * filled).reshape(30, 1, 2, 2, SLOTS)
    stacked = jnp.concatenate([fractions, polarizability[None], later], 0)
    ghosts = with_halo(stacked, SIDES)

    gram = exchange(local_gram(history, occupancy, plane), ("gy", "gz"))
    gram = exchange(sum_parts(gram, line), "gx")

    geo = ghosts[:4].reshape(4, TILES, SLOTS)
    later = ghosts[4:].reshape(30, TILES, SLOTS)
    pair_list, count, pairs = build_pairs(pair_mask.reshape(-1), geo)
    dipoles = first_field(pair_list, count, gram, geo, later, occupancy, perm, pairs)
    dipoles = with_halo(dipoles.reshape(6, 1, 2, 2, SLOTS), SIDES).reshape(6, TILES, SLOTS)
    induced, sizes = second_field(
        pair_list, count, geo, dipoles, occupancy, perm, pairs, plane
    )
    sizes = exchange(sizes, ("gy", "gz"))
    sizes = exchange(sum_parts(sizes, line), "gx")
    totals = jnp.sum(sizes, axis=(0, 1))
    change = jnp.sqrt(totals[0] / (totals[1] + 1.0))
    return induced.reshape(6, 1, 2, 2, SLOTS), change


def solution(mesh):
    from jax.sharding import PartitionSpec as P

    tiles = P("gx", "gy", "gz", None)
    sets = P(None, "gx", "gy", "gz", None)
    return jax.shard_map(
        on_device,
        mesh=mesh,
        in_specs=(
            sets,
            tiles,
            tiles,
            tiles,
            sets,
            P(None, None, "gx", "gy", "gz", None),
        ),
        out_specs=(sets, P()),
        check_vma=False,
    )
```

time: 433 us -> 161 us (0.37); the launches traced: 427 us -> 160 us
  other arithmetic: 223 us -> 4.62 us
  blocking collectives: 89.3 us -> 34.2 us
  Pallas kernels: 0 us -> 31.7 us
  local copies, waits for them, and re-layouts: 45.7 us -> 14.8 us
  starting transfers between devices: 43.1 us -> 56.5 us
  loops' own time: 10.2 us -> 0 us
  waiting for transfers between devices: 9.63 us -> 14.7 us
    slice x54 -> x0, other arithmetic: 104 us -> none  [pair_field(): moment[3 * which_set + axis_num][:, None, :]]
    reduce_sum x110 -> x1, other arithmetic: 104 us -> 0.03 us  [on_device(): totals = jnp.sum(sizes, axis=(0, 1))]
    psum x8 -> x0, blocking collectives: 89.3 us -> none  [one_axis_at_a_time(): return functools.reduce(lax.psum, axes, shard)]
    slice x62 -> x8, local copies, waits for them, and re-layouts: 36.5 us -> 1.96 us  [the longest x1 0.83 us: on_device(): later = (history[1:] * filled).reshape(30, 1, 2, 2, SLOTS)]
    all_to_all x0 -> x2, blocking collectives: none -> 34.2 us  [exchange(): return lax.all_to_all(parts, axes, 0, 0)]
    pallas_call x0 -> x6, Pallas kernels: none -> 31.7 us  [the longest x1 11.1 us: build_pairs(): pl.pallas_call(pair_kernel, name='build_pairs', in_specs=[pl.BlockSpec(me...]
    all_to_all x0 -> x2, starting transfers between devices: none -> 18.5 us  [exchange(): return lax.all_to_all(parts, axes, 0, 0)]
    unnamed x11 -> x10, local copies, waits for them, and re-layouts: 1.67 us -> 12 us
  transfers between devices with their start and end apart: 12 -> 14, of which waited for: 8 -> 9; matrix products, arithmetic and copies ran while one was open for 1% -> 1% of each run, Pallas kernels for 0% -> 9%
where the time goes in v1:
time: 161 us; the launch traced here: 160 us
  starting transfers between devices  56.5 us (35%)
  blocking collectives  34.2 us (21%)
  Pallas kernels  31.7 us (20%)
  local copies, waits for them, and re-layouts  14.8 us (9%)
  waiting for transfers between devices  14.7 us (9%)
  other arithmetic  4.62 us (3%)
  between operations  3.35 us (2%)
    all_to_all x2, blocking collectives, exchange(): return lax.all_to_all(parts, axes, 0, 0)  34.2 us
    ppermute x6, starting transfers between devices, with_halo(): lax.ppermute(head, axis, [((i + 1) % count, i) for i in range(count)])  28 us
    all_to_all x2, starting transfers between devices, exchange(): return lax.all_to_all(parts, axes, 0, 0)  18.5 us
    unnamed x10, local copies, waits for them, and re-layouts  12 us
    pallas_call x1, Pallas kernels, build_pairs(): pl.pallas_call(pair_kernel, name='build_pairs', in_specs=[pl.BlockSpec(me...  11.1 us
    ppermute x6, starting transfers between devices, with_halo(): lax.ppermute(tail, axis, [(i, (i + 1) % count) for i in range(count)])  9.95 us
    pallas_call x1, Pallas kernels, first_field(): pl.pallas_call(first_kernel, name='first_field', in_specs=[smem_spec(), s...  8.55 us
    all_to_all x2, waiting for transfers between devices, exchange(): return lax.all_to_all(parts, axes, 0, 0)  7.89 us
  transfers between devices with their start and end apart: 14, of which 9 were waited for; matrix products, arithmetic and copies ran while one was open for 1% of the time, Pallas kernels for 9%

profile of v1, /device:TPU:1, one launch (start us, length us, event | category | flops | bytes accessed | tf_op | source)
XLA Modules:
  0.0 159.9 jit_solution(1474544919810409067)
XLA Ops:
  0.6 0.7 convert_bitcast_fusion
  1.3 0.8 slice.42
  2.2 0.7 pad_maximum_fusion.5
  2.9 6.9 %collective-permute-start.1 = (f32[34,1,2,2,128]{4,3,2,1,0:T(2,128)S(1)}, f32[34,1,2,2,128]{4,3,2,1,0:T(2,128)S(1)}, u32[]{:S(2)}, u32[]{:S(2)}) collective-permute-start(f32[34,1,2,2,128]{4,3,2,1,0:T(2,128)S(1)} %pad_maximum_fusion.5), channel_id=1, source_target_pairs={{32,0},{64,32},{96,64},{128,96},{160,128},{192,160},{224,192},{256... | collective-permute-start | bytes 208904 | tf_op jit(solution)/shard_map/ppermute | solution.py:428
  9.8 0.0 collective-permute-start
  9.8 0.9 collective-permute-done.1
  10.7 0.5 collective-permute-done
  11.2 0.8 pad_maximum_fusion.2
  12.0 0.1 fusion.1
  12.0 1.9 %collective-permute-start.2 = (f32[34,3,1,2,128]{4,3,2,1,0:T(2,128)S(1)}, f32[34,3,1,2,128]{4,3,2,1,0:T(2,128)S(1)}, u32[]{:S(2)}, u32[]{:S(2)}) collective-permute-start(f32[34,3,1,2,128]{4,3,2,1,0:T(2,128)S(1)} %get-tuple-element.16), channel_id=1, source_target_pairs={{0,8},{8,16},{16,24},{24,0},{1,9},{9,17},{17,25},{25,1},{2,10},{10... | collective-permute-start | bytes 313352 | tf_op jit(solution)/shard_map/ppermute | solution.py:426
  14.0 4.6 %collective-permute-start.3 = (f32[34,3,1,2,128]{4,3,2,1,0:T(2,128)S(1)}, f32[34,3,1,2,128]{4,3,2,1,0:T(2,128)S(1)}, u32[]{:S(2)}, u32[]{:S(2)}) collective-permute-start(f32[34,3,1,2,128]{4,3,2,1,0:T(2,128)S(1)} %get-tuple-element.17), channel_id=1, source_target_pairs={{8,0},{16,8},{24,16},{0,24},{9,1},{17,9},{25,17},{1,25},{10,2},{18... | collective-permute-start | bytes 313352 | tf_op jit(solution)/shard_map/ppermute | solution.py:428
  18.5 0.1 collective-permute-done.2
  18.7 1.5 collective-permute-done.3
  20.2 0.9 pad_maximum_fusion.1
  21.1 0.3 fusion
  21.4 1.9 %collective-permute-start.4 = (f32[34,3,4,1,128]{4,3,2,1,0:T(1,128)S(1)}, f32[34,3,4,1,128]{4,3,2,1,0:T(1,128)S(1)}, u32[]{:S(2)}, u32[]{:S(2)}) collective-permute-start(f32[34,3,4,1,128]{4,3,2,1,0:T(1,128)S(1)} %get-tuple-element.14), channel_id=1, source_target_pairs={{0,1},{1,2},{2,3},{3,4},{4,5},{5,6},{6,7},{7,0},{8,9},{9,10},{10,1... | collective-permute-start | bytes 626696 | tf_op jit(solution)/shard_map/ppermute | solution.py:426
  23.4 8.0 %collective-permute-start.5 = (f32[34,3,4,1,128]{4,3,2,1,0:T(1,128)S(1)}, f32[34,3,4,1,128]{4,3,2,1,0:T(1,128)S(1)}, u32[]{:S(2)}, u32[]{:S(2)}) collective-permute-start(f32[34,3,4,1,128]{4,3,2,1,0:T(1,128)S(1)} %get-tuple-element.15), channel_id=1, source_target_pairs={{1,0},{2,1},{3,2},{4,3},{5,4},{6,5},{7,6},{0,7},{9,8},{10,9},{11,1... | collective-permute-start | bytes 626696 | tf_op jit(solution)/shard_map/ppermute | solution.py:428
  31.4 1.6 %local_gram.1 = f32[32,1,128]{2,1,0:T(1,128)} custom-call(f32[6,6,4,128]{3,2,1,0:T(4,128)} %bitcast.35, s32[4,128]{1,0:T(4,128)} %bitcast.32), custom_call_target="tpu_custom_call" | custom-call | tf_op jit(solution)/shard_map/local_gram/pallas_call | solution.py:309
  33.0 6.7 %all-to-all-start = ((f32[32,1,128]{2,1,0:T(1,128)}), f32[32,1,128]{2,1,0:T(1,128)S(1)}, u32[]{:S(2)}, u32[]{:S(2)}) async-start(f32[32,1,128]{2,1,0:T(1,128)} %local_gram.1), calls=%async_computation | async-start | bytes 32768 | tf_op jit(solution)/shard_map/all_to_all | solution.py:439
  39.7 0.8 reshape.55.mask_ref
  40.5 7.9 %all-to-all-done.parts_ref = f32[32,1,128]{2,1,0:T(1,128)S(1)} async-done(((f32[32,1,128]{2,1,0:T(1,128)}), f32[32,1,128]{2,1,0:T(1,128)S(1)}, u32[]{:S(2)}, u32[]{:S(2)}) %all-to-all-start) | async-done | bytes 16416 | tf_op jit(solution)/shard_map/all_to_all | solution.py:439
  48.4 0.0 copy-start.4
  48.4 0.6 copy-done.4
  49.0 1.4 sum_parts.2
  50.3 11.8 %all-to-all-start.1 = ((f32[16,1,128]{2,1,0:T(1,128)}), f32[16,1,128]{2,1,0:T(1,128)S(1)}, u32[]{:S(2)}, u32[]{:S(2)}) async-start(f32[16,1,128]{2,1,0:T(1,128)} %sum_parts.2), calls=%async_computation.1 | async-start | bytes 16384 | tf_op jit(solution)/shard_map/all_to_all | solution.py:439
  62.2 0.0 collective-permute-done.4
  62.2 0.0 collective-permute-done.5
  62.2 1.3 pad_maximum_fusion
  63.5 11.1 %build_pairs.1 = (s32[116]{0:T(128)S(1)}, s32[1]{0:T(128)}, bf16[108,512,128]{2,1,0:T(8,128)(2,1)S(1)}) custom-call(s32[108]{0:T(128)S(1)} %reshape.55.mask_ref, f32[4,48,128]{2,1,0:T(8,128)S(1)} %bitcast.21), custom_call_target="tpu_custom_call" | custom-call | tf_op jit(solution)/shard_map/build_pairs/pallas_call | solution.py:150
  74.6 0.0 copy-start
  74.6 5.0 %copy-done = bf16[108,512,128]{2,1,0:T(8,128)(2,1)} copy-done((bf16[108,512,128]{2,1,0:T(8,128)(2,1)}, bf16[108,512,128]{2,1,0:T(8,128)(2,1)S(1)}, u32[]{:S(2)}) %copy-start) | copy-done | bytes 14155800
  79.7 0.0 all-to-all-done.1.gram_ref
  79.7 0.0 copy-start.1
  79.7 5.0 %copy-done.1 = bf16[108,512,128]{2,1,0:T(8,128)(2,1)S(1)} copy-done((bf16[108,512,128]{2,1,0:T(8,128)(2,1)S(1)}, bf16[108,512,128]{2,1,0:T(8,128)(2,1)}, u32[]{:S(2)}) %copy-start.1) | copy-done | bytes 14155800
  84.7 0.0 copy-start.2
  84.7 0.7 copy-done.2
  85.4 0.0 copy-start.3
  85.4 0.7 copy-done.3
  86.1 8.6 %first_field.1 = f32[6,4,128]{2,1,0:T(4,128)S(1)} custom-call(s32[116]{0:T(128)S(1)} %get-tuple-element.7.list_ref, s32[1]{0:T(128)} %get-tuple-element.8.count_ref, f32[16,1,128]{2,1,0:T(1,128)S(1)} %all-to-all-done.1.gram_ref, f32[4,48,128]{2,1,0:T(8,128)S(1)} %bitcast.22, f32[30,48,128]{2,1,0:T(8,128)S(1)} %bitcast.20, s32[4,128]{1,0:T(4,128)S(1)} %bitcast.33, ...), custom_call_target="tpu_custom_call" | custom-call | tf_op jit(solution)/shard_map/first_field/pallas_call | solution.py:393
  94.6 0.1 collective-permute-start.7
  94.7 1.6 %collective-permute-start.6 = (f32[6,1,2,2,128]{4,3,2,1,0:T(2,128)S(1)}, f32[6,1,2,2,128]{4,3,2,1,0:T(2,128)S(1)}, u32[]{:S(2)}, u32[]{:S(2)}) collective-permute-start(f32[6,1,2,2,128]{4,3,2,1,0:T(2,128)S(1)} %bitcast.26), channel_id=1, source_target_pairs={{0,32},{32,64},{64,96},{96,128},{128,160},{160,192},{192,224},{224... | collective-permute-start | bytes 36872 | tf_op jit(solution)/shard_map/ppermute | solution.py:426
  96.4 1.4 collective-permute-done.7
  97.8 0.5 collective-permute-done.6
  98.3 2.5 %collective-permute-start.8 = (f32[6,3,1,2,128]{4,3,2,1,0:T(2,128)S(1)}, f32[6,3,1,2,128]{4,3,2,1,0:T(2,128)S(1)}, u32[]{:S(2)}, u32[]{:S(2)}) collective-permute-start(f32[6,3,1,2,128]{4,3,2,1,0:T(2,128)S(1)} %get-tuple-element.20), channel_id=1, source_target_pairs={{0,8},{8,16},{16,24},{24,0},{1,9},{9,17},{17,25},{25,1},{2,10},{10... | collective-permute-start | bytes 55304 | tf_op jit(solution)/shard_map/ppermute | solution.py:426
  100.9 3.9 %collective-permute-start.9 = (f32[6,3,1,2,128]{4,3,2,1,0:T(2,128)S(1)}, f32[6,3,1,2,128]{4,3,2,1,0:T(2,128)S(1)}, u32[]{:S(2)}, u32[]{:S(2)}) collective-permute-start(f32[6,3,1,2,128]{4,3,2,1,0:T(2,128)S(1)} %get-tuple-element.21), channel_id=1, source_target_pairs={{8,0},{16,8},{24,16},{0,24},{9,1},{17,9},{25,17},{1,25},{10,2},{18... | collective-permute-start | bytes 55304 | tf_op jit(solution)/shard_map/ppermute | solution.py:428
  104.8 0.0 collective-permute-done.8
  104.8 0.9 collective-permute-done.9
  105.7 0.1 fusion.2
  105.8 1.9 %collective-permute-start.10 = (f32[6,3,4,1,128]{4,3,2,1,0:T(1,128)S(1)}, f32[6,3,4,1,128]{4,3,2,1,0:T(1,128)S(1)}, u32[]{:S(2)}, u32[]{:S(2)}) collective-permute-start(f32[6,3,4,1,128]{4,3,2,1,0:T(1,128)S(1)} %get-tuple-element.18), channel_id=1, source_target_pairs={{0,1},{1,2},{2,3},{3,4},{4,5},{5,6},{6,7},{7,0},{8,9},{9,10},{10,1... | collective-permute-start | bytes 110600 | tf_op jit(solution)/shard_map/ppermute | solution.py:426
  107.7 4.6 %collective-permute-start.11 = (f32[6,3,4,1,128]{4,3,2,1,0:T(1,128)S(1)}, f32[6,3,4,1,128]{4,3,2,1,0:T(1,128)S(1)}, u32[]{:S(2)}, u32[]{:S(2)}) collective-permute-start(f32[6,3,4,1,128]{4,3,2,1,0:T(1,128)S(1)} %get-tuple-element.19), channel_id=1, source_target_pairs={{1,0},{2,1},{3,2},{4,3},{5,4},{6,5},{7,6},{0,7},{9,8},{10,9},{11,1... | collective-permute-start | bytes 110600 | tf_op jit(solution)/shard_map/ppermute | solution.py:428
  112.3 0.0 collective-permute-done.10
  112.3 1.0 collective-permute-done.11
  113.3 0.1 pad_maximum_fusion.3
  113.4 7.7 %second_field.1 = (f32[6,4,128]{2,1,0:T(4,128)}, f32[32,1,128]{2,1,0:T(1,128)S(1)}) custom-call(s32[116]{0:T(128)S(1)} %get-tuple-element.7.list_ref, s32[1]{0:T(128)} %get-tuple-element.8.count_ref, f32[4,48,128]{2,1,0:T(8,128)S(1)} %bitcast.23, f32[6,48,128]{2,1,0:T(8,128)S(1)} %bitcast.24, s32[4,128]{1,0:T(4,128)S(1)} %bitcast.34, ...), custom_call_target="tpu_custom_call" | custom-call | tf_op jit(solution)/shard_map/second_field/pallas_call | solution.py:405
  121.2 15.8 %all_to_all.20.parts_ref = f32[32,1,128]{2,1,0:T(1,128)} all-to-all(f32[32,1,128]{2,1,0:T(1,128)S(1)} %get-tuple-element.11), channel_id=1, replica_groups=mesh['gx'=16,'gy'=4,'gz'=8] {'gy','gz'}, dimensions={0} | all-to-all | bytes 32768 | tf_op jit(solution)/shard_map/all_to_all | solution.py:439
  137.0 1.4 sum_parts.3
  138.4 18.4 %all_to_all.21 = f32[16,1,128]{2,1,0:T(1,128)S(1)} all-to-all(f32[16,1,128]{2,1,0:T(1,128)} %sum_parts.3), channel_id=1, replica_groups=mesh['gx'=16,'gy'=4,'gz'=8] {'gx'}, dimensions={0} | all-to-all | bytes 16384 | tf_op jit(solution)/shard_map/all_to_all | solution.py:439
  156.8 0.6 fusion.4
  (7 shorter events, 0.2 us)
Async XLA Ops:
  2.9 7.8 %collective-permute-start.1 = (f32[34,1,2,2,128]{4,3,2,1,0:T(2,128)S(1)}, f32[34,1,2,2,128]{4,3,2,1,0:T(2,128)S(1)}, u32[]{:S(2)}, u32[]{:S(2)}) collective-permute-start(f32[34,1,2,2,128]{4,3,2,1,0:T(2,128)S(1)} %pad_maximum_fusion.5), channel_id=1, source_target_pairs={{32,0},{64,32},{96,64},{128,96},{160,128},{192,160},{224,192},{256... | collective-permute-start | bytes 208904 | tf_op jit(solution)/shard_map/ppermute | solution.py:428
  9.8 1.4 collective-permute-start
  12.0 6.6 %collective-permute-start.2 = (f32[34,3,1,2,128]{4,3,2,1,0:T(2,128)S(1)}, f32[34,3,1,2,128]{4,3,2,1,0:T(2,128)S(1)}, u32[]{:S(2)}, u32[]{:S(2)}) collective-permute-start(f32[34,3,1,2,128]{4,3,2,1,0:T(2,128)S(1)} %get-tuple-element.16), channel_id=1, source_target_pairs={{0,8},{8,16},{16,24},{24,0},{1,9},{9,17},{17,25},{25,1},{2,10},{10... | collective-permute-start | bytes 313352 | tf_op jit(solution)/shard_map/ppermute | solution.py:426
  14.0 6.3 %collective-permute-start.3 = (f32[34,3,1,2,128]{4,3,2,1,0:T(2,128)S(1)}, f32[34,3,1,2,128]{4,3,2,1,0:T(2,128)S(1)}, u32[]{:S(2)}, u32[]{:S(2)}) collective-permute-start(f32[34,3,1,2,128]{4,3,2,1,0:T(2,128)S(1)} %get-tuple-element.17), channel_id=1, source_target_pairs={{8,0},{16,8},{24,16},{0,24},{9,1},{17,9},{25,17},{1,25},{10,2},{18... | collective-permute-start | bytes 313352 | tf_op jit(solution)/shard_map/ppermute | solution.py:428
  21.4 40.7 %collective-permute-start.4 = (f32[34,3,4,1,128]{4,3,2,1,0:T(1,128)S(1)}, f32[34,3,4,1,128]{4,3,2,1,0:T(1,128)S(1)}, u32[]{:S(2)}, u32[]{:S(2)}) collective-permute-start(f32[34,3,4,1,128]{4,3,2,1,0:T(1,128)S(1)} %get-tuple-element.14), channel_id=1, source_target_pairs={{0,1},{1,2},{2,3},{3,4},{4,5},{5,6},{6,7},{7,0},{8,9},{9,10},{10,1... | collective-permute-start | bytes 626696 | tf_op jit(solution)/shard_map/ppermute | solution.py:426
  23.4 38.8 %collective-permute-start.5 = (f32[34,3,4,1,128]{4,3,2,1,0:T(1,128)S(1)}, f32[34,3,4,1,128]{4,3,2,1,0:T(1,128)S(1)}, u32[]{:S(2)}, u32[]{:S(2)}) collective-permute-start(f32[34,3,4,1,128]{4,3,2,1,0:T(1,128)S(1)} %get-tuple-element.15), channel_id=1, source_target_pairs={{1,0},{2,1},{3,2},{4,3},{5,4},{6,5},{7,6},{0,7},{9,8},{10,9},{11,1... | collective-permute-start | bytes 626696 | tf_op jit(solution)/shard_map/ppermute | solution.py:428
  33.0 15.4 %all-to-all-start = ((f32[32,1,128]{2,1,0:T(1,128)}), f32[32,1,128]{2,1,0:T(1,128)S(1)}, u32[]{:S(2)}, u32[]{:S(2)}) async-start(f32[32,1,128]{2,1,0:T(1,128)} %local_gram.1), calls=%async_computation | async-start | bytes 32768 | tf_op jit(solution)/shard_map/all_to_all | solution.py:439
  48.4 0.6 copy-start.4
  50.3 29.3 %all-to-all-start.1 = ((f32[16,1,128]{2,1,0:T(1,128)}), f32[16,1,128]{2,1,0:T(1,128)S(1)}, u32[]{:S(2)}, u32[]{:S(2)}) async-start(f32[16,1,128]{2,1,0:T(1,128)} %sum_parts.2), calls=%async_computation.1 | async-start | bytes 16384 | tf_op jit(solution)/shard_map/all_to_all | solution.py:439
  74.6 5.0 %copy-start = (bf16[108,512,128]{2,1,0:T(8,128)(2,1)}, bf16[108,512,128]{2,1,0:T(8,128)(2,1)S(1)}, u32[]{:S(2)}) copy-start(bf16[108,512,128]{2,1,0:T(8,128)(2,1)S(1)} %get-tuple-element.9.pair_ref) | copy-start | bytes 42467332
  79.7 5.0 %copy-start.1 = (bf16[108,512,128]{2,1,0:T(8,128)(2,1)S(1)}, bf16[108,512,128]{2,1,0:T(8,128)(2,1)}, u32[]{:S(2)}) copy-start(bf16[108,512,128]{2,1,0:T(8,128)(2,1)} %copy-done) | copy-start | bytes 42467332
  84.7 0.7 copy-start.2
  85.4 0.7 copy-start.3
  94.6 3.1 %collective-permute-start.7 = (f32[6,1,2,2,128]{4,3,2,1,0:T(2,128)S(1)}, f32[6,1,2,2,128]{4,3,2,1,0:T(2,128)S(1)}, u32[]{:S(2)}, u32[]{:S(2)}) collective-permute-start(f32[6,1,2,2,128]{4,3,2,1,0:T(2,128)S(1)} %bitcast.25), channel_id=1, source_target_pairs={{32,0},{64,32},{96,64},{128,96},{160,128},{192,160},{224,192},{256... | collective-permute-start | bytes 36872 | tf_op jit(solution)/shard_map/ppermute | solution.py:428
  94.7 3.5 %collective-permute-start.6 = (f32[6,1,2,2,128]{4,3,2,1,0:T(2,128)S(1)}, f32[6,1,2,2,128]{4,3,2,1,0:T(2,128)S(1)}, u32[]{:S(2)}, u32[]{:S(2)}) collective-permute-start(f32[6,1,2,2,128]{4,3,2,1,0:T(2,128)S(1)} %bitcast.26), channel_id=1, source_target_pairs={{0,32},{32,64},{64,96},{96,128},{128,160},{160,192},{192,224},{224... | collective-permute-start | bytes 36872 | tf_op jit(solution)/shard_map/ppermute | solution.py:426
  98.3 6.5 %collective-permute-start.8 = (f32[6,3,1,2,128]{4,3,2,1,0:T(2,128)S(1)}, f32[6,3,1,2,128]{4,3,2,1,0:T(2,128)S(1)}, u32[]{:S(2)}, u32[]{:S(2)}) collective-permute-start(f32[6,3,1,2,128]{4,3,2,1,0:T(2,128)S(1)} %get-tuple-element.20), channel_id=1, source_target_pairs={{0,8},{8,16},{16,24},{24,0},{1,9},{9,17},{17,25},{25,1},{2,10},{10... | collective-permute-start | bytes 55304 | tf_op jit(solution)/shard_map/ppermute | solution.py:426
  100.9 4.8 %collective-permute-start.9 = (f32[6,3,1,2,128]{4,3,2,1,0:T(2,128)S(1)}, f32[6,3,1,2,128]{4,3,2,1,0:T(2,128)S(1)}, u32[]{:S(2)}, u32[]{:S(2)}) collective-permute-start(f32[6,3,1,2,128]{4,3,2,1,0:T(2,128)S(1)} %get-tuple-element.21), channel_id=1, source_target_pairs={{8,0},{16,8},{24,16},{0,24},{9,1},{17,9},{25,17},{1,25},{10,2},{18... | collective-permute-start | bytes 55304 | tf_op jit(solution)/shard_map/ppermute | solution.py:428
  105.8 6.5 %collective-permute-start.10 = (f32[6,3,4,1,128]{4,3,2,1,0:T(1,128)S(1)}, f32[6,3,4,1,128]{4,3,2,1,0:T(1,128)S(1)}, u32[]{:S(2)}, u32[]{:S(2)}) collective-permute-start(f32[6,3,4,1,128]{4,3,2,1,0:T(1,128)S(1)} %get-tuple-element.18), channel_id=1, source_target_pairs={{0,1},{1,2},{2,3},{3,4},{4,5},{5,6},{6,7},{7,0},{8,9},{9,10},{10,1... | collective-permute-start | bytes 110600 | tf_op jit(solution)/shard_map/ppermute | solution.py:426
  107.7 5.6 %collective-permute-start.11 = (f32[6,3,4,1,128]{4,3,2,1,0:T(1,128)S(1)}, f32[6,3,4,1,128]{4,3,2,1,0:T(1,128)S(1)}, u32[]{:S(2)}, u32[]{:S(2)}) collective-permute-start(f32[6,3,4,1,128]{4,3,2,1,0:T(1,128)S(1)} %get-tuple-element.19), channel_id=1, source_target_pairs={{1,0},{2,1},{3,2},{4,3},{5,4},{6,5},{7,6},{0,7},{9,8},{10,9},{11,1... | collective-permute-start | bytes 110600 | tf_op jit(solution)/shard_map/ppermute | solution.py:428

commit v2 on v1

v2 whole, which is shorter than its diff:
```python
import functools

import jax
import jax.numpy as jnp
from jax import lax
from jax.experimental import pallas as pl
from jax.experimental.pallas import tpu as pltpu

ALL = ("gx", "gy", "gz")
CELL_EDGE = 10.0
SOFTENING = 0.3
THOLE_DAMP = 0.39
RELAXATION = 0.7
LN2 = 0.6931471805599453

SLOTS = 128
NX, NY, NZ = 3, 4, 4
TILES = NX * NY * NZ
OWN = 4
OFFSETS = 27
TERMS = 48
A_ROWS = 96
B_ROWS = 24
BATCH = 8
PAIRS = OWN + OWN * (OFFSETS - 1)
LIST = 128
COUNT_AT = LIST - 1
GRAM = tuple((a, b) for a in range(6) for b in range(a + 1))


def source_tile(tile, offset):
    x = offset // 9
    y = tile // 2 + offset // 3 % 3
    z = tile % 2 + offset % 3
    return (x * NY + y) * NZ + z


OWN_TILES = tuple(source_tile(t, 13) for t in range(OWN))


def split3(value):
    high = value.astype(jnp.bfloat16).astype(jnp.float32)
    rest = value - high
    middle = rest.astype(jnp.bfloat16).astype(jnp.float32)
    return high, middle, rest - middle


def positions(geo):
    tile = lax.broadcasted_iota(jnp.int32, (TILES, SLOTS), 0)
    x = (tile // (NY * NZ)).astype(jnp.float32)
    y = (tile // NZ % NY).astype(jnp.float32)
    z = (tile % NZ).astype(jnp.float32)
    return (
        (geo[0] + (x - 1.5)) * CELL_EDGE,
        (geo[1] + (y - 2.0)) * CELL_EDGE,
        (geo[2] + (z - 2.0)) * CELL_EDGE,
    )


def scale_of(polar):
    factor = (THOLE_DAMP / LN2) ** (1.0 / 3.0)
    return factor * jnp.exp(jnp.log(polar) * (-1.0 / 3.0))


def own_rows(value):
    return [value[t : t + 1] for t in OWN_TILES]


def prepare_distances(geo, q_ref, p_ref):
    r = positions(geo)
    a = scale_of(geo[3])
    norm = r[0] * r[0] + r[1] * r[1] + r[2] * r[2]
    sources = [a, a * (norm + SOFTENING), a * r[0], a * r[1], a * r[2]]
    targets = [a * norm, a, -2.0 * a * r[0], -2.0 * a * r[1], -2.0 * a * r[2]]
    row = 0
    for source, target in zip(sources, targets):
        source_parts = split3(source)
        target_parts = split3(target)
        for s in range(3):
            for t in range(3):
                q_ref[pl.ds(row, TILES, stride=TERMS + 1), :] = source_parts[s]
                for own in range(OWN):
                    p_ref[own, row : row + 1, :] = target_parts[t][
                        OWN_TILES[own] : OWN_TILES[own] + 1
                    ]
                row += 1
    zero = jnp.zeros((TILES, SLOTS), jnp.float32)
    for rest in range(row, TERMS):
        q_ref[pl.ds(rest, TILES, stride=TERMS + 1), :] = zero
        for own in range(OWN):
            p_ref[own, rest : rest + 1, :] = zero[0:1]

    q_ref[TILES * (TERMS + 1) : TILES * (TERMS + 1) + TERMS, :] = q_ref[0:TERMS, :]


def list_pairs(mask_ref, list_ref):
    count = jnp.int32(OWN)
    for t in range(OWN):
        list_ref[t] = OWN_TILES[t] * OWN + t
    for t in range(OWN):
        for k in range(OFFSETS):
            if k == 13:
                continue
            list_ref[count] = source_tile(t, k) * OWN + t
            count = count + (mask_ref[t, k] != 0).astype(jnp.int32)
    for extra in range(BATCH):
        list_ref[count + extra] = TILES * OWN
    list_ref[COUNT_AT] = count
    return count


def pair_functions(n, t, q_ref, p_ref, keep):
    dist = lax.dot_general(
        q_ref[pl.ds(n * (TERMS + 1), TERMS), :].astype(jnp.bfloat16),
        p_ref[t].astype(jnp.bfloat16),
        (((0,), (0,)), ((), ())),
        preferred_element_type=jnp.float32,
    )
    inv = lax.rsqrt(dist)
    arg = dist * (dist * inv)
    damp = jnp.exp2(-arg)
    inv2 = inv * inv
    direct = (1.0 - damp) * (inv2 * inv)
    radial = inv2 * (direct - LN2 * damp)
    if keep is not None:
        direct = jnp.where(keep, direct, 0.0)
        radial = jnp.where(keep, radial, 0.0)
    result = []
    for value in (radial, direct):
        high = value.astype(jnp.bfloat16)
        low = (value - high.astype(jnp.float32)).astype(jnp.bfloat16)
        result.append(jnp.concatenate([high, low], axis=0))
    return result


def prepare_moments(geo, moment, a_ref, b_ref):
    r = positions(geo)
    scale_a, scale_b = factors(geo)
    zero = jnp.zeros((TILES, SLOTS), jnp.float32)
    for kind in range(2):
        m = [moment[3 * kind + c] * scale_a for c in range(3)]
        outer = [r[c] * m[d] for c in range(3) for d in range(3)]
        g = outer[0] + outer[4] + outer[8]
        values = [None] + [r[c] * g for c in range(3)] + m + outer
        for index, value in enumerate(values):
            parts = (zero, zero, zero) if value is None else split3(value)
            for s, part in enumerate(parts):
                row = 32 * s + 16 * kind + index
                a_ref[pl.ds(row, TILES, stride=A_ROWS + 1), :] = part
    for c in range(8):
        parts = (zero, zero, zero) if c >= 6 else split3(moment[c] * scale_b)
        for s, part in enumerate(parts):
            b_ref[pl.ds(8 * s + c, TILES, stride=B_ROWS + 1), :] = part
    a_ref[TILES * (A_ROWS + 1) : TILES * (A_ROWS + 1) + A_ROWS, :] = jnp.zeros((A_ROWS, SLOTS), jnp.float32)
    b_ref[TILES * (B_ROWS + 1) : TILES * (B_ROWS + 1) + B_ROWS, :] = jnp.zeros((B_ROWS, SLOTS), jnp.float32)


def factors(geo):
    a = scale_of(geo[3])
    scale_b = a * jnp.sqrt(a)
    return scale_b * a, scale_b


def product(n, radial, direct, a_ref, b_ref):
    left = a_ref[pl.ds(n * (A_ROWS + 1), A_ROWS), :].astype(jnp.bfloat16)
    part_a = jnp.dot(
        jnp.concatenate([left, left], axis=1), radial, preferred_element_type=jnp.float32
    )
    left = b_ref[pl.ds(n * (B_ROWS + 1), B_ROWS), :].astype(jnp.bfloat16)
    part_b = jnp.dot(
        jnp.concatenate([left, left], axis=1), direct, preferred_element_type=jnp.float32
    )
    return part_a, part_b


def field_of(geo, sum_a, sum_b):
    r = positions(geo)
    scale_a, scale_b = factors(geo)
    own_r = [jnp.concatenate(own_rows(r[c]), 0) for c in range(3)]
    own_a = 3.0 * jnp.concatenate(own_rows(scale_a), 0)
    own_b = jnp.concatenate(own_rows(scale_b), 0)

    def total_a(kind, index):
        row = 16 * kind + index
        return sum_a[:, row, :] + sum_a[:, 32 + row, :] + sum_a[:, 64 + row, :]

    def total_b(row):
        return sum_b[:, row, :] + sum_b[:, 8 + row, :] + sum_b[:, 16 + row, :]

    fields = []
    for kind in range(2):
        outer = [[total_a(kind, 7 + 3 * c + d) for d in range(3)] for c in range(3)]
        g = outer[0][0] + outer[1][1] + outer[2][2]
        m = [total_a(kind, 4 + c) for c in range(3)]
        dot = own_r[0] * m[0] + own_r[1] * m[1] + own_r[2] * m[2] - g
        for c in range(3):
            cross = sum(own_r[d] * outer[c][d] for d in range(3))
            radial = total_a(kind, 1 + c) - cross + own_r[c] * dot
            fields.append(own_a * radial - own_b * total_b(3 * kind + c))
    return fields


def own_part(value):
    return jnp.concatenate(own_rows(value), 0)


def solve(gram):
    count = 5
    matrix = [[gram[max(a, b), min(a, b)] for b in range(count)] for a in range(count)]
    right = [gram[count, a] for a in range(count)]
    trace = matrix[0][0]
    for a in range(1, count):
        trace = trace + matrix[a][a]
    ridge = 0.001 * trace / count + 1.0
    for a in range(count):
        matrix[a][a] = matrix[a][a] + ridge
    for c in range(count):
        for a in range(c + 1, count):
            ratio = matrix[a][c] / matrix[c][c]
            for b in range(c + 1, a + 1):
                matrix[a][b] = matrix[a][b] - ratio * matrix[b][c]
            right[a] = right[a] - ratio * right[c]
    result = [None] * count
    for a in reversed(range(count)):
        rest = right[a]
        for b in range(a + 1, count):
            rest = rest - matrix[b][a] * result[b]
        result[a] = rest / matrix[a][a]
    return result


def gram_kernel(history_ref, occupancy_ref, out_ref):
    filled = occupancy_ref[...].astype(jnp.float32)
    masked = [
        [history_ref[h, c] * filled for c in range(6)] for h in range(6)
    ]
    lane = lax.broadcasted_iota(jnp.int32, (1, SLOTS), 1)
    row = jnp.zeros((1, SLOTS), jnp.float32)
    for index, (a, b) in enumerate(GRAM):
        product = masked[a][0] * masked[b][0]
        for c in range(1, 6):
            product = product + masked[a][c] * masked[b][c]
        total = jnp.sum(jnp.sum(product, axis=0, keepdims=True), axis=1, keepdims=True)
        row = jnp.where(lane == index, total, row)
    out_ref[...] = jnp.broadcast_to(row[None], out_ref.shape)


def vmem_spec():
    return pl.BlockSpec(memory_space=pltpu.VMEM)


def smem_spec():
    return pl.BlockSpec(memory_space=pltpu.SMEM)


def local_gram(history, occupancy, copies):
    return pl.pallas_call(
        gram_kernel,
        name="local_gram",
        in_specs=[vmem_spec(), vmem_spec()],
        out_specs=vmem_spec(),
        out_shape=jax.ShapeDtypeStruct((copies, 1, SLOTS), jnp.float32),
    )(history, occupancy)


def sum_parts(parts, copies):
    total = jnp.sum(parts, axis=0, keepdims=True)
    return jnp.broadcast_to(total, (copies,) + total.shape[1:])


SCRATCH = [
    pltpu.VMEM(((TILES + 1) * (A_ROWS + 1), SLOTS), jnp.float32),
    pltpu.VMEM(((TILES + 1) * (B_ROWS + 1), SLOTS), jnp.float32),
    pltpu.VMEM((OWN, A_ROWS, SLOTS), jnp.float32),
    pltpu.VMEM((OWN, B_ROWS, SLOTS), jnp.float32),
]


def first_kernel(
    mask_ref, gram_ref, geo_ref, later_ref, occupancy_ref, perm_ref,
    out_ref, list_ref, pair_ref, q_ref, p_ref, a_ref, b_ref, sum_a, sum_b,
):
    geo = [geo_ref[a] for a in range(4)]
    total = jnp.sum(gram_ref[...], axis=0)
    gram = {ab: total[0:1, i : i + 1] for i, ab in enumerate(GRAM)}
    coeffs = solve(gram)
    moment = []
    for c in range(6):
        value = coeffs[0] * later_ref[c]
        for h in range(1, 5):
            value = value + coeffs[h] * later_ref[6 * h + c]
        moment.append(value)
    prepare_distances(geo, q_ref, p_ref)
    prepare_moments(geo, moment, a_ref, b_ref)
    count = list_pairs(mask_ref, list_ref)

    def pair(slot, n, t, keep):
        radial, direct = pair_functions(n, t, q_ref, p_ref, keep)
        pair_ref[slot, 0 : 2 * SLOTS, :] = radial
        pair_ref[slot, 2 * SLOTS : 4 * SLOTS, :] = direct
        return product(n, radial, direct, a_ref, b_ref)

    keep = lax.broadcasted_iota(jnp.int32, (SLOTS, SLOTS), 0) != lax.broadcasted_iota(
        jnp.int32, (SLOTS, SLOTS), 1
    )
    for slot in range(OWN):
        sum_a[slot], sum_b[slot] = pair(slot, OWN_TILES[slot], slot, keep)

    def batch(b, carry):
        for u in range(BATCH):
            slot = OWN + b * BATCH + u
            entry = list_ref[slot]
            t = entry % OWN
            part_a, part_b = pair(slot, entry // OWN, t, None)
            sum_a[t] += part_a
            sum_b[t] += part_b
        return carry

    lax.fori_loop(0, (count - OWN + BATCH - 1) // BATCH, batch, 0)
    fields = field_of(geo, sum_a, sum_b)
    scaled = RELAXATION * occupancy_ref[...].astype(jnp.float32) * own_part(geo[3])
    for c in range(6):
        out_ref[c] = (1.0 - RELAXATION) * own_part(moment[c]) + scaled * (
            perm_ref[c] + fields[c]
        )


def second_kernel(
    list_ref, geo_ref, dipole_ref, occupancy_ref, perm_ref, pair_ref,
    out_ref, size_ref, a_ref, b_ref, sum_a, sum_b,
):
    geo = [geo_ref[a] for a in range(4)]
    moment = [dipole_ref[c] for c in range(6)]
    prepare_moments(geo, moment, a_ref, b_ref)

    def pair(slot, n):
        return product(
            n,
            pair_ref[slot, 0 : 2 * SLOTS, :],
            pair_ref[slot, 2 * SLOTS : 4 * SLOTS, :],
            a_ref,
            b_ref,
        )

    for slot in range(OWN):
        sum_a[slot], sum_b[slot] = pair(slot, OWN_TILES[slot])

    def batch(b, carry):
        for u in range(BATCH):
            slot = OWN + b * BATCH + u
            entry = list_ref[slot]
            t = entry % OWN
            part_a, part_b = pair(slot, entry // OWN)
            sum_a[t] += part_a
            sum_b[t] += part_b
        return carry

    lax.fori_loop(0, (list_ref[COUNT_AT] - OWN + BATCH - 1) // BATCH, batch, 0)
    fields = field_of(geo, sum_a, sum_b)
    scaled = RELAXATION * occupancy_ref[...].astype(jnp.float32) * own_part(geo[3])
    moved = jnp.zeros((OWN, SLOTS), jnp.float32)
    size = jnp.zeros((OWN, SLOTS), jnp.float32)
    for c in range(6):
        old = own_part(moment[c])
        new = (1.0 - RELAXATION) * old + scaled * (perm_ref[c] + fields[c])
        out_ref[c] = new
        moved = moved + (new - old) * (new - old)
        size = size + new * new
    for index, value in enumerate((moved, size)):
        total = jnp.sum(jnp.sum(value, axis=0, keepdims=True), axis=1, keepdims=True)
        size_ref[:, index : index + 1, :] = jnp.broadcast_to(
            total[None], (size_ref.shape[0], 1, SLOTS)
        )


def first_field(mask, gram, geo, later, occupancy, perm):
    return pl.pallas_call(
        first_kernel,
        name="first_field",
        in_specs=[smem_spec()] + [vmem_spec()] * 5,
        out_specs=[vmem_spec(), smem_spec(), vmem_spec()],
        out_shape=[
            jax.ShapeDtypeStruct((6, OWN, SLOTS), jnp.float32),
            jax.ShapeDtypeStruct((LIST,), jnp.int32),
            jax.ShapeDtypeStruct((PAIRS, 4 * SLOTS, SLOTS), jnp.bfloat16),
        ],
        scratch_shapes=[
            pltpu.VMEM(((TILES + 1) * (TERMS + 1), SLOTS), jnp.float32),
            pltpu.VMEM((OWN, TERMS, SLOTS), jnp.float32),
        ]
        + SCRATCH,
        compiler_params=pltpu.CompilerParams(vmem_limit_bytes=24 * 1024 * 1024),
        cost_estimate=pl.CostEstimate(
            flops=2_000_000_000, bytes_accessed=1_000_000, transcendentals=0
        ),
    )(mask, gram, geo, later, occupancy, perm)


def second_field(pair_list, geo, dipoles, occupancy, perm, pairs, copies):
    return pl.pallas_call(
        second_kernel,
        name="second_field",
        in_specs=[smem_spec()] + [vmem_spec()] * 5,
        out_specs=[vmem_spec(), vmem_spec()],
        out_shape=[
            jax.ShapeDtypeStruct((6, OWN, SLOTS), jnp.float32),
            jax.ShapeDtypeStruct((copies, 2, SLOTS), jnp.float32),
        ],
        scratch_shapes=SCRATCH,
        compiler_params=pltpu.CompilerParams(vmem_limit_bytes=24 * 1024 * 1024),
        cost_estimate=pl.CostEstimate(
            flops=1_000_000_000, bytes_accessed=1_000_000, transcendentals=0
        ),
    )(pair_list, geo, dipoles, occupancy, perm, pairs)


def with_halo(cells, sides):
    for axis, dim in sides:
        count = lax.axis_size(axis)
        head = lax.slice_in_dim(cells, 0, 1, axis=dim)
        tail = lax.slice_in_dim(cells, cells.shape[dim] - 1, cells.shape[dim], axis=dim)
        cells = jnp.concatenate(
            [
                lax.ppermute(tail, axis, [(i, (i + 1) % count) for i in range(count)]),
                cells,
                lax.ppermute(head, axis, [((i + 1) % count, i) for i in range(count)]),
            ],
            axis=dim,
        )
    return cells


SIDES = (("gx", 1), ("gy", 2), ("gz", 3))


def exchange(parts, axes):
    return lax.all_to_all(parts, axes, 0, 0)


def on_device(fractions, polarizability, occupancy, pair_mask, perm_field, history):
    plane = lax.axis_size("gy") * lax.axis_size("gz")
    line = lax.axis_size("gx")
    history = history.reshape(6, 6, OWN, SLOTS)
    occupancy = occupancy.reshape(OWN, SLOTS)
    perm = perm_field.reshape(6, OWN, SLOTS)

    gram = local_gram(history, occupancy, plane)
    filled = occupancy.astype(jnp.float32)
    later = (history[1:] * filled).reshape(30, 1, 2, 2, SLOTS)
    stacked = jnp.concatenate([fractions, polarizability[None], later], 0)
    stacked, gram = lax.optimization_barrier((stacked, gram))
    gram = exchange(gram, ("gy", "gz"))
    ghosts = with_halo(stacked, SIDES[:2])
    gram = sum_parts(gram, line)
    ghosts, gram = lax.optimization_barrier((ghosts, gram))
    gram = exchange(gram, "gx")
    ghosts = with_halo(ghosts, SIDES[2:])

    geo = ghosts[:4].reshape(4, TILES, SLOTS)
    later = ghosts[4:].reshape(30, TILES, SLOTS)
    dipoles, pair_list, pairs = first_field(
        pair_mask.reshape(OWN, OFFSETS), gram, geo, later, occupancy, perm
    )
    dipoles = with_halo(dipoles.reshape(6, 1, 2, 2, SLOTS), SIDES).reshape(6, TILES, SLOTS)
    induced, sizes = second_field(
        pair_list, geo, dipoles, occupancy, perm, pairs, plane
    )
    sizes = exchange(sizes, ("gy", "gz"))
    sizes = exchange(sum_parts(sizes, line), "gx")
    totals = jnp.sum(sizes, axis=0)
    change = jnp.sqrt(totals[0] / (totals[1] + 1.0))
    return induced.reshape(6, 1, 2, 2, SLOTS), change[0]


def solution(mesh):
    from jax.sharding import PartitionSpec as P

    tiles = P("gx", "gy", "gz", None)
    sets = P(None, "gx", "gy", "gz", None)
    return jax.shard_map(
        on_device,
        mesh=mesh,
        in_specs=(
            sets,
            tiles,
            tiles,
            tiles,
            sets,
            P(None, None, "gx", "gy", "gz", None),
        ),
        out_specs=(sets, P()),
        check_vma=False,
    )
```

time: 161 us -> 139 us (0.86)
  blocking collectives: 34.2 us -> 52.7 us
  starting transfers between devices: 56.5 us -> 44.4 us
  local copies, waits for them, and re-layouts: 14.8 us -> 4.74 us
  Pallas kernels: 31.7 us -> 22.9 us
  waiting for transfers between devices: 14.7 us -> 10.5 us
  between operations: 3.35 us -> 0.83 us
    all_to_all x2 -> x3, blocking collectives: 34.2 us -> 52.7 us  [exchange(): return lax.all_to_all(parts, axes, 0, 0)]
    unnamed x10, local copies, waits for them, and re-layouts: 12 us -> 2.8 us
    pallas_call x5 -> x2, Pallas kernels: 30.1 us -> 21.3 us  [the longest x1 16.9 us: first_field(): pl.pallas_call(first_kernel, name='first_field', in_specs=[smem_spec()] +...]
    all_to_all x2 -> x1, starting transfers between devices: 18.5 us -> 9.77 us  [exchange(): return lax.all_to_all(parts, axes, 0, 0)]
    ppermute x6, starting transfers between devices: 28 us -> 22.5 us  [with_halo(): lax.ppermute(head, axis, [((i + 1) % count, i) for i in range(count)])]
    ppermute x6, waiting for transfers between devices: 5.71 us -> 3.4 us  [with_halo(): lax.ppermute(head, axis, [((i + 1) % count, i) for i in range(count)])]
    concatenate x6 -> x5, other arithmetic: 3.12 us -> 0.84 us  [with_halo(): jnp.concatenate([lax.ppermute(tail, axis, [(i, (i + 1) % count) for i in...]
    ppermute x6, starting transfers between devices: 9.95 us -> 12.1 us  [with_halo(): lax.ppermute(tail, axis, [(i, (i + 1) % count) for i in range(count)])]
  transfers between devices with their start and end apart: 14 -> 13, of which waited for: 9 -> 6; matrix products, arithmetic and copies ran while one was open for 1% -> 0% of each run, Pallas kernels for 9% -> 0%
where the time goes in v2:
time: 139 us
  blocking collectives  52.7 us (38%)
  starting transfers between devices  44.4 us (32%)
  Pallas kernels  22.9 us (16%)
  waiting for transfers between devices  10.5 us (8%)
  local copies, waits for them, and re-layouts  4.74 us (3%)
  other arithmetic  3.02 us (2%)
    all_to_all x3, blocking collectives, exchange(): return lax.all_to_all(parts, axes, 0, 0)  52.7 us
    ppermute x6, starting transfers between devices, with_halo(): lax.ppermute(head, axis, [((i + 1) % count, i) for i in range(count)])  22.5 us
    pallas_call x1, Pallas kernels, first_field(): pl.pallas_call(first_kernel, name='first_field', in_specs=[smem_spec()] +...  16.9 us
    ppermute x6, starting transfers between devices, with_halo(): lax.ppermute(tail, axis, [(i, (i + 1) % count) for i in range(count)])  12.1 us
    all_to_all x1, starting transfers between devices, exchange(): return lax.all_to_all(parts, axes, 0, 0)  9.77 us
    all_to_all x1, waiting for transfers between devices, exchange(): return lax.all_to_all(parts, axes, 0, 0)  6.37 us
    pallas_call x1, Pallas kernels, second_field(): pl.pallas_call(second_kernel, name='second_field', in_specs=[smem_spec()]...  4.43 us
    ppermute x6, waiting for transfers between devices, with_halo(): lax.ppermute(head, axis, [((i + 1) % count, i) for i in range(count)])  3.4 us
  transfers between devices with their start and end apart: 13, of which 6 were waited for; matrix products, arithmetic and copies ran while one was open for 0% of the time, Pallas kernels for 0%

profile of v2, /device:TPU:1, one launch (start us, length us, event | category | flops | bytes accessed | tf_op | source)
XLA Modules:
  0.0 139.1 jit_solution(616374105974707017)
XLA Ops:
  0.6 0.7 convert_bitcast_fusion
  1.3 0.8 slice.46
  2.1 1.6 %local_gram.1 = f32[32,1,128]{2,1,0:T(1,128)} custom-call(f32[6,6,4,128]{3,2,1,0:T(4,128)} %bitcast.37, s32[4,128]{1,0:T(4,128)} %bitcast.31), custom_call_target="tpu_custom_call" | custom-call | tf_op jit(solution)/shard_map/local_gram/pallas_call | solution.py:257
  3.8 0.7 pad_maximum_fusion.6
  4.6 2.7 %collective-permute-start = (f32[34,1,2,2,128]{4,3,2,1,0:T(2,128)S(1)}, f32[34,1,2,2,128]{4,3,2,1,0:T(2,128)S(1)}, u32[]{:S(2)}, u32[]{:S(2)}) collective-permute-start(f32[34,1,2,2,128]{4,3,2,1,0:T(2,128)S(1)} %pad_maximum_fusion.6), channel_id=1, source_target_pairs={{0,32},{32,64},{64,96},{96,128},{128,160},{160,192},{192,224},{224... | collective-permute-start | bytes 208904 | tf_op jit(solution)/shard_map/ppermute | solution.py:424
  7.2 4.2 %collective-permute-start.1 = (f32[34,1,2,2,128]{4,3,2,1,0:T(2,128)S(1)}, f32[34,1,2,2,128]{4,3,2,1,0:T(2,128)S(1)}, u32[]{:S(2)}, u32[]{:S(2)}) collective-permute-start(f32[34,1,2,2,128]{4,3,2,1,0:T(2,128)S(1)} %pad_maximum_fusion.6), channel_id=1, source_target_pairs={{32,0},{64,32},{96,64},{128,96},{160,128},{192,160},{224,192},{256... | collective-permute-start | bytes 208904 | tf_op jit(solution)/shard_map/ppermute | solution.py:426
  11.4 0.7 collective-permute-done
  12.2 0.1 collective-permute-done.1
  12.4 0.1 fusion.2
  12.4 1.9 %collective-permute-start.2 = (f32[34,3,1,2,128]{4,3,2,1,0:T(2,128)S(1)}, f32[34,3,1,2,128]{4,3,2,1,0:T(2,128)S(1)}, u32[]{:S(2)}, u32[]{:S(2)}) collective-permute-start(f32[34,3,1,2,128]{4,3,2,1,0:T(2,128)S(1)} %get-tuple-element.28), channel_id=1, source_target_pairs={{0,8},{8,16},{16,24},{24,0},{1,9},{9,17},{17,25},{25,1},{2,10},{10... | collective-permute-start | bytes 313352 | tf_op jit(solution)/shard_map/ppermute | solution.py:424
  14.4 4.6 %collective-permute-start.3 = (f32[34,3,1,2,128]{4,3,2,1,0:T(2,128)S(1)}, f32[34,3,1,2,128]{4,3,2,1,0:T(2,128)S(1)}, u32[]{:S(2)}, u32[]{:S(2)}) collective-permute-start(f32[34,3,1,2,128]{4,3,2,1,0:T(2,128)S(1)} %get-tuple-element.29), channel_id=1, source_target_pairs={{8,0},{16,8},{24,16},{0,24},{9,1},{17,9},{25,17},{1,25},{10,2},{18... | collective-permute-start | bytes 313352 | tf_op jit(solution)/shard_map/ppermute | solution.py:426
  19.0 19.0 %all_to_all.20 = f32[32,1,128]{2,1,0:T(1,128)S(1)} all-to-all(f32[32,1,128]{2,1,0:T(1,128)} %local_gram.1), channel_id=1, replica_groups=mesh['gx'=16,'gy'=4,'gz'=8] {'gy','gz'}, dimensions={0} | all-to-all | bytes 32768 | tf_op jit(solution)/shard_map/all_to_all | solution.py:437
  37.9 0.1 reduce_sum.27
  38.0 0.0 collective-permute-done.2
  38.0 0.0 collective-permute-done.3
  38.0 0.2 pad_maximum_fusion.2
  38.2 0.6 broadcast_in_dim.7
  38.8 0.3 fusion.1
  39.1 2.2 %collective-permute-start.4 = (f32[34,3,4,1,128]{4,3,2,1,0:T(1,128)S(1)}, f32[34,3,4,1,128]{4,3,2,1,0:T(1,128)S(1)}, u32[]{:S(2)}, u32[]{:S(2)}) collective-permute-start(f32[34,3,4,1,128]{4,3,2,1,0:T(1,128)S(1)} %get-tuple-element.26), channel_id=1, source_target_pairs={{0,1},{1,2},{2,3},{3,4},{4,5},{5,6},{6,7},{7,0},{8,9},{9,10},{10,1... | collective-permute-start | bytes 626696 | tf_op jit(solution)/shard_map/ppermute | solution.py:424
  41.4 4.3 %collective-permute-start.5 = (f32[34,3,4,1,128]{4,3,2,1,0:T(1,128)S(1)}, f32[34,3,4,1,128]{4,3,2,1,0:T(1,128)S(1)}, u32[]{:S(2)}, u32[]{:S(2)}) collective-permute-start(f32[34,3,4,1,128]{4,3,2,1,0:T(1,128)S(1)} %get-tuple-element.27), channel_id=1, source_target_pairs={{1,0},{2,1},{3,2},{4,3},{5,4},{6,5},{7,6},{0,7},{9,8},{10,9},{11,1... | collective-permute-start | bytes 626696 | tf_op jit(solution)/shard_map/ppermute | solution.py:426
  45.6 9.8 %all-to-all-start.1 = ((f32[16,1,128]{2,1,0:T(1,128)}), f32[16,1,128]{2,1,0:T(1,128)S(1)}, u32[]{:S(2)}, u32[]{:S(2)}) async-start(f32[16,1,128]{2,1,0:T(1,128)} %broadcast_in_dim.7), calls=%async_computation.1 | async-start | bytes 16384 | tf_op jit(solution)/shard_map/all_to_all | solution.py:437
  55.4 0.0 collective-permute-done.4
  55.4 0.0 collective-permute-done.5
  55.4 0.5 pad_maximum_fusion
  55.9 0.1 pad_maximum_fusion.4
  56.0 6.4 %all-to-all-done.1.gram_ref = f32[16,1,128]{2,1,0:T(1,128)S(1)} async-done(((f32[16,1,128]{2,1,0:T(1,128)}), f32[16,1,128]{2,1,0:T(1,128)S(1)}, u32[]{:S(2)}, u32[]{:S(2)}) %all-to-all-start.1) | async-done | bytes 8224 | tf_op jit(solution)/shard_map/all_to_all | solution.py:437
  62.4 0.0 copy-start
  62.4 0.7 copy-done
  63.0 0.0 copy-start.1
  63.0 0.7 copy-done.1
  63.8 0.0 copy-start.3
  63.8 0.7 copy-done.3
  64.4 16.9 %first_field.1 = (f32[6,4,128]{2,1,0:T(4,128)S(1)}, s32[128]{0:T(128)S(1)}, bf16[108,512,128]{2,1,0:T(8,128)(2,1)S(1)}) custom-call(s32[4,27]{1,0:T(4,128)S(1)} %bitcast.36, f32[16,1,128]{2,1,0:T(1,128)S(1)} %all-to-all-done.1.gram_ref, f32[4,48,128]{2,1,0:T(8,128)S(1)} %bitcast.24, f32[30,48,128]{2,1,0:T(8,128)S(1)} %bitcast.22, s32[4,128]{1,0:T(4,128)S(1)} %bitcast.32, ...), custom_call_target="tpu_custom_call" | custom-call | flops 2000000000 | bytes 1000000 | tf_op jit(solution)/shard_map/first_field/pallas_call | solution.py:377
  81.3 0.7 collective-permute-start.7
  82.0 1.1 collective-permute-start.6
  83.1 1.4 collective-permute-done.7
  84.4 0.0 collective-permute-done.6
  84.5 2.2 %collective-permute-start.8 = (f32[6,3,1,2,128]{4,3,2,1,0:T(2,128)S(1)}, f32[6,3,1,2,128]{4,3,2,1,0:T(2,128)S(1)}, u32[]{:S(2)}, u32[]{:S(2)}) collective-permute-start(f32[6,3,1,2,128]{4,3,2,1,0:T(2,128)S(1)} %get-tuple-element.32), channel_id=1, source_target_pairs={{0,8},{8,16},{16,24},{24,0},{1,9},{9,17},{17,25},{25,1},{2,10},{10... | collective-permute-start | bytes 55304 | tf_op jit(solution)/shard_map/ppermute | solution.py:424
  86.8 4.2 %collective-permute-start.9 = (f32[6,3,1,2,128]{4,3,2,1,0:T(2,128)S(1)}, f32[6,3,1,2,128]{4,3,2,1,0:T(2,128)S(1)}, u32[]{:S(2)}, u32[]{:S(2)}) collective-permute-start(f32[6,3,1,2,128]{4,3,2,1,0:T(2,128)S(1)} %get-tuple-element.33), channel_id=1, source_target_pairs={{8,0},{16,8},{24,16},{0,24},{9,1},{17,9},{25,17},{1,25},{10,2},{18... | collective-permute-start | bytes 55304 | tf_op jit(solution)/shard_map/ppermute | solution.py:426
  91.0 0.0 collective-permute-done.8
  91.0 0.9 collective-permute-done.9
  91.9 0.1 fusion.3
  92.0 1.9 %collective-permute-start.10 = (f32[6,3,4,1,128]{4,3,2,1,0:T(1,128)S(1)}, f32[6,3,4,1,128]{4,3,2,1,0:T(1,128)S(1)}, u32[]{:S(2)}, u32[]{:S(2)}) collective-permute-start(f32[6,3,4,1,128]{4,3,2,1,0:T(1,128)S(1)} %get-tuple-element.30), channel_id=1, source_target_pairs={{0,1},{1,2},{2,3},{3,4},{4,5},{5,6},{6,7},{7,0},{8,9},{9,10},{10,1... | collective-permute-start | bytes 110600 | tf_op jit(solution)/shard_map/ppermute | solution.py:424
  93.9 4.6 %collective-permute-start.11 = (f32[6,3,4,1,128]{4,3,2,1,0:T(1,128)S(1)}, f32[6,3,4,1,128]{4,3,2,1,0:T(1,128)S(1)}, u32[]{:S(2)}, u32[]{:S(2)}) collective-permute-start(f32[6,3,4,1,128]{4,3,2,1,0:T(1,128)S(1)} %get-tuple-element.31), channel_id=1, source_target_pairs={{1,0},{2,1},{3,2},{4,3},{5,4},{6,5},{7,6},{0,7},{9,8},{10,9},{11,1... | collective-permute-start | bytes 110600 | tf_op jit(solution)/shard_map/ppermute | solution.py:426
  98.5 0.0 collective-permute-done.10
  98.5 1.0 collective-permute-done.11
  99.5 0.1 pad_maximum_fusion.3
  99.6 0.0 copy-start.2
  99.6 0.7 copy-done.2
  100.3 4.4 %second_field.1 = (f32[6,4,128]{2,1,0:T(4,128)}, f32[32,2,128]{2,1,0:T(2,128)S(1)}) custom-call(s32[128]{0:T(128)S(1)} %get-tuple-element.15.list_ref, f32[4,48,128]{2,1,0:T(8,128)S(1)} %bitcast.25, f32[6,48,128]{2,1,0:T(8,128)S(1)} %bitcast.23, s32[4,128]{1,0:T(4,128)S(1)} %bitcast.33, f32[6,4,128]{2,1,0:T(4,128)S(1)} %bitcast.35, ...), custom_call_target="tpu_custom_call" | custom-call | flops 1000000000 | bytes 1000000 | tf_op jit(solution)/shard_map/second_field/pallas_call | solution.py:400
  104.8 15.8 %all_to_all.21 = f32[32,2,128]{2,1,0:T(2,128)S(1)} all-to-all(f32[32,2,128]{2,1,0:T(2,128)S(1)} %get-tuple-element.19), channel_id=1, replica_groups=mesh['gx'=16,'gy'=4,'gz'=8] {'gy','gz'}, dimensions={0} | all-to-all | bytes 65536 | tf_op jit(solution)/shard_map/all_to_all | solution.py:437
  120.6 17.9 %all_to_all.22 = f32[16,2,128]{2,1,0:T(2,128)S(1)} all-to-all(f32[16,2,128]{2,1,0:T(2,128)S(1)} %broadcast_in_dim.8), channel_id=1, replica_groups=mesh['gx'=16,'gy'=4,'gz'=8] {'gx'}, dimensions={0} | all-to-all | bytes 32768 | tf_op jit(solution)/shard_map/all_to_all | solution.py:437
  138.6 0.5 fusion
  (10 shorter events, 0.2 us)
Async XLA Ops:
  4.6 7.6 %collective-permute-start = (f32[34,1,2,2,128]{4,3,2,1,0:T(2,128)S(1)}, f32[34,1,2,2,128]{4,3,2,1,0:T(2,128)S(1)}, u32[]{:S(2)}, u32[]{:S(2)}) collective-permute-start(f32[34,1,2,2,128]{4,3,2,1,0:T(2,128)S(1)} %pad_maximum_fusion.6), channel_id=1, source_target_pairs={{0,32},{32,64},{64,96},{96,128},{128,160},{160,192},{192,224},{224... | collective-permute-start | bytes 208904 | tf_op jit(solution)/shard_map/ppermute | solution.py:424
  7.2 5.1 %collective-permute-start.1 = (f32[34,1,2,2,128]{4,3,2,1,0:T(2,128)S(1)}, f32[34,1,2,2,128]{4,3,2,1,0:T(2,128)S(1)}, u32[]{:S(2)}, u32[]{:S(2)}) collective-permute-start(f32[34,1,2,2,128]{4,3,2,1,0:T(2,128)S(1)} %pad_maximum_fusion.6), channel_id=1, source_target_pairs={{32,0},{64,32},{96,64},{128,96},{160,128},{192,160},{224,192},{256... | collective-permute-start | bytes 208904 | tf_op jit(solution)/shard_map/ppermute | solution.py:426
  12.4 25.5 %collective-permute-start.2 = (f32[34,3,1,2,128]{4,3,2,1,0:T(2,128)S(1)}, f32[34,3,1,2,128]{4,3,2,1,0:T(2,128)S(1)}, u32[]{:S(2)}, u32[]{:S(2)}) collective-permute-start(f32[34,3,1,2,128]{4,3,2,1,0:T(2,128)S(1)} %get-tuple-element.28), channel_id=1, source_target_pairs={{0,8},{8,16},{16,24},{24,0},{1,9},{9,17},{17,25},{25,1},{2,10},{10... | collective-permute-start | bytes 313352 | tf_op jit(solution)/shard_map/ppermute | solution.py:424
  14.4 23.6 %collective-permute-start.3 = (f32[34,3,1,2,128]{4,3,2,1,0:T(2,128)S(1)}, f32[34,3,1,2,128]{4,3,2,1,0:T(2,128)S(1)}, u32[]{:S(2)}, u32[]{:S(2)}) collective-permute-start(f32[34,3,1,2,128]{4,3,2,1,0:T(2,128)S(1)} %get-tuple-element.29), channel_id=1, source_target_pairs={{8,0},{16,8},{24,16},{0,24},{9,1},{17,9},{25,17},{1,25},{10,2},{18... | collective-permute-start | bytes 313352 | tf_op jit(solution)/shard_map/ppermute | solution.py:426
  39.1 16.3 %collective-permute-start.4 = (f32[34,3,4,1,128]{4,3,2,1,0:T(1,128)S(1)}, f32[34,3,4,1,128]{4,3,2,1,0:T(1,128)S(1)}, u32[]{:S(2)}, u32[]{:S(2)}) collective-permute-start(f32[34,3,4,1,128]{4,3,2,1,0:T(1,128)S(1)} %get-tuple-element.26), channel_id=1, source_target_pairs={{0,1},{1,2},{2,3},{3,4},{4,5},{5,6},{6,7},{7,0},{8,9},{9,10},{10,1... | collective-permute-start | bytes 626696 | tf_op jit(solution)/shard_map/ppermute | solution.py:424
  41.4 14.0 %collective-permute-start.5 = (f32[34,3,4,1,128]{4,3,2,1,0:T(1,128)S(1)}, f32[34,3,4,1,128]{4,3,2,1,0:T(1,128)S(1)}, u32[]{:S(2)}, u32[]{:S(2)}) collective-permute-start(f32[34,3,4,1,128]{4,3,2,1,0:T(1,128)S(1)} %get-tuple-element.27), channel_id=1, source_target_pairs={{1,0},{2,1},{3,2},{4,3},{5,4},{6,5},{7,6},{0,7},{9,8},{10,9},{11,1... | collective-permute-start | bytes 626696 | tf_op jit(solution)/shard_map/ppermute | solution.py:426
  45.6 16.7 %all-to-all-start.1 = ((f32[16,1,128]{2,1,0:T(1,128)}), f32[16,1,128]{2,1,0:T(1,128)S(1)}, u32[]{:S(2)}, u32[]{:S(2)}) async-start(f32[16,1,128]{2,1,0:T(1,128)} %broadcast_in_dim.7), calls=%async_computation.1 | async-start | bytes 16384 | tf_op jit(solution)/shard_map/all_to_all | solution.py:437
  62.4 0.7 copy-start
  63.0 0.7 copy-start.1
  63.8 0.7 copy-start.3
  81.3 3.1 %collective-permute-start.7 = (f32[6,1,2,2,128]{4,3,2,1,0:T(2,128)S(1)}, f32[6,1,2,2,128]{4,3,2,1,0:T(2,128)S(1)}, u32[]{:S(2)}, u32[]{:S(2)}) collective-permute-start(f32[6,1,2,2,128]{4,3,2,1,0:T(2,128)S(1)} %bitcast.26), channel_id=1, source_target_pairs={{32,0},{64,32},{96,64},{128,96},{160,128},{192,160},{224,192},{256... | collective-permute-start | bytes 36872 | tf_op jit(solution)/shard_map/ppermute | solution.py:426
  82.0 2.5 %collective-permute-start.6 = (f32[6,1,2,2,128]{4,3,2,1,0:T(2,128)S(1)}, f32[6,1,2,2,128]{4,3,2,1,0:T(2,128)S(1)}, u32[]{:S(2)}, u32[]{:S(2)}) collective-permute-start(f32[6,1,2,2,128]{4,3,2,1,0:T(2,128)S(1)} %bitcast.27), channel_id=1, source_target_pairs={{0,32},{32,64},{64,96},{96,128},{128,160},{160,192},{192,224},{224... | collective-permute-start | bytes 36872 | tf_op jit(solution)/shard_map/ppermute | solution.py:424
  84.5 6.5 %collective-permute-start.8 = (f32[6,3,1,2,128]{4,3,2,1,0:T(2,128)S(1)}, f32[6,3,1,2,128]{4,3,2,1,0:T(2,128)S(1)}, u32[]{:S(2)}, u32[]{:S(2)}) collective-permute-start(f32[6,3,1,2,128]{4,3,2,1,0:T(2,128)S(1)} %get-tuple-element.32), channel_id=1, source_target_pairs={{0,8},{8,16},{16,24},{24,0},{1,9},{9,17},{17,25},{25,1},{2,10},{10... | collective-permute-start | bytes 55304 | tf_op jit(solution)/shard_map/ppermute | solution.py:424
  86.8 5.1 %collective-permute-start.9 = (f32[6,3,1,2,128]{4,3,2,1,0:T(2,128)S(1)}, f32[6,3,1,2,128]{4,3,2,1,0:T(2,128)S(1)}, u32[]{:S(2)}, u32[]{:S(2)}) collective-permute-start(f32[6,3,1,2,128]{4,3,2,1,0:T(2,128)S(1)} %get-tuple-element.33), channel_id=1, source_target_pairs={{8,0},{16,8},{24,16},{0,24},{9,1},{17,9},{25,17},{1,25},{10,2},{18... | collective-permute-start | bytes 55304 | tf_op jit(solution)/shard_map/ppermute | solution.py:426
  92.0 6.5 %collective-permute-start.10 = (f32[6,3,4,1,128]{4,3,2,1,0:T(1,128)S(1)}, f32[6,3,4,1,128]{4,3,2,1,0:T(1,128)S(1)}, u32[]{:S(2)}, u32[]{:S(2)}) collective-permute-start(f32[6,3,4,1,128]{4,3,2,1,0:T(1,128)S(1)} %get-tuple-element.30), channel_id=1, source_target_pairs={{0,1},{1,2},{2,3},{3,4},{4,5},{5,6},{6,7},{7,0},{8,9},{9,10},{10,1... | collective-permute-start | bytes 110600 | tf_op jit(solution)/shard_map/ppermute | solution.py:424
  93.9 5.6 %collective-permute-start.11 = (f32[6,3,4,1,128]{4,3,2,1,0:T(1,128)S(1)}, f32[6,3,4,1,128]{4,3,2,1,0:T(1,128)S(1)}, u32[]{:S(2)}, u32[]{:S(2)}) collective-permute-start(f32[6,3,4,1,128]{4,3,2,1,0:T(1,128)S(1)} %get-tuple-element.31), channel_id=1, source_target_pairs={{1,0},{2,1},{3,2},{4,3},{5,4},{6,5},{7,6},{0,7},{9,8},{10,9},{11,1... | collective-permute-start | bytes 110600 | tf_op jit(solution)/shard_map/ppermute | solution.py:426
  99.6 0.7 copy-start.2

commit v3 on v2

--- a/solution.py
+++ b/solution.py
@@ -1,12 +1,10 @@
-import functools
-
 import jax
 import jax.numpy as jnp
 from jax import lax
 from jax.experimental import pallas as pl
 from jax.experimental.pallas import tpu as pltpu
 
-ALL = ("gx", "gy", "gz")
+
 CELL_EDGE = 10.0
 SOFTENING = 0.3
 THOLE_DAMP = 0.39
@@ -21,7 +19,7 @@
 TERMS = 48
 A_ROWS = 96
 B_ROWS = 24
-BATCH = 8
+BATCH = 13
 PAIRS = OWN + OWN * (OFFSETS - 1)
 LIST = 128
 COUNT_AT = LIST - 1
@@ -173,6 +171,32 @@
     return part_a, part_b
 
 
+def apply_pairs(list_ref, pair_ref, a_ref, b_ref, sum_a, sum_b):
+    def pair(slot, n):
+        return product(
+            n,
+            pair_ref[slot, 0 : 2 * SLOTS, :],
+            pair_ref[slot, 2 * SLOTS : 4 * SLOTS, :],
+            a_ref,
+            b_ref,
+        )
+
+    for slot in range(OWN):
+        sum_a[slot], sum_b[slot] = pair(slot, OWN_TILES[slot])
+
+    def batch(b, carry):
+        for u in range(BATCH):
+            slot = OWN + b * BATCH + u
+            entry = list_ref[slot]
+            t = entry % OWN
+            part_a, part_b = pair(slot, entry // OWN)
+            sum_a[t] += part_a
+            sum_b[t] += part_b
+        return carry
+
+    lax.fori_loop(0, (list_ref[COUNT_AT] - OWN + BATCH - 1) // BATCH, batch, 0)
+
+
 def field_of(geo, sum_a, sum_b):
     r = positions(geo)
     scale_a, scale_b = factors(geo)
@@ -294,29 +318,26 @@
     prepare_moments(geo, moment, a_ref, b_ref)
     count = list_pairs(mask_ref, list_ref)
 
-    def pair(slot, n, t, keep):
+    def build(slot, n, t, keep):
         radial, direct = pair_functions(n, t, q_ref, p_ref, keep)
         pair_ref[slot, 0 : 2 * SLOTS, :] = radial
         pair_ref[slot, 2 * SLOTS : 4 * SLOTS, :] = direct
-        return product(n, radial, direct, a_ref, b_ref)
 
     keep = lax.broadcasted_iota(jnp.int32, (SLOTS, SLOTS), 0) != lax.broadcasted_iota(
         jnp.int32, (SLOTS, SLOTS), 1
     )
     for slot in range(OWN):
-        sum_a[slot], sum_b[slot] = pair(slot, OWN_TILES[slot], slot, keep)
+        build(slot, OWN_TILES[slot], slot, keep)
 
     def batch(b, carry):
         for u in range(BATCH):
             slot = OWN + b * BATCH + u
             entry = list_ref[slot]
-            t = entry % OWN
-            part_a, part_b = pair(slot, entry // OWN, t, None)
-            sum_a[t] += part_a
-            sum_b[t] += part_b
+            build(slot, entry // OWN, entry % OWN, None)
         return carry
 
     lax.fori_loop(0, (count - OWN + BATCH - 1) // BATCH, batch, 0)
+    apply_pairs(list_ref, pair_ref, a_ref, b_ref, sum_a, sum_b)
     fields = field_of(geo, sum_a, sum_b)
     scaled = RELAXATION * occupancy_ref[...].astype(jnp.float32) * own_part(geo[3])
     for c in range(6):
@@ -333,29 +354,7 @@
     moment = [dipole_ref[c] for c in range(6)]
     prepare_moments(geo, moment, a_ref, b_ref)
 
-    def pair(slot, n):
-        return product(
-            n,
-            pair_ref[slot, 0 : 2 * SLOTS, :],
-            pair_ref[slot, 2 * SLOTS : 4 * SLOTS, :],
-            a_ref,
-            b_ref,
-        )
-
-    for slot in range(OWN):
-        sum_a[slot], sum_b[slot] = pair(slot, OWN_TILES[slot])
-
-    def batch(b, carry):
-        for u in range(BATCH):
-            slot = OWN + b * BATCH + u
-            entry = list_ref[slot]
-            t = entry % OWN
-            part_a, part_b = pair(slot, entry // OWN)
-            sum_a[t] += part_a
-            sum_b[t] += part_b
-        return carry
-
-    lax.fori_loop(0, (list_ref[COUNT_AT] - OWN + BATCH - 1) // BATCH, batch, 0)
+    apply_pairs(list_ref, pair_ref, a_ref, b_ref, sum_a, sum_b)
     fields = field_of(geo, sum_a, sum_b)
     scaled = RELAXATION * occupancy_ref[...].astype(jnp.float32) * own_part(geo[3])
     moved = jnp.zeros((OWN, SLOTS), jnp.float32)
@@ -419,14 +418,9 @@
         count = lax.axis_size(axis)
         head = lax.slice_in_dim(cells, 0, 1, axis=dim)
         tail = lax.slice_in_dim(cells, cells.shape[dim] - 1, cells.shape[dim], axis=dim)
-        cells = jnp.concatenate(
-            [
-                lax.ppermute(tail, axis, [(i, (i + 1) % count) for i in range(count)]),
-                cells,
-                lax.ppermute(head, axis, [((i + 1) % count, i) for i in range(count)]),
-            ],
-            axis=dim,
-        )
+        before = lax.ppermute(tail, axis, [(i, (i + 1) % count) for i in range(count)])
+        after = lax.ppermute(head, axis, [((i + 1) % count, i) for i in range(count)])
+        cells = jnp.concatenate([before, cells, after], axis=dim)
     return cells
 
 
@@ -437,7 +431,7 @@
     return lax.all_to_all(parts, axes, 0, 0)
 
 
-def on_device(fractions, polarizability, occupancy, pair_mask, perm_field, history):
+def device_step(fractions, polarizability, occupancy, pair_mask, perm_field, history):
     plane = lax.axis_size("gy") * lax.axis_size("gz")
     line = lax.axis_size("gx")
     history = history.reshape(6, 6, OWN, SLOTS)
@@ -478,7 +472,7 @@
     tiles = P("gx", "gy", "gz", None)
     sets = P(None, "gx", "gy", "gz", None)
     return jax.shard_map(
-        on_device,
+        device_step,
         mesh=mesh,
         in_specs=(
             sets,

time: 139 us -> 131 us (0.942)
  Pallas kernels: 22.9 us -> 14.8 us
    pallas_call x1, Pallas kernels: 16.9 us -> 9.17 us  [first_field(): pl.pallas_call(first_kernel, name='first_field', in_specs=[smem_spec()] +...]
  transfers between devices with their start and end apart: 13 -> 13, of which waited for: 6 -> 6; matrix products, arithmetic and copies ran while one was open for 0% -> 1% of each run, Pallas kernels for 0% -> 0%
where the time goes in v3:
time: 131 us; the launch traced here: 130 us
  blocking collectives  52.1 us (40%)
  starting transfers between devices  44.4 us (34%)
  Pallas kernels  14.8 us (11%)
  waiting for transfers between devices  10.5 us (8%)
  local copies, waits for them, and re-layouts  4.74 us (4%)
  other arithmetic  3.02 us (2%)
    all_to_all x3, blocking collectives, exchange(): return lax.all_to_all(parts, axes, 0, 0)  52.1 us
    ppermute x6, starting transfers between devices, with_halo(): lax.ppermute(head, axis, [((i + 1) % count, i) for i in range(count)])  22.5 us
    ppermute x6, starting transfers between devices, with_halo(): lax.ppermute(tail, axis, [(i, (i + 1) % count) for i in range(count)])  12.1 us
    all_to_all x1, starting transfers between devices, exchange(): return lax.all_to_all(parts, axes, 0, 0)  9.77 us
    pallas_call x1, Pallas kernels, first_field(): pl.pallas_call(first_kernel, name='first_field', in_specs=[smem_spec()] +...  9.17 us
    all_to_all x1, waiting for transfers between devices, exchange(): return lax.all_to_all(parts, axes, 0, 0)  6.37 us
    pallas_call x1, Pallas kernels, second_field(): pl.pallas_call(second_kernel, name='second_field', in_specs=[smem_spec()]...  4.03 us
    ppermute x6, waiting for transfers between devices, with_halo(): lax.ppermute(head, axis, [((i + 1) % count, i) for i in range(count)])  3.4 us
  transfers between devices with their start and end apart: 13, of which 6 were waited for; matrix products, arithmetic and copies ran while one was open for 1% of the time, Pallas kernels for 0%

profile of v3, /device:TPU:1, one launch (start us, length us, event | category | flops | bytes accessed | tf_op | source)
XLA Modules:
  0.0 130.4 jit_solution(12831073829679779636)
XLA Ops:
  0.6 0.7 convert_bitcast_fusion
  1.3 0.8 slice.46
  2.1 1.6 %local_gram.1 = f32[32,1,128]{2,1,0:T(1,128)} custom-call(f32[6,6,4,128]{3,2,1,0:T(4,128)} %bitcast.37, s32[4,128]{1,0:T(4,128)} %bitcast.31), custom_call_target="tpu_custom_call" | custom-call | tf_op jit(solution)/shard_map/local_gram/pallas_call | solution.py:281
  3.8 0.7 pad_maximum_fusion.6
  4.6 2.7 %collective-permute-start = (f32[34,1,2,2,128]{4,3,2,1,0:T(2,128)S(1)}, f32[34,1,2,2,128]{4,3,2,1,0:T(2,128)S(1)}, u32[]{:S(2)}, u32[]{:S(2)}) collective-permute-start(f32[34,1,2,2,128]{4,3,2,1,0:T(2,128)S(1)} %pad_maximum_fusion.6), channel_id=1, source_target_pairs={{0,32},{32,64},{64,96},{96,128},{128,160},{160,192},{192,224},{224... | collective-permute-start | bytes 208904 | tf_op jit(solution)/shard_map/ppermute | solution.py:421
  7.2 4.2 %collective-permute-start.1 = (f32[34,1,2,2,128]{4,3,2,1,0:T(2,128)S(1)}, f32[34,1,2,2,128]{4,3,2,1,0:T(2,128)S(1)}, u32[]{:S(2)}, u32[]{:S(2)}) collective-permute-start(f32[34,1,2,2,128]{4,3,2,1,0:T(2,128)S(1)} %pad_maximum_fusion.6), channel_id=1, source_target_pairs={{32,0},{64,32},{96,64},{128,96},{160,128},{192,160},{224,192},{256... | collective-permute-start | bytes 208904 | tf_op jit(solution)/shard_map/ppermute | solution.py:422
  11.4 0.7 collective-permute-done
  12.2 0.1 collective-permute-done.1
  12.4 0.1 fusion.2
  12.4 1.9 %collective-permute-start.2 = (f32[34,3,1,2,128]{4,3,2,1,0:T(2,128)S(1)}, f32[34,3,1,2,128]{4,3,2,1,0:T(2,128)S(1)}, u32[]{:S(2)}, u32[]{:S(2)}) collective-permute-start(f32[34,3,1,2,128]{4,3,2,1,0:T(2,128)S(1)} %get-tuple-element.28), channel_id=1, source_target_pairs={{0,8},{8,16},{16,24},{24,0},{1,9},{9,17},{17,25},{25,1},{2,10},{10... | collective-permute-start | bytes 313352 | tf_op jit(solution)/shard_map/ppermute | solution.py:421
  14.4 4.6 %collective-permute-start.3 = (f32[34,3,1,2,128]{4,3,2,1,0:T(2,128)S(1)}, f32[34,3,1,2,128]{4,3,2,1,0:T(2,128)S(1)}, u32[]{:S(2)}, u32[]{:S(2)}) collective-permute-start(f32[34,3,1,2,128]{4,3,2,1,0:T(2,128)S(1)} %get-tuple-element.29), channel_id=1, source_target_pairs={{8,0},{16,8},{24,16},{0,24},{9,1},{17,9},{25,17},{1,25},{10,2},{18... | collective-permute-start | bytes 313352 | tf_op jit(solution)/shard_map/ppermute | solution.py:422
  19.0 19.0 %all_to_all.20 = f32[32,1,128]{2,1,0:T(1,128)S(1)} all-to-all(f32[32,1,128]{2,1,0:T(1,128)} %local_gram.1), channel_id=1, replica_groups=mesh['gx'=16,'gy'=4,'gz'=8] {'gy','gz'}, dimensions={0} | all-to-all | bytes 32768 | tf_op jit(solution)/shard_map/all_to_all | solution.py:431
  37.9 0.1 reduce_sum.27
  38.0 0.0 collective-permute-done.2
  38.0 0.0 collective-permute-done.3
  38.0 0.2 pad_maximum_fusion.2
  38.2 0.6 broadcast_in_dim.7
  38.8 0.3 fusion.1
  39.1 2.2 %collective-permute-start.4 = (f32[34,3,4,1,128]{4,3,2,1,0:T(1,128)S(1)}, f32[34,3,4,1,128]{4,3,2,1,0:T(1,128)S(1)}, u32[]{:S(2)}, u32[]{:S(2)}) collective-permute-start(f32[34,3,4,1,128]{4,3,2,1,0:T(1,128)S(1)} %get-tuple-element.26), channel_id=1, source_target_pairs={{0,1},{1,2},{2,3},{3,4},{4,5},{5,6},{6,7},{7,0},{8,9},{9,10},{10,1... | collective-permute-start | bytes 626696 | tf_op jit(solution)/shard_map/ppermute | solution.py:421
  41.4 4.3 %collective-permute-start.5 = (f32[34,3,4,1,128]{4,3,2,1,0:T(1,128)S(1)}, f32[34,3,4,1,128]{4,3,2,1,0:T(1,128)S(1)}, u32[]{:S(2)}, u32[]{:S(2)}) collective-permute-start(f32[34,3,4,1,128]{4,3,2,1,0:T(1,128)S(1)} %get-tuple-element.27), channel_id=1, source_target_pairs={{1,0},{2,1},{3,2},{4,3},{5,4},{6,5},{7,6},{0,7},{9,8},{10,9},{11,1... | collective-permute-start | bytes 626696 | tf_op jit(solution)/shard_map/ppermute | solution.py:422
  45.6 9.8 %all-to-all-start.1 = ((f32[16,1,128]{2,1,0:T(1,128)}), f32[16,1,128]{2,1,0:T(1,128)S(1)}, u32[]{:S(2)}, u32[]{:S(2)}) async-start(f32[16,1,128]{2,1,0:T(1,128)} %broadcast_in_dim.7), calls=%async_computation.1 | async-start | bytes 16384 | tf_op jit(solution)/shard_map/all_to_all | solution.py:431
  55.4 0.0 collective-permute-done.4
  55.4 0.0 collective-permute-done.5
  55.4 0.5 pad_maximum_fusion
  55.9 0.1 pad_maximum_fusion.4
  56.0 6.4 %all-to-all-done.1.gram_ref = f32[16,1,128]{2,1,0:T(1,128)S(1)} async-done(((f32[16,1,128]{2,1,0:T(1,128)}), f32[16,1,128]{2,1,0:T(1,128)S(1)}, u32[]{:S(2)}, u32[]{:S(2)}) %all-to-all-start.1) | async-done | bytes 8224 | tf_op jit(solution)/shard_map/all_to_all | solution.py:431
  62.4 0.0 copy-start
  62.4 0.7 copy-done
  63.0 0.0 copy-start.1
  63.0 0.7 copy-done.1
  63.8 0.0 copy-start.3
  63.8 0.7 copy-done.3
  64.4 9.2 %first_field.1 = (f32[6,4,128]{2,1,0:T(4,128)S(1)}, s32[128]{0:T(128)S(1)}, bf16[108,512,128]{2,1,0:T(8,128)(2,1)S(1)}) custom-call(s32[4,27]{1,0:T(4,128)S(1)} %bitcast.36, f32[16,1,128]{2,1,0:T(1,128)S(1)} %all-to-all-done.1.gram_ref, f32[4,48,128]{2,1,0:T(8,128)S(1)} %bitcast.24, f32[30,48,128]{2,1,0:T(8,128)S(1)} %bitcast.22, s32[4,128]{1,0:T(4,128)S(1)} %bitcast.32, ...), custom_call_target="tpu_custom_call" | custom-call | flops 2000000000 | bytes 1000000 | tf_op jit(solution)/shard_map/first_field/pallas_call | solution.py:376
  73.6 0.7 collective-permute-start.7
  74.3 1.1 collective-permute-start.6
  75.4 1.4 %collective-permute-done.7 = f32[6,1,2,2,128]{4,3,2,1,0:T(2,128)S(1)} collective-permute-done((f32[6,1,2,2,128]{4,3,2,1,0:T(2,128)S(1)}, f32[6,1,2,2,128]{4,3,2,1,0:T(2,128)S(1)}, u32[]{:S(2)}, u32[]{:S(2)}) %collective-permute-start.7) | collective-permute-done | bytes 12320 | tf_op jit(solution)/shard_map/ppermute | solution.py:422
  76.7 0.0 collective-permute-done.6
  76.8 2.2 %collective-permute-start.8 = (f32[6,3,1,2,128]{4,3,2,1,0:T(2,128)S(1)}, f32[6,3,1,2,128]{4,3,2,1,0:T(2,128)S(1)}, u32[]{:S(2)}, u32[]{:S(2)}) collective-permute-start(f32[6,3,1,2,128]{4,3,2,1,0:T(2,128)S(1)} %get-tuple-element.32), channel_id=1, source_target_pairs={{0,8},{8,16},{16,24},{24,0},{1,9},{9,17},{17,25},{25,1},{2,10},{10... | collective-permute-start | bytes 55304 | tf_op jit(solution)/shard_map/ppermute | solution.py:421
  79.0 4.3 %collective-permute-start.9 = (f32[6,3,1,2,128]{4,3,2,1,0:T(2,128)S(1)}, f32[6,3,1,2,128]{4,3,2,1,0:T(2,128)S(1)}, u32[]{:S(2)}, u32[]{:S(2)}) collective-permute-start(f32[6,3,1,2,128]{4,3,2,1,0:T(2,128)S(1)} %get-tuple-element.33), channel_id=1, source_target_pairs={{8,0},{16,8},{24,16},{0,24},{9,1},{17,9},{25,17},{1,25},{10,2},{18... | collective-permute-start | bytes 55304 | tf_op jit(solution)/shard_map/ppermute | solution.py:422
  83.3 0.0 collective-permute-done.8
  83.3 0.9 collective-permute-done.9
  84.2 0.1 fusion.3
  84.3 1.9 %collective-permute-start.10 = (f32[6,3,4,1,128]{4,3,2,1,0:T(1,128)S(1)}, f32[6,3,4,1,128]{4,3,2,1,0:T(1,128)S(1)}, u32[]{:S(2)}, u32[]{:S(2)}) collective-permute-start(f32[6,3,4,1,128]{4,3,2,1,0:T(1,128)S(1)} %get-tuple-element.30), channel_id=1, source_target_pairs={{0,1},{1,2},{2,3},{3,4},{4,5},{5,6},{6,7},{7,0},{8,9},{9,10},{10,1... | collective-permute-start | bytes 110600 | tf_op jit(solution)/shard_map/ppermute | solution.py:421
  86.2 4.6 %collective-permute-start.11 = (f32[6,3,4,1,128]{4,3,2,1,0:T(1,128)S(1)}, f32[6,3,4,1,128]{4,3,2,1,0:T(1,128)S(1)}, u32[]{:S(2)}, u32[]{:S(2)}) collective-permute-start(f32[6,3,4,1,128]{4,3,2,1,0:T(1,128)S(1)} %get-tuple-element.31), channel_id=1, source_target_pairs={{1,0},{2,1},{3,2},{4,3},{5,4},{6,5},{7,6},{0,7},{9,8},{10,9},{11,1... | collective-permute-start | bytes 110600 | tf_op jit(solution)/shard_map/ppermute | solution.py:422
  90.8 0.0 collective-permute-done.10
  90.8 1.0 collective-permute-done.11
  91.8 0.1 pad_maximum_fusion.3
  91.9 0.0 copy-start.2
  91.9 0.7 copy-done.2
  92.6 4.0 %second_field.1 = (f32[6,4,128]{2,1,0:T(4,128)}, f32[32,2,128]{2,1,0:T(2,128)S(1)}) custom-call(s32[128]{0:T(128)S(1)} %get-tuple-element.15.list_ref, f32[4,48,128]{2,1,0:T(8,128)S(1)} %bitcast.25, f32[6,48,128]{2,1,0:T(8,128)S(1)} %bitcast.23, s32[4,128]{1,0:T(4,128)S(1)} %bitcast.33, f32[6,4,128]{2,1,0:T(4,128)S(1)} %bitcast.35, ...), custom_call_target="tpu_custom_call" | custom-call | flops 1000000000 | bytes 1000000 | tf_op jit(solution)/shard_map/second_field/pallas_call | solution.py:399
  96.7 15.8 %all_to_all.21 = f32[32,2,128]{2,1,0:T(2,128)S(1)} all-to-all(f32[32,2,128]{2,1,0:T(2,128)S(1)} %get-tuple-element.19), channel_id=1, replica_groups=mesh['gx'=16,'gy'=4,'gz'=8] {'gy','gz'}, dimensions={0} | all-to-all | bytes 65536 | tf_op jit(solution)/shard_map/all_to_all | solution.py:431
  112.5 17.3 %all_to_all.22 = f32[16,2,128]{2,1,0:T(2,128)S(1)} all-to-all(f32[16,2,128]{2,1,0:T(2,128)S(1)} %broadcast_in_dim.8), channel_id=1, replica_groups=mesh['gx'=16,'gy'=4,'gz'=8] {'gx'}, dimensions={0} | all-to-all | bytes 32768 | tf_op jit(solution)/shard_map/all_to_all | solution.py:431
  129.9 0.5 fusion
  (10 shorter events, 0.2 us)
Async XLA Ops:
  4.6 7.6 %collective-permute-start = (f32[34,1,2,2,128]{4,3,2,1,0:T(2,128)S(1)}, f32[34,1,2,2,128]{4,3,2,1,0:T(2,128)S(1)}, u32[]{:S(2)}, u32[]{:S(2)}) collective-permute-start(f32[34,1,2,2,128]{4,3,2,1,0:T(2,128)S(1)} %pad_maximum_fusion.6), channel_id=1, source_target_pairs={{0,32},{32,64},{64,96},{96,128},{128,160},{160,192},{192,224},{224... | collective-permute-start | bytes 208904 | tf_op jit(solution)/shard_map/ppermute | solution.py:421
  7.2 5.1 %collective-permute-start.1 = (f32[34,1,2,2,128]{4,3,2,1,0:T(2,128)S(1)}, f32[34,1,2,2,128]{4,3,2,1,0:T(2,128)S(1)}, u32[]{:S(2)}, u32[]{:S(2)}) collective-permute-start(f32[34,1,2,2,128]{4,3,2,1,0:T(2,128)S(1)} %pad_maximum_fusion.6), channel_id=1, source_target_pairs={{32,0},{64,32},{96,64},{128,96},{160,128},{192,160},{224,192},{256... | collective-permute-start | bytes 208904 | tf_op jit(solution)/shard_map/ppermute | solution.py:422
  12.4 25.5 %collective-permute-start.2 = (f32[34,3,1,2,128]{4,3,2,1,0:T(2,128)S(1)}, f32[34,3,1,2,128]{4,3,2,1,0:T(2,128)S(1)}, u32[]{:S(2)}, u32[]{:S(2)}) collective-permute-start(f32[34,3,1,2,128]{4,3,2,1,0:T(2,128)S(1)} %get-tuple-element.28), channel_id=1, source_target_pairs={{0,8},{8,16},{16,24},{24,0},{1,9},{9,17},{17,25},{25,1},{2,10},{10... | collective-permute-start | bytes 313352 | tf_op jit(solution)/shard_map/ppermute | solution.py:421
  14.4 23.6 %collective-permute-start.3 = (f32[34,3,1,2,128]{4,3,2,1,0:T(2,128)S(1)}, f32[34,3,1,2,128]{4,3,2,1,0:T(2,128)S(1)}, u32[]{:S(2)}, u32[]{:S(2)}) collective-permute-start(f32[34,3,1,2,128]{4,3,2,1,0:T(2,128)S(1)} %get-tuple-element.29), channel_id=1, source_target_pairs={{8,0},{16,8},{24,16},{0,24},{9,1},{17,9},{25,17},{1,25},{10,2},{18... | collective-permute-start | bytes 313352 | tf_op jit(solution)/shard_map/ppermute | solution.py:422
  39.1 16.3 %collective-permute-start.4 = (f32[34,3,4,1,128]{4,3,2,1,0:T(1,128)S(1)}, f32[34,3,4,1,128]{4,3,2,1,0:T(1,128)S(1)}, u32[]{:S(2)}, u32[]{:S(2)}) collective-permute-start(f32[34,3,4,1,128]{4,3,2,1,0:T(1,128)S(1)} %get-tuple-element.26), channel_id=1, source_target_pairs={{0,1},{1,2},{2,3},{3,4},{4,5},{5,6},{6,7},{7,0},{8,9},{9,10},{10,1... | collective-permute-start | bytes 626696 | tf_op jit(solution)/shard_map/ppermute | solution.py:421
  41.4 14.0 %collective-permute-start.5 = (f32[34,3,4,1,128]{4,3,2,1,0:T(1,128)S(1)}, f32[34,3,4,1,128]{4,3,2,1,0:T(1,128)S(1)}, u32[]{:S(2)}, u32[]{:S(2)}) collective-permute-start(f32[34,3,4,1,128]{4,3,2,1,0:T(1,128)S(1)} %get-tuple-element.27), channel_id=1, source_target_pairs={{1,0},{2,1},{3,2},{4,3},{5,4},{6,5},{7,6},{0,7},{9,8},{10,9},{11,1... | collective-permute-start | bytes 626696 | tf_op jit(solution)/shard_map/ppermute | solution.py:422
  45.6 16.7 %all-to-all-start.1 = ((f32[16,1,128]{2,1,0:T(1,128)}), f32[16,1,128]{2,1,0:T(1,128)S(1)}, u32[]{:S(2)}, u32[]{:S(2)}) async-start(f32[16,1,128]{2,1,0:T(1,128)} %broadcast_in_dim.7), calls=%async_computation.1 | async-start | bytes 16384 | tf_op jit(solution)/shard_map/all_to_all | solution.py:431
  62.4 0.7 copy-start
  63.0 0.7 copy-start.1
  63.8 0.7 copy-start.3
  73.6 3.1 %collective-permute-start.7 = (f32[6,1,2,2,128]{4,3,2,1,0:T(2,128)S(1)}, f32[6,1,2,2,128]{4,3,2,1,0:T(2,128)S(1)}, u32[]{:S(2)}, u32[]{:S(2)}) collective-permute-start(f32[6,1,2,2,128]{4,3,2,1,0:T(2,128)S(1)} %bitcast.26), channel_id=1, source_target_pairs={{32,0},{64,32},{96,64},{128,96},{160,128},{192,160},{224,192},{256... | collective-permute-start | bytes 36872 | tf_op jit(solution)/shard_map/ppermute | solution.py:422
  74.3 2.5 %collective-permute-start.6 = (f32[6,1,2,2,128]{4,3,2,1,0:T(2,128)S(1)}, f32[6,1,2,2,128]{4,3,2,1,0:T(2,128)S(1)}, u32[]{:S(2)}, u32[]{:S(2)}) collective-permute-start(f32[6,1,2,2,128]{4,3,2,1,0:T(2,128)S(1)} %bitcast.27), channel_id=1, source_target_pairs={{0,32},{32,64},{64,96},{96,128},{128,160},{160,192},{192,224},{224... | collective-permute-start | bytes 36872 | tf_op jit(solution)/shard_map/ppermute | solution.py:421
  76.8 6.5 %collective-permute-start.8 = (f32[6,3,1,2,128]{4,3,2,1,0:T(2,128)S(1)}, f32[6,3,1,2,128]{4,3,2,1,0:T(2,128)S(1)}, u32[]{:S(2)}, u32[]{:S(2)}) collective-permute-start(f32[6,3,1,2,128]{4,3,2,1,0:T(2,128)S(1)} %get-tuple-element.32), channel_id=1, source_target_pairs={{0,8},{8,16},{16,24},{24,0},{1,9},{9,17},{17,25},{25,1},{2,10},{10... | collective-permute-start | bytes 55304 | tf_op jit(solution)/shard_map/ppermute | solution.py:421
  79.0 5.1 %collective-permute-start.9 = (f32[6,3,1,2,128]{4,3,2,1,0:T(2,128)S(1)}, f32[6,3,1,2,128]{4,3,2,1,0:T(2,128)S(1)}, u32[]{:S(2)}, u32[]{:S(2)}) collective-permute-start(f32[6,3,1,2,128]{4,3,2,1,0:T(2,128)S(1)} %get-tuple-element.33), channel_id=1, source_target_pairs={{8,0},{16,8},{24,16},{0,24},{9,1},{17,9},{25,17},{1,25},{10,2},{18... | collective-permute-start | bytes 55304 | tf_op jit(solution)/shard_map/ppermute | solution.py:422
  84.3 6.5 %collective-permute-start.10 = (f32[6,3,4,1,128]{4,3,2,1,0:T(1,128)S(1)}, f32[6,3,4,1,128]{4,3,2,1,0:T(1,128)S(1)}, u32[]{:S(2)}, u32[]{:S(2)}) collective-permute-start(f32[6,3,4,1,128]{4,3,2,1,0:T(1,128)S(1)} %get-tuple-element.30), channel_id=1, source_target_pairs={{0,1},{1,2},{2,3},{3,4},{4,5},{5,6},{6,7},{7,0},{8,9},{9,10},{10,1... | collective-permute-start | bytes 110600 | tf_op jit(solution)/shard_map/ppermute | solution.py:421
  86.2 5.6 %collective-permute-start.11 = (f32[6,3,4,1,128]{4,3,2,1,0:T(1,128)S(1)}, f32[6,3,4,1,128]{4,3,2,1,0:T(1,128)S(1)}, u32[]{:S(2)}, u32[]{:S(2)}) collective-permute-start(f32[6,3,4,1,128]{4,3,2,1,0:T(1,128)S(1)} %get-tuple-element.31), channel_id=1, source_target_pairs={{1,0},{2,1},{3,2},{4,3},{5,4},{6,5},{7,6},{0,7},{9,8},{10,9},{11,1... | collective-permute-start | bytes 110600 | tf_op jit(solution)/shard_map/ppermute | solution.py:422
  91.9 0.7 copy-start.2

commit v4 on v3

--- a/solution.py
+++ b/solution.py
@@ -23,6 +23,8 @@
 PAIRS = OWN + OWN * (OFFSETS - 1)
 LIST = 128
 COUNT_AT = LIST - 1
+ROWS = 34
+PLANE = NY * NZ
 GRAM = tuple((a, b) for a in range(6) for b in range(a + 1))
 
 
@@ -253,11 +255,15 @@
     return result
 
 
-def gram_kernel(history_ref, occupancy_ref, out_ref):
+def prepare_kernel(fractions_ref, polar_ref, occupancy_ref, history_ref, stacked_ref, gram_ref):
     filled = occupancy_ref[...].astype(jnp.float32)
-    masked = [
-        [history_ref[h, c] * filled for c in range(6)] for h in range(6)
-    ]
+    masked = [[history_ref[h, c] * filled for c in range(6)] for h in range(6)]
+    for a in range(3):
+        stacked_ref[a] = fractions_ref[a]
+    stacked_ref[3] = polar_ref[...]
+    for h in range(1, 6):
+        for c in range(6):
+            stacked_ref[4 + 6 * (h - 1) + c] = masked[h][c]
     lane = lax.broadcasted_iota(jnp.int32, (1, SLOTS), 1)
     row = jnp.zeros((1, SLOTS), jnp.float32)
     for index, (a, b) in enumerate(GRAM):
@@ -266,7 +272,7 @@
             product = product + masked[a][c] * masked[b][c]
         total = jnp.sum(jnp.sum(product, axis=0, keepdims=True), axis=1, keepdims=True)
         row = jnp.where(lane == index, total, row)
-    out_ref[...] = jnp.broadcast_to(row[None], out_ref.shape)
+    gram_ref[...] = jnp.broadcast_to(row[None], gram_ref.shape)
 
 
 def vmem_spec():
@@ -277,14 +283,17 @@
     return pl.BlockSpec(memory_space=pltpu.SMEM)
 
 
-def local_gram(history, occupancy, copies):
+def prepare(fractions, polarizability, occupancy, history, copies):
     return pl.pallas_call(
-        gram_kernel,
-        name="local_gram",
-        in_specs=[vmem_spec(), vmem_spec()],
-        out_specs=vmem_spec(),
-        out_shape=jax.ShapeDtypeStruct((copies, 1, SLOTS), jnp.float32),
-    )(history, occupancy)
+        prepare_kernel,
+        name="prepare",
+        in_specs=[vmem_spec()] * 4,
+        out_specs=[vmem_spec(), vmem_spec()],
+        out_shape=[
+            jax.ShapeDtypeStruct((ROWS, OWN, SLOTS), jnp.float32),
+            jax.ShapeDtypeStruct((copies, 1, SLOTS), jnp.float32),
+        ],
+    )(fractions, polarizability, occupancy, history)
 
 
 def sum_parts(parts, copies):
@@ -300,11 +309,27 @@
 ]
 
 
+def whole(slabs, row):
+    return jnp.concatenate([slab[row] for slab in slabs], axis=0)
+
+
 def first_kernel(
-    mask_ref, gram_ref, geo_ref, later_ref, occupancy_ref, perm_ref,
-    out_ref, list_ref, pair_ref, q_ref, p_ref, a_ref, b_ref, sum_a, sum_b,
+    mask_hbm, occupancy_hbm, perm_hbm, gram_ref, before_ref, own_ref, after_ref,
+    out_ref, list_ref, geo_ref, scaled_ref, perm_ref, pair_ref,
+    mask_ref, occupancy_ref, q_ref, p_ref, a_ref, b_ref, sum_a, sum_b, mask_sem, own_sem, perm_sem,
 ):
-    geo = [geo_ref[a] for a in range(4)]
+    copies = [
+        pltpu.make_async_copy(mask_hbm, mask_ref, mask_sem),
+        pltpu.make_async_copy(occupancy_hbm, occupancy_ref, own_sem),
+        pltpu.make_async_copy(perm_hbm, perm_ref, perm_sem),
+    ]
+    for copy in copies:
+        copy.start()
+    slabs = (before_ref, own_ref, after_ref)
+    geo = [whole(slabs, a) for a in range(4)]
+    for a in range(4):
+        geo_ref[a] = geo[a]
+    later_ref = [whole(slabs, row) for row in range(4, ROWS)]
     total = jnp.sum(gram_ref[...], axis=0)
     gram = {ab: total[0:1, i : i + 1] for i, ab in enumerate(GRAM)}
     coeffs = solve(gram)
@@ -316,6 +341,8 @@
         moment.append(value)
     prepare_distances(geo, q_ref, p_ref)
     prepare_moments(geo, moment, a_ref, b_ref)
+    for copy in copies:
+        copy.wait()
     count = list_pairs(mask_ref, list_ref)
 
     def build(slot, n, t, keep):
@@ -340,6 +367,7 @@
     apply_pairs(list_ref, pair_ref, a_ref, b_ref, sum_a, sum_b)
     fields = field_of(geo, sum_a, sum_b)
     scaled = RELAXATION * occupancy_ref[...].astype(jnp.float32) * own_part(geo[3])
+    scaled_ref[...] = scaled
     for c in range(6):
         out_ref[c] = (1.0 - RELAXATION) * own_part(moment[c]) + scaled * (
             perm_ref[c] + fields[c]
@@ -347,16 +375,17 @@
 
 
 def second_kernel(
-    list_ref, geo_ref, dipole_ref, occupancy_ref, perm_ref, pair_ref,
+    list_ref, geo_ref, before_ref, own_ref, after_ref, scaled_ref, perm_ref, pair_ref,
     out_ref, size_ref, a_ref, b_ref, sum_a, sum_b,
 ):
     geo = [geo_ref[a] for a in range(4)]
-    moment = [dipole_ref[c] for c in range(6)]
+    slabs = (before_ref, own_ref, after_ref)
+    moment = [whole(slabs, c) for c in range(6)]
     prepare_moments(geo, moment, a_ref, b_ref)
 
     apply_pairs(list_ref, pair_ref, a_ref, b_ref, sum_a, sum_b)
     fields = field_of(geo, sum_a, sum_b)
-    scaled = RELAXATION * occupancy_ref[...].astype(jnp.float32) * own_part(geo[3])
+    scaled = scaled_ref[...]
     moved = jnp.zeros((OWN, SLOTS), jnp.float32)
     size = jnp.zeros((OWN, SLOTS), jnp.float32)
     for c in range(6):
@@ -372,34 +401,41 @@
         )
 
 
-def first_field(mask, gram, geo, later, occupancy, perm):
+def first_field(mask, occupancy, perm, gram, slabs):
+    whole_array = pl.BlockSpec(memory_space=pltpu.HBM)
     return pl.pallas_call(
         first_kernel,
         name="first_field",
-        in_specs=[smem_spec()] + [vmem_spec()] * 5,
-        out_specs=[vmem_spec(), smem_spec(), vmem_spec()],
+        in_specs=[whole_array] * 3 + [vmem_spec()] * 4,
+        out_specs=[vmem_spec(), smem_spec()] + [vmem_spec()] * 4,
         out_shape=[
             jax.ShapeDtypeStruct((6, OWN, SLOTS), jnp.float32),
             jax.ShapeDtypeStruct((LIST,), jnp.int32),
+            jax.ShapeDtypeStruct((4, TILES, SLOTS), jnp.float32),
+            jax.ShapeDtypeStruct((OWN, SLOTS), jnp.float32),
+            jax.ShapeDtypeStruct((6, OWN, SLOTS), jnp.float32),
             jax.ShapeDtypeStruct((PAIRS, 4 * SLOTS, SLOTS), jnp.bfloat16),
         ],
         scratch_shapes=[
+            pltpu.SMEM((OWN, OFFSETS), jnp.int32),
+            pltpu.VMEM((OWN, SLOTS), jnp.int32),
             pltpu.VMEM(((TILES + 1) * (TERMS + 1), SLOTS), jnp.float32),
             pltpu.VMEM((OWN, TERMS, SLOTS), jnp.float32),
         ]
-        + SCRATCH,
+        + SCRATCH
+        + [pltpu.SemaphoreType.DMA] * 3,
         compiler_params=pltpu.CompilerParams(vmem_limit_bytes=24 * 1024 * 1024),
         cost_estimate=pl.CostEstimate(
             flops=2_000_000_000, bytes_accessed=1_000_000, transcendentals=0
         ),
-    )(mask, gram, geo, later, occupancy, perm)
-
-
-def second_field(pair_list, geo, dipoles, occupancy, perm, pairs, copies):
+    )(mask, occupancy, perm, gram, *slabs)
+
+
+def second_field(pair_list, geo, slabs, scaled, perm, pairs, copies):
     return pl.pallas_call(
         second_kernel,
         name="second_field",
-        in_specs=[smem_spec()] + [vmem_spec()] * 5,
+        in_specs=[smem_spec()] + [vmem_spec()] * 7,
         out_specs=[vmem_spec(), vmem_spec()],
         out_shape=[
             jax.ShapeDtypeStruct((6, OWN, SLOTS), jnp.float32),
@@ -410,21 +446,29 @@
         cost_estimate=pl.CostEstimate(
             flops=1_000_000_000, bytes_accessed=1_000_000, transcendentals=0
         ),
-    )(pair_list, geo, dipoles, occupancy, perm, pairs)
-
-
-def with_halo(cells, sides):
-    for axis, dim in sides:
-        count = lax.axis_size(axis)
-        head = lax.slice_in_dim(cells, 0, 1, axis=dim)
-        tail = lax.slice_in_dim(cells, cells.shape[dim] - 1, cells.shape[dim], axis=dim)
-        before = lax.ppermute(tail, axis, [(i, (i + 1) % count) for i in range(count)])
-        after = lax.ppermute(head, axis, [((i + 1) % count, i) for i in range(count)])
-        cells = jnp.concatenate([before, cells, after], axis=dim)
-    return cells
-
-
-SIDES = (("gx", 1), ("gy", 2), ("gz", 3))
+    )(pair_list, geo, *slabs, scaled, perm, pairs)
+
+
+def both_ways(low, high, axis):
+    count = lax.axis_size(axis)
+    before = lax.ppermute(high, axis, [(i, (i + 1) % count) for i in range(count)])
+    after = lax.ppermute(low, axis, [((i + 1) % count, i) for i in range(count)])
+    return before, after
+
+
+def joined(cells, axis, dim):
+    size = cells.shape[dim]
+    low = lax.slice_in_dim(cells, 0, 1, axis=dim)
+    high = lax.slice_in_dim(cells, size - 1, size, axis=dim)
+    before, after = both_ways(low, high, axis)
+    return jnp.concatenate([before, cells, after], axis=dim)
+
+
+def three_slabs(cells):
+    before, after = both_ways(cells, cells, "gx")
+    return [
+        slab.reshape(slab.shape[0], PLANE, SLOTS) for slab in (before, cells, after)
+    ]
 
 
 def exchange(parts, axes):
@@ -434,30 +478,32 @@
 def device_step(fractions, polarizability, occupancy, pair_mask, perm_field, history):
     plane = lax.axis_size("gy") * lax.axis_size("gz")
     line = lax.axis_size("gx")
-    history = history.reshape(6, 6, OWN, SLOTS)
     occupancy = occupancy.reshape(OWN, SLOTS)
-    perm = perm_field.reshape(6, OWN, SLOTS)
-
-    gram = local_gram(history, occupancy, plane)
-    filled = occupancy.astype(jnp.float32)
-    later = (history[1:] * filled).reshape(30, 1, 2, 2, SLOTS)
-    stacked = jnp.concatenate([fractions, polarizability[None], later], 0)
-    stacked, gram = lax.optimization_barrier((stacked, gram))
+    stacked, gram = prepare(
+        fractions.reshape(3, OWN, SLOTS),
+        polarizability.reshape(OWN, SLOTS),
+        occupancy,
+        history.reshape(6, 6, OWN, SLOTS),
+        plane,
+    )
     gram = exchange(gram, ("gy", "gz"))
-    ghosts = with_halo(stacked, SIDES[:2])
+    cells = joined(stacked.reshape(ROWS, 2, 2, SLOTS), "gz", 2)
+    cells = joined(cells, "gy", 1)
     gram = sum_parts(gram, line)
-    ghosts, gram = lax.optimization_barrier((ghosts, gram))
+    cells, gram = lax.optimization_barrier((cells, gram))
     gram = exchange(gram, "gx")
-    ghosts = with_halo(ghosts, SIDES[2:])
-
-    geo = ghosts[:4].reshape(4, TILES, SLOTS)
-    later = ghosts[4:].reshape(30, TILES, SLOTS)
-    dipoles, pair_list, pairs = first_field(
-        pair_mask.reshape(OWN, OFFSETS), gram, geo, later, occupancy, perm
-    )
-    dipoles = with_halo(dipoles.reshape(6, 1, 2, 2, SLOTS), SIDES).reshape(6, TILES, SLOTS)
+    slabs = three_slabs(cells)
+    dipoles, pair_list, geo, scaled, perm, pairs = first_field(
+        pair_mask.reshape(OWN, OFFSETS),
+        occupancy,
+        perm_field.reshape(6, OWN, SLOTS),
+        gram,
+        slabs,
+    )
+    cells = joined(dipoles.reshape(6, 2, 2, SLOTS), "gz", 2)
+    cells = joined(cells, "gy", 1)
     induced, sizes = second_field(
-        pair_list, geo, dipoles, occupancy, perm, pairs, plane
+        pair_list, geo, three_slabs(cells), scaled, perm, pairs, plane
     )
     sizes = exchange(sizes, ("gy", "gz"))
     sizes = exchange(sum_parts(sizes, line), "gx")

time: 131 us -> 126 us (0.962)
  blocking collectives: 52.1 us -> 58.4 us
  waiting for transfers between devices: 10.5 us -> 4.32 us
  starting transfers between devices: 44.4 us -> 41.4 us
  local copies, waits for them, and re-layouts: 4.74 us -> 3.15 us
    all_to_all x1 -> x0, starting transfers between devices: 9.77 us -> none  [exchange(): return lax.all_to_all(parts, axes, 0, 0)]
    ppermute x12, starting transfers between devices: 34.6 us -> 41.4 us  [the longest x6 27.4 us: both_ways(): lax.ppermute(low, axis, [((i + 1) % count, i) for i in range(count)])]
    all_to_all x1 -> x0, waiting for transfers between devices: 6.37 us -> none  [exchange(): return lax.all_to_all(parts, axes, 0, 0)]
    all_to_all x3 -> x4, blocking collectives: 52.1 us -> 58.4 us  [exchange(): return lax.all_to_all(parts, axes, 0, 0)]
    unnamed x10 -> x6, local copies, waits for them, and re-layouts: 2.8 us -> 2.07 us
  transfers between devices with their start and end apart: 13 -> 12, of which waited for: 6 -> 4; matrix products, arithmetic and copies ran while one was open for 1% -> 0% of each run, Pallas kernels for 0% -> 0%
where the time goes in v4:
time: 126 us; the launch traced here: 125 us
  blocking collectives  58.4 us (46%)
  starting transfers between devices  41.4 us (33%)
  Pallas kernels  14.8 us (12%)
  waiting for transfers between devices  4.32 us (3%)
  local copies, waits for them, and re-layouts  3.15 us (2%)
  other arithmetic  2.7 us (2%)
    all_to_all x4, blocking collectives, exchange(): return lax.all_to_all(parts, axes, 0, 0)  58.4 us
    ppermute x6, starting transfers between devices, both_ways(): lax.ppermute(low, axis, [((i + 1) % count, i) for i in range(count)])  27.4 us
    ppermute x6, starting transfers between devices, both_ways(): lax.ppermute(high, axis, [(i, (i + 1) % count) for i in range(count)])  13.9 us
    pallas_call x1, Pallas kernels, first_field(): pl.pallas_call(first_kernel, name='first_field', in_specs=[whole_array] *...  9.04 us
    ppermute x6, waiting for transfers between devices, both_ways(): lax.ppermute(low, axis, [((i + 1) % count, i) for i in range(count)])  4.3 us
    pallas_call x1, Pallas kernels, second_field(): pl.pallas_call(second_kernel, name='second_field', in_specs=[smem_spec()]...  4.03 us
  transfers between devices with their start and end apart: 12, of which 4 were waited for; matrix products, arithmetic and copies ran while one was open for 0% of the time, Pallas kernels for 0%

profile of v4, /device:TPU:1, one launch (start us, length us, event | category | flops | bytes accessed | tf_op | source)
XLA Modules:
  0.0 125.4 jit_solution(7884584124182740699)
XLA Ops:
  0.6 1.7 %prepare.1 = (f32[34,4,128]{2,1,0:T(4,128)}, f32[32,1,128]{2,1,0:T(1,128)}) custom-call(f32[3,4,128]{2,1,0:T(4,128)} %bitcast.36, f32[4,128]{1,0:T(4,128)} %bitcast.37, s32[4,128]{1,0:T(4,128)} %bitcast.26, f32[6,6,4,128]{3,2,1,0:T(4,128)} %bitcast.35), custom_call_target="tpu_custom_call" | custom-call | tf_op jit(solution)/shard_map/prepare/pallas_call | solution.py:287
  2.3 1.0 fusion.2
  3.3 4.8 %collective-permute-start = (f32[34,2,1,128]{3,2,1,0:T(1,128)S(1)}, f32[34,2,1,128]{3,2,1,0:T(1,128)S(1)}, u32[]{:S(2)}, u32[]{:S(2)}) collective-permute-start(f32[34,2,1,128]{3,2,1,0:T(1,128)S(1)} %get-tuple-element.34), channel_id=1, source_target_pairs={{0,1},{1,2},{2,3},{3,4},{4,5},{5,6},{6,7},{7,0},{8,9},{9,10},{10,1... | collective-permute-start | bytes 104456 | tf_op jit(solution)/shard_map/ppermute | solution.py:454
  8.2 8.6 %collective-permute-start.1 = (f32[34,2,1,128]{3,2,1,0:T(1,128)S(1)}, f32[34,2,1,128]{3,2,1,0:T(1,128)S(1)}, u32[]{:S(2)}, u32[]{:S(2)}) collective-permute-start(f32[34,2,1,128]{3,2,1,0:T(1,128)S(1)} %get-tuple-element.35), channel_id=1, source_target_pairs={{1,0},{2,1},{3,2},{4,3},{5,4},{6,5},{7,6},{0,7},{9,8},{10,9},{11,1... | collective-permute-start | bytes 104456 | tf_op jit(solution)/shard_map/ppermute | solution.py:455
  16.8 0.0 collective-permute-done
  16.8 1.0 collective-permute-done.1
  17.8 1.0 pad_maximum_fusion.1
  18.8 3.1 %collective-permute-start.2 = (f32[34,1,4,128]{3,2,1,0:T(4,128)S(1)}, f32[34,1,4,128]{3,2,1,0:T(4,128)S(1)}, u32[]{:S(2)}, u32[]{:S(2)}) collective-permute-start(f32[34,1,4,128]{3,2,1,0:T(4,128)S(1)} %get-tuple-element.32), channel_id=1, source_target_pairs={{0,8},{8,16},{16,24},{24,0},{1,9},{9,17},{17,25},{25,1},{2,10},{10... | collective-permute-start | bytes 208904 | tf_op jit(solution)/shard_map/ppermute | solution.py:454
  21.9 3.4 %collective-permute-start.3 = (f32[34,1,4,128]{3,2,1,0:T(4,128)S(1)}, f32[34,1,4,128]{3,2,1,0:T(4,128)S(1)}, u32[]{:S(2)}, u32[]{:S(2)}) collective-permute-start(f32[34,1,4,128]{3,2,1,0:T(4,128)S(1)} %get-tuple-element.33), channel_id=1, source_target_pairs={{8,0},{16,8},{24,16},{0,24},{9,1},{17,9},{25,17},{1,25},{10,2},{18... | collective-permute-start | bytes 208904 | tf_op jit(solution)/shard_map/ppermute | solution.py:455
  25.3 14.8 %all_to_all.20 = f32[32,1,128]{2,1,0:T(1,128)S(1)} all-to-all(f32[32,1,128]{2,1,0:T(1,128)} %get-tuple-element.15), channel_id=1, replica_groups=mesh['gx'=16,'gy'=4,'gz'=8] {'gy','gz'}, dimensions={0} | all-to-all | bytes 32768 | tf_op jit(solution)/shard_map/all_to_all | solution.py:475
  40.1 0.1 reduce_sum.27
  40.1 0.0 collective-permute-done.2
  40.1 0.0 collective-permute-done.3
  40.1 1.0 pad_maximum_fusion
  41.2 4.1 %collective-permute-start.5 = (f32[34,4,4,128]{3,2,1,0:T(4,128)S(1)}, f32[34,4,4,128]{3,2,1,0:T(4,128)S(1)}, u32[]{:S(2)}, u32[]{:S(2)}) collective-permute-start(f32[34,4,4,128]{3,2,1,0:T(4,128)S(1)} %pad_maximum_fusion), channel_id=1, source_target_pairs={{32,0},{64,32},{96,64},{128,96},{160,128},{192,160},{224,192},{256... | collective-permute-start | bytes 835592 | tf_op jit(solution)/shard_map/ppermute | solution.py:455
  45.3 1.2 collective-permute-start.4
  46.5 13.2 %all_to_all.21.gram_ref = f32[16,1,128]{2,1,0:T(1,128)S(1)} all-to-all(f32[16,1,128]{2,1,0:T(1,128)S(1)} %broadcast_in_dim.4), channel_id=1, replica_groups=mesh['gx'=16,'gy'=4,'gz'=8] {'gx'}, dimensions={0} | all-to-all | bytes 16384 | tf_op jit(solution)/shard_map/all_to_all | solution.py:475
  59.7 0.0 collective-permute-done.5
  59.7 0.0 collective-permute-done.4
  59.7 0.0 copy-start
  59.8 0.7 copy-done
  60.4 0.0 copy-start.1
  60.4 0.7 copy-done.1
  61.1 0.0 copy-start.2
  61.1 0.7 copy-done.2
  61.8 9.0 %first_field.1 = (f32[6,4,128]{2,1,0:T(4,128)S(1)}, s32[128]{0:T(128)S(1)}, f32[4,48,128]{2,1,0:T(8,128)S(1)}, f32[4,128]{1,0:T(4,128)S(1)}, f32[6,4,128]{2,1,0:...) custom-call(s32[4,27]{1,0:T(4,128)S(1)} %bitcast.31, s32[4,128]{1,0:T(4,128)S(1)} %bitcast.27, f32[6,4,128]{2,1,0:T(4,128)S(1)} %bitcast.30, ...), custom_call_target="tpu_custom_call" | custom-call | flops 2000000000 | bytes 1000000 | tf_op jit(solution)/shard_map/first_field/pallas_call | solution.py:406
  70.9 2.3 %collective-permute-start.6 = (f32[6,2,1,128]{3,2,1,0:T(1,128)S(1)}, f32[6,2,1,128]{3,2,1,0:T(1,128)S(1)}, u32[]{:S(2)}, u32[]{:S(2)}) collective-permute-start(f32[6,2,1,128]{3,2,1,0:T(1,128)S(1)} %get-tuple-element.38), channel_id=1, source_target_pairs={{0,1},{1,2},{2,3},{3,4},{4,5},{5,6},{6,7},{7,0},{8,9},{9,10},{10,1... | collective-permute-start | bytes 18440 | tf_op jit(solution)/shard_map/ppermute | solution.py:454
  73.2 4.2 %collective-permute-start.7 = (f32[6,2,1,128]{3,2,1,0:T(1,128)S(1)}, f32[6,2,1,128]{3,2,1,0:T(1,128)S(1)}, u32[]{:S(2)}, u32[]{:S(2)}) collective-permute-start(f32[6,2,1,128]{3,2,1,0:T(1,128)S(1)} %get-tuple-element.39), channel_id=1, source_target_pairs={{1,0},{2,1},{3,2},{4,3},{5,4},{6,5},{7,6},{0,7},{9,8},{10,9},{11,1... | collective-permute-start | bytes 18440 | tf_op jit(solution)/shard_map/ppermute | solution.py:455
  77.4 0.0 collective-permute-done.6
  77.4 0.7 collective-permute-done.7
  78.2 2.3 %collective-permute-start.8 = (f32[6,1,4,128]{3,2,1,0:T(4,128)S(1)}, f32[6,1,4,128]{3,2,1,0:T(4,128)S(1)}, u32[]{:S(2)}, u32[]{:S(2)}) collective-permute-start(f32[6,1,4,128]{3,2,1,0:T(4,128)S(1)} %get-tuple-element.36), channel_id=1, source_target_pairs={{0,8},{8,16},{16,24},{24,0},{1,9},{9,17},{17,25},{25,1},{2,10},{10... | collective-permute-start | bytes 36872 | tf_op jit(solution)/shard_map/ppermute | solution.py:454
  80.5 4.2 %collective-permute-start.9 = (f32[6,1,4,128]{3,2,1,0:T(4,128)S(1)}, f32[6,1,4,128]{3,2,1,0:T(4,128)S(1)}, u32[]{:S(2)}, u32[]{:S(2)}) collective-permute-start(f32[6,1,4,128]{3,2,1,0:T(4,128)S(1)} %get-tuple-element.37), channel_id=1, source_target_pairs={{8,0},{16,8},{24,16},{0,24},{9,1},{17,9},{25,17},{1,25},{10,2},{18... | collective-permute-start | bytes 36872 | tf_op jit(solution)/shard_map/ppermute | solution.py:455
  84.7 0.0 collective-permute-done.8
  84.7 0.8 collective-permute-done.9
  85.5 2.9 %collective-permute-start.11 = (f32[6,4,4,128]{3,2,1,0:T(4,128)S(1)}, f32[6,4,4,128]{3,2,1,0:T(4,128)S(1)}, u32[]{:S(2)}, u32[]{:S(2)}) collective-permute-start(f32[6,4,4,128]{3,2,1,0:T(4,128)S(1)} %pad_maximum_fusion.2), channel_id=1, source_target_pairs={{32,0},{64,32},{96,64},{128,96},{160,128},{192,160},{224,192},{256... | collective-permute-start | bytes 147464 | tf_op jit(solution)/shard_map/ppermute | solution.py:455
  88.5 0.2 collective-permute-start.10
  88.7 1.7 %collective-permute-done.11 = f32[6,4,4,128]{3,2,1,0:T(4,128)S(1)} collective-permute-done((f32[6,4,4,128]{3,2,1,0:T(4,128)S(1)}, f32[6,4,4,128]{3,2,1,0:T(4,128)S(1)}, u32[]{:S(2)}, u32[]{:S(2)}) %collective-permute-start.11) | collective-permute-done | bytes 49184 | tf_op jit(solution)/shard_map/ppermute | solution.py:455
  90.4 0.0 collective-permute-done.10
  90.4 4.0 %second_field.1 = (f32[6,4,128]{2,1,0:T(4,128)}, f32[32,2,128]{2,1,0:T(2,128)S(1)}) custom-call(s32[128]{0:T(128)S(1)} %get-tuple-element.18.list_ref, f32[4,48,128]{2,1,0:T(8,128)S(1)} %get-tuple-element.19.geo_ref, f32[6,16,128]{2,1,0:T(8,128)S(1)} %bitcast.25, f32[6,16,128]{2,1,0:T(8,128)S(1)} %bitcast.20, f32[6,16,128]{2,1,0:T(8,128)S(1)} %bitcast.24, ...), custom_call_target="tpu_custom_call" | custom-call | flops 1000000000 | bytes 1000000 | tf_op jit(solution)/shard_map/second_field/pallas_call | solution.py:435
  94.5 16.4 %all_to_all.22 = f32[32,2,128]{2,1,0:T(2,128)S(1)} all-to-all(f32[32,2,128]{2,1,0:T(2,128)S(1)} %get-tuple-element.25), channel_id=1, replica_groups=mesh['gx'=16,'gy'=4,'gz'=8] {'gy','gz'}, dimensions={0} | all-to-all | bytes 65536 | tf_op jit(solution)/shard_map/all_to_all | solution.py:475
  110.9 14.0 %all_to_all.23 = f32[16,2,128]{2,1,0:T(2,128)S(1)} all-to-all(f32[16,2,128]{2,1,0:T(2,128)S(1)} %broadcast_in_dim.5), channel_id=1, replica_groups=mesh['gx'=16,'gy'=4,'gz'=8] {'gx'}, dimensions={0} | all-to-all | bytes 32768 | tf_op jit(solution)/shard_map/all_to_all | solution.py:475
  124.9 0.5 fusion
  (9 shorter events, 0.2 us)
Async XLA Ops:
  3.3 13.4 %collective-permute-start = (f32[34,2,1,128]{3,2,1,0:T(1,128)S(1)}, f32[34,2,1,128]{3,2,1,0:T(1,128)S(1)}, u32[]{:S(2)}, u32[]{:S(2)}) collective-permute-start(f32[34,2,1,128]{3,2,1,0:T(1,128)S(1)} %get-tuple-element.34), channel_id=1, source_target_pairs={{0,1},{1,2},{2,3},{3,4},{4,5},{5,6},{6,7},{7,0},{8,9},{9,10},{10,1... | collective-permute-start | bytes 104456 | tf_op jit(solution)/shard_map/ppermute | solution.py:454
  8.2 9.6 %collective-permute-start.1 = (f32[34,2,1,128]{3,2,1,0:T(1,128)S(1)}, f32[34,2,1,128]{3,2,1,0:T(1,128)S(1)}, u32[]{:S(2)}, u32[]{:S(2)}) collective-permute-start(f32[34,2,1,128]{3,2,1,0:T(1,128)S(1)} %get-tuple-element.35), channel_id=1, source_target_pairs={{1,0},{2,1},{3,2},{4,3},{5,4},{6,5},{7,6},{0,7},{9,8},{10,9},{11,1... | collective-permute-start | bytes 104456 | tf_op jit(solution)/shard_map/ppermute | solution.py:455
  18.8 21.3 %collective-permute-start.2 = (f32[34,1,4,128]{3,2,1,0:T(4,128)S(1)}, f32[34,1,4,128]{3,2,1,0:T(4,128)S(1)}, u32[]{:S(2)}, u32[]{:S(2)}) collective-permute-start(f32[34,1,4,128]{3,2,1,0:T(4,128)S(1)} %get-tuple-element.32), channel_id=1, source_target_pairs={{0,8},{8,16},{16,24},{24,0},{1,9},{9,17},{17,25},{25,1},{2,10},{10... | collective-permute-start | bytes 208904 | tf_op jit(solution)/shard_map/ppermute | solution.py:454
  21.9 18.2 %collective-permute-start.3 = (f32[34,1,4,128]{3,2,1,0:T(4,128)S(1)}, f32[34,1,4,128]{3,2,1,0:T(4,128)S(1)}, u32[]{:S(2)}, u32[]{:S(2)}) collective-permute-start(f32[34,1,4,128]{3,2,1,0:T(4,128)S(1)} %get-tuple-element.33), channel_id=1, source_target_pairs={{8,0},{16,8},{24,16},{0,24},{9,1},{17,9},{25,17},{1,25},{10,2},{18... | collective-permute-start | bytes 208904 | tf_op jit(solution)/shard_map/ppermute | solution.py:455
  41.2 18.6 %collective-permute-start.5 = (f32[34,4,4,128]{3,2,1,0:T(4,128)S(1)}, f32[34,4,4,128]{3,2,1,0:T(4,128)S(1)}, u32[]{:S(2)}, u32[]{:S(2)}) collective-permute-start(f32[34,4,4,128]{3,2,1,0:T(4,128)S(1)} %pad_maximum_fusion), channel_id=1, source_target_pairs={{32,0},{64,32},{96,64},{128,96},{160,128},{192,160},{224,192},{256... | collective-permute-start | bytes 835592 | tf_op jit(solution)/shard_map/ppermute | solution.py:455
  45.3 14.5 %collective-permute-start.4 = (f32[34,4,4,128]{3,2,1,0:T(4,128)S(1)}, f32[34,4,4,128]{3,2,1,0:T(4,128)S(1)}, u32[]{:S(2)}, u32[]{:S(2)}) collective-permute-start(f32[34,4,4,128]{3,2,1,0:T(4,128)S(1)} %pad_maximum_fusion), channel_id=1, source_target_pairs={{0,32},{32,64},{64,96},{96,128},{128,160},{160,192},{192,224},{224... | collective-permute-start | bytes 835592 | tf_op jit(solution)/shard_map/ppermute | solution.py:454
  59.7 0.7 copy-start
  60.4 0.7 copy-start.1
  61.1 0.7 copy-start.2
  70.9 6.5 %collective-permute-start.6 = (f32[6,2,1,128]{3,2,1,0:T(1,128)S(1)}, f32[6,2,1,128]{3,2,1,0:T(1,128)S(1)}, u32[]{:S(2)}, u32[]{:S(2)}) collective-permute-start(f32[6,2,1,128]{3,2,1,0:T(1,128)S(1)} %get-tuple-element.38), channel_id=1, source_target_pairs={{0,1},{1,2},{2,3},{3,4},{4,5},{5,6},{6,7},{7,0},{8,9},{9,10},{10,1... | collective-permute-start | bytes 18440 | tf_op jit(solution)/shard_map/ppermute | solution.py:454
  73.2 5.0 %collective-permute-start.7 = (f32[6,2,1,128]{3,2,1,0:T(1,128)S(1)}, f32[6,2,1,128]{3,2,1,0:T(1,128)S(1)}, u32[]{:S(2)}, u32[]{:S(2)}) collective-permute-start(f32[6,2,1,128]{3,2,1,0:T(1,128)S(1)} %get-tuple-element.39), channel_id=1, source_target_pairs={{1,0},{2,1},{3,2},{4,3},{5,4},{6,5},{7,6},{0,7},{9,8},{10,9},{11,1... | collective-permute-start | bytes 18440 | tf_op jit(solution)/shard_map/ppermute | solution.py:455
  78.2 6.5 %collective-permute-start.8 = (f32[6,1,4,128]{3,2,1,0:T(4,128)S(1)}, f32[6,1,4,128]{3,2,1,0:T(4,128)S(1)}, u32[]{:S(2)}, u32[]{:S(2)}) collective-permute-start(f32[6,1,4,128]{3,2,1,0:T(4,128)S(1)} %get-tuple-element.36), channel_id=1, source_target_pairs={{0,8},{8,16},{16,24},{24,0},{1,9},{9,17},{17,25},{25,1},{2,10},{10... | collective-permute-start | bytes 36872 | tf_op jit(solution)/shard_map/ppermute | solution.py:454
  80.5 5.0 %collective-permute-start.9 = (f32[6,1,4,128]{3,2,1,0:T(4,128)S(1)}, f32[6,1,4,128]{3,2,1,0:T(4,128)S(1)}, u32[]{:S(2)}, u32[]{:S(2)}) collective-permute-start(f32[6,1,4,128]{3,2,1,0:T(4,128)S(1)} %get-tuple-element.37), channel_id=1, source_target_pairs={{8,0},{16,8},{24,16},{0,24},{9,1},{17,9},{25,17},{1,25},{10,2},{18... | collective-permute-start | bytes 36872 | tf_op jit(solution)/shard_map/ppermute | solution.py:455
  85.5 4.9 %collective-permute-start.11 = (f32[6,4,4,128]{3,2,1,0:T(4,128)S(1)}, f32[6,4,4,128]{3,2,1,0:T(4,128)S(1)}, u32[]{:S(2)}, u32[]{:S(2)}) collective-permute-start(f32[6,4,4,128]{3,2,1,0:T(4,128)S(1)} %pad_maximum_fusion.2), channel_id=1, source_target_pairs={{32,0},{64,32},{96,64},{128,96},{160,128},{192,160},{224,192},{256... | collective-permute-start | bytes 147464 | tf_op jit(solution)/shard_map/ppermute | solution.py:455
  88.5 2.0 %collective-permute-start.10 = (f32[6,4,4,128]{3,2,1,0:T(4,128)S(1)}, f32[6,4,4,128]{3,2,1,0:T(4,128)S(1)}, u32[]{:S(2)}, u32[]{:S(2)}) collective-permute-start(f32[6,4,4,128]{3,2,1,0:T(4,128)S(1)} %pad_maximum_fusion.2), channel_id=1, source_target_pairs={{0,32},{32,64},{64,96},{96,128},{128,160},{160,192},{192,224},{224... | collective-permute-start | bytes 147464 | tf_op jit(solution)/shard_map/ppermute | solution.py:454

commit v5 on v4

v5 whole, which is shorter than its diff:
```python
import jax
import jax.numpy as jnp
from jax import lax
from jax.experimental import pallas as pl
from jax.experimental.pallas import tpu as pltpu


CELL_EDGE = 10.0
SOFTENING = 0.3
THOLE_DAMP = 0.39
RELAXATION = 0.7
LN2 = 0.6931471805599453

SLOTS = 128
NX, NY, NZ = 3, 4, 4
TILES = NX * NY * NZ
OWN = 4
OFFSETS = 27
TERMS = 48
A_ROWS = 96
B_ROWS = 24
BATCH = 13
LIST = 128
COUNT_AT = LIST - 1
ROWS = 34
LAYER = NX * NY
INNER = 2 * LAYER
GRAM = tuple((a, b) for a in range(6) for b in range(a + 1))


def source_tile(tile, offset):
    x = offset // 9
    y = tile // 2 + offset // 3 % 3
    z = tile % 2 + offset % 3
    column = x * NY + y
    if z == 0:
        return INNER + column
    if z == NZ - 1:
        return INNER + LAYER + column
    return column * 2 + z - 1


def candidates(inner):
    return [
        (t, k)
        for t in range(OWN)
        for k in range(OFFSETS)
        if k != 13 and (source_tile(t, k) < INNER) == inner
    ]


OWN_TILES = tuple(source_tile(t, 13) for t in range(OWN))


def split3(value):
    high = value.astype(jnp.bfloat16).astype(jnp.float32)
    rest = value - high
    middle = rest.astype(jnp.bfloat16).astype(jnp.float32)
    return high, middle, rest - middle


def positions(geo, first):
    shape = geo[0].shape
    tile = lax.broadcasted_iota(jnp.int32, shape, 0) + first
    own = tile < INNER
    edge = tile - INNER
    above = edge >= LAYER
    column = jnp.where(own, tile // 2, jnp.where(above, edge - LAYER, edge))
    layer = jnp.where(own, tile % 2 + 1, jnp.where(above, NZ - 1, 0))
    x = (column // NY).astype(jnp.float32)
    y = (column % NY).astype(jnp.float32)
    z = layer.astype(jnp.float32)
    return (
        (geo[0] + (x - 1.5)) * CELL_EDGE,
        (geo[1] + (y - 2.0)) * CELL_EDGE,
        (geo[2] + (z - 2.0)) * CELL_EDGE,
    )


def scale_of(polar):
    factor = (THOLE_DAMP / LN2) ** (1.0 / 3.0)
    return factor * jnp.exp(jnp.log(polar) * (-1.0 / 3.0))


def own_rows(value):
    return [value[t : t + 1] for t in OWN_TILES]


def prepare_distances(own_geo, source_geo, first, q_ref, p_ref):
    def terms(geo, at):
        r = positions(geo, at)
        a = scale_of(geo[3])
        return r, a, r[0] * r[0] + r[1] * r[1] + r[2] * r[2]

    r, a, norm = terms(source_geo, first)
    count = a.shape[0]
    sources = [a, a * (norm + SOFTENING), a * r[0], a * r[1], a * r[2]]
    r, a, norm = terms(own_geo, 0)
    targets = [a * norm, a, -2.0 * a * r[0], -2.0 * a * r[1], -2.0 * a * r[2]]
    row = 0
    for source, target in zip(sources, targets):
        source_parts = split3(source)
        target_parts = split3(target)
        for s in range(3):
            for t in range(3):
                q_ref[pl.ds(row, count, stride=TERMS + 1), :] = source_parts[s]
                for own in range(OWN):
                    p_ref[own, row : row + 1, :] = target_parts[t][
                        OWN_TILES[own] : OWN_TILES[own] + 1
                    ]
                row += 1
    zero = jnp.zeros((count, SLOTS), jnp.float32)
    for rest in range(row, TERMS):
        q_ref[pl.ds(rest, count, stride=TERMS + 1), :] = zero
        for own in range(OWN):
            p_ref[own, rest : rest + 1, :] = zero[0:1]
    last = INNER * (TERMS + 1)
    q_ref[last : last + TERMS, :] = q_ref[0:TERMS, :]


def list_pairs(mask_ref, list_ref, inner):
    first = 0 if inner else INNER
    count = jnp.int32(0)
    for t, k in candidates(inner):
        list_ref[count] = (source_tile(t, k) - first) * OWN + t
        count = count + (mask_ref[t, k] != 0).astype(jnp.int32)
    for extra in range(BATCH):
        list_ref[count + extra] = INNER * OWN
    list_ref[COUNT_AT] = count
    return count


def trips(count):
    return (count + BATCH - 1) // BATCH


def build_all(list_ref, count, start, pair_ref, q_ref, p_ref):
    def batch(b, carry):
        for u in range(BATCH):
            slot = b * BATCH + u
            entry = list_ref[slot]
            build(start + slot, entry // OWN, entry % OWN, None, pair_ref, q_ref, p_ref)
        return carry

    lax.fori_loop(0, trips(count), batch, 0)


def build(slot, n, t, keep, pair_ref, q_ref, p_ref):
    radial, direct = pair_functions(n, t, q_ref, p_ref, keep)
    pair_ref[slot, 0 : 2 * SLOTS, :] = radial
    pair_ref[slot, 2 * SLOTS : 4 * SLOTS, :] = direct


def pair_functions(n, t, q_ref, p_ref, keep):
    dist = lax.dot_general(
        q_ref[pl.ds(n * (TERMS + 1), TERMS), :].astype(jnp.bfloat16),
        p_ref[t].astype(jnp.bfloat16),
        (((0,), (0,)), ((), ())),
        preferred_element_type=jnp.float32,
    )
    inv = lax.rsqrt(dist)
    arg = dist * (dist * inv)
    damp = jnp.exp2(-arg)
    inv2 = inv * inv
    direct = (1.0 - damp) * (inv2 * inv)
    radial = inv2 * (direct - LN2 * damp)
    if keep is not None:
        direct = jnp.where(keep, direct, 0.0)
        radial = jnp.where(keep, radial, 0.0)
    result = []
    for value in (radial, direct):
        high = value.astype(jnp.bfloat16)
        low = (value - high.astype(jnp.float32)).astype(jnp.bfloat16)
        result.append(jnp.concatenate([high, low], axis=0))
    return result


def prepare_moments(geo, first, moment, a_ref, b_ref):
    r = positions(geo, first)
    count = geo[0].shape[0]
    scale_a, scale_b = factors(geo)
    zero = jnp.zeros((count, SLOTS), jnp.float32)
    for kind in range(2):
        m = [moment[3 * kind + c] * scale_a for c in range(3)]
        outer = [r[c] * m[d] for c in range(3) for d in range(3)]
        g = outer[0] + outer[4] + outer[8]
        values = [None] + [r[c] * g for c in range(3)] + m + outer
        for index, value in enumerate(values):
            parts = (zero, zero, zero) if value is None else split3(value)
            for s, part in enumerate(parts):
                row = 32 * s + 16 * kind + index
                a_ref[pl.ds(row, count, stride=A_ROWS + 1), :] = part
    for c in range(8):
        parts = (zero, zero, zero) if c >= 6 else split3(moment[c] * scale_b)
        for s, part in enumerate(parts):
            b_ref[pl.ds(8 * s + c, count, stride=B_ROWS + 1), :] = part
    last_a = INNER * (A_ROWS + 1)
    last_b = INNER * (B_ROWS + 1)
    a_ref[last_a : last_a + A_ROWS, :] = jnp.zeros((A_ROWS, SLOTS), jnp.float32)
    b_ref[last_b : last_b + B_ROWS, :] = jnp.zeros((B_ROWS, SLOTS), jnp.float32)


def factors(geo):
    a = scale_of(geo[3])
    scale_b = a * jnp.sqrt(a)
    return scale_b * a, scale_b


def product(n, radial, direct, a_ref, b_ref):
    left = a_ref[pl.ds(n * (A_ROWS + 1), A_ROWS), :].astype(jnp.bfloat16)
    part_a = jnp.dot(
        jnp.concatenate([left, left], axis=1), radial, preferred_element_type=jnp.float32
    )
    left = b_ref[pl.ds(n * (B_ROWS + 1), B_ROWS), :].astype(jnp.bfloat16)
    part_b = jnp.dot(
        jnp.concatenate([left, left], axis=1), direct, preferred_element_type=jnp.float32
    )
    return part_a, part_b


def apply_slot(slot, n, pair_ref, a_ref, b_ref):
    return product(
        n,
        pair_ref[slot, 0 : 2 * SLOTS, :],
        pair_ref[slot, 2 * SLOTS : 4 * SLOTS, :],
        a_ref,
        b_ref,
    )


def apply_selves(pair_ref, a_ref, b_ref, sum_a, sum_b):
    for slot in range(OWN):
        sum_a[slot], sum_b[slot] = apply_slot(slot, OWN_TILES[slot], pair_ref, a_ref, b_ref)


def apply_all(list_ref, count, start, pair_ref, a_ref, b_ref, sum_a, sum_b):
    def batch(b, carry):
        for u in range(BATCH):
            slot = b * BATCH + u
            entry = list_ref[slot]
            t = entry % OWN
            part_a, part_b = apply_slot(start + slot, entry // OWN, pair_ref, a_ref, b_ref)
            sum_a[t] += part_a
            sum_b[t] += part_b
        return carry

    lax.fori_loop(0, trips(count), batch, 0)


def field_of(geo, sum_a, sum_b):
    r = positions(geo, 0)
    scale_a, scale_b = factors(geo)
    own_r = [jnp.concatenate(own_rows(r[c]), 0) for c in range(3)]
    own_a = 3.0 * jnp.concatenate(own_rows(scale_a), 0)
    own_b = jnp.concatenate(own_rows(scale_b), 0)

    def total_a(kind, index):
        row = 16 * kind + index
        return sum_a[:, row, :] + sum_a[:, 32 + row, :] + sum_a[:, 64 + row, :]

    def total_b(row):
        return sum_b[:, row, :] + sum_b[:, 8 + row, :] + sum_b[:, 16 + row, :]

    fields = []
    for kind in range(2):
        outer = [[total_a(kind, 7 + 3 * c + d) for d in range(3)] for c in range(3)]
        g = outer[0][0] + outer[1][1] + outer[2][2]
        m = [total_a(kind, 4 + c) for c in range(3)]
        dot = own_r[0] * m[0] + own_r[1] * m[1] + own_r[2] * m[2] - g
        for c in range(3):
            cross = sum(own_r[d] * outer[c][d] for d in range(3))
            radial = total_a(kind, 1 + c) - cross + own_r[c] * dot
            fields.append(own_a * radial - own_b * total_b(3 * kind + c))
    return fields


def own_part(value):
    return jnp.concatenate(own_rows(value), 0)


def solve(gram):
    count = 5
    matrix = [[gram[max(a, b), min(a, b)] for b in range(count)] for a in range(count)]
    right = [gram[count, a] for a in range(count)]
    trace = matrix[0][0]
    for a in range(1, count):
        trace = trace + matrix[a][a]
    ridge = 0.001 * trace / count + 1.0
    for a in range(count):
        matrix[a][a] = matrix[a][a] + ridge
    for c in range(count):
        for a in range(c + 1, count):
            ratio = matrix[a][c] / matrix[c][c]
            for b in range(c + 1, a + 1):
                matrix[a][b] = matrix[a][b] - ratio * matrix[b][c]
            right[a] = right[a] - ratio * right[c]
    result = [None] * count
    for a in reversed(range(count)):
        rest = right[a]
        for b in range(a + 1, count):
            rest = rest - matrix[b][a] * result[b]
        result[a] = rest / matrix[a][a]
    return result


def prepare_kernel(
    fractions_ref, polar_ref, occupancy_ref, history_ref, perm_ref, mask_ref,
    stacked_ref, gram_ref, own_ref, mask_copy_ref,
):
    filled = occupancy_ref[...].astype(jnp.float32)
    scaled = RELAXATION * filled * polar_ref[...]
    own_ref[0] = scaled
    for c in range(6):
        own_ref[1 + c] = perm_ref[c]
    mask_copy_ref[...] = mask_ref[...]
    masked = [[history_ref[h, c] * filled for c in range(6)] for h in range(6)]
    for a in range(3):
        stacked_ref[a] = fractions_ref[a]
    stacked_ref[3] = polar_ref[...]
    for h in range(1, 6):
        for c in range(6):
            stacked_ref[4 + 6 * (h - 1) + c] = masked[h][c]
    lane = lax.broadcasted_iota(jnp.int32, (1, SLOTS), 1)
    row = jnp.zeros((1, SLOTS), jnp.float32)
    for index, (a, b) in enumerate(GRAM):
        product = masked[a][0] * masked[b][0]
        for c in range(1, 6):
            product = product + masked[a][c] * masked[b][c]
        total = jnp.sum(jnp.sum(product, axis=0, keepdims=True), axis=1, keepdims=True)
        row = jnp.where(lane == index, total, row)
    gram_ref[...] = jnp.broadcast_to(row[None], gram_ref.shape)


def vmem_spec():
    return pl.BlockSpec(memory_space=pltpu.VMEM)


def smem_spec():
    return pl.BlockSpec(memory_space=pltpu.SMEM)


def prepare(fractions, polarizability, occupancy, history, perm, mask, copies):
    return pl.pallas_call(
        prepare_kernel,
        name="prepare",
        in_specs=[vmem_spec()] * 6,
        out_specs=[vmem_spec()] * 4,
        out_shape=[
            jax.ShapeDtypeStruct((ROWS, OWN, SLOTS), jnp.float32),
            jax.ShapeDtypeStruct((copies, 1, SLOTS), jnp.float32),
            jax.ShapeDtypeStruct((7, OWN, SLOTS), jnp.float32),
            jax.ShapeDtypeStruct((OWN, OFFSETS), jnp.int32),
        ],
    )(fractions, polarizability, occupancy, history, perm, mask)


def sum_parts(parts, copies):
    total = jnp.sum(parts, axis=0, keepdims=True)
    return jnp.broadcast_to(total, (copies,) + total.shape[1:])


MOMENT_ROWS = [
    pltpu.VMEM(((INNER + 1) * (A_ROWS + 1), SLOTS), jnp.float32),
    pltpu.VMEM(((INNER + 1) * (B_ROWS + 1), SLOTS), jnp.float32),
]
DISTANCE_ROWS = [
    pltpu.VMEM(((INNER + 1) * (TERMS + 1), SLOTS), jnp.float32),
    pltpu.VMEM((OWN, TERMS, SLOTS), jnp.float32),
]
SUMS = [
    jax.ShapeDtypeStruct((OWN, A_ROWS, SLOTS), jnp.float32),
    jax.ShapeDtypeStruct((OWN, B_ROWS, SLOTS), jnp.float32),
]
PARAMS = pltpu.CompilerParams(vmem_limit_bytes=16 * 1024 * 1024)


def slots_for(inner):
    batches = -(-len(candidates(inner)) // BATCH)
    return batches * BATCH + (OWN if inner else 0)


def pair_shape(inner):
    return jax.ShapeDtypeStruct((slots_for(inner), 4 * SLOTS, SLOTS), jnp.bfloat16)


def cost(flops):
    return pl.CostEstimate(flops=flops, bytes_accessed=1_000_000, transcendentals=0)


def edge_rows(before_ref, after_ref, row):
    rows = pl.ds(row * LAYER, LAYER)
    return jnp.concatenate([before_ref[rows, :], after_ref[rows, :]], axis=0)


def coefficients(gram_ref):
    total = jnp.sum(gram_ref[...], axis=0)
    return solve({ab: total[0:1, i : i + 1] for i, ab in enumerate(GRAM)})


def predict(coeffs, later):
    moment = []
    for c in range(6):
        value = coeffs[0] * later[c]
        for h in range(1, 5):
            value = value + coeffs[h] * later[6 * h + c]
        moment.append(value)
    return moment


def inner_build_kernel(
    mask_ref, gram_ref, own_ref,
    list_ref, pair_ref, moment_ref, sum_a, sum_b,
    q_ref, p_ref, a_ref, b_ref,
):
    geo = [own_ref[a] for a in range(4)]
    prepare_distances(geo, geo, 0, q_ref, p_ref)
    count = list_pairs(mask_ref, list_ref, True)
    moment = predict(coefficients(gram_ref), [own_ref[row] for row in range(4, ROWS)])
    prepare_moments(geo, 0, moment, a_ref, b_ref)
    for c in range(6):
        moment_ref[c] = own_part(moment[c])
    keep = lax.broadcasted_iota(jnp.int32, (SLOTS, SLOTS), 0) != lax.broadcasted_iota(
        jnp.int32, (SLOTS, SLOTS), 1
    )
    for slot in range(OWN):
        build(slot, OWN_TILES[slot], slot, keep, pair_ref, q_ref, p_ref)
    build_all(list_ref, count, OWN, pair_ref, q_ref, p_ref)
    apply_selves(pair_ref, a_ref, b_ref, sum_a, sum_b)
    apply_all(list_ref, count, OWN, pair_ref, a_ref, b_ref, sum_a, sum_b)


def inner_build(mask, gram, own):
    return pl.pallas_call(
        inner_build_kernel,
        name="inner_build",
        in_specs=[smem_spec()] + [vmem_spec()] * 2,
        out_specs=[smem_spec()] + [vmem_spec()] * 4,
        out_shape=[
            jax.ShapeDtypeStruct((LIST,), jnp.int32),
            pair_shape(True),
            jax.ShapeDtypeStruct((6, OWN, SLOTS), jnp.float32),
        ]
        + SUMS,
        scratch_shapes=DISTANCE_ROWS + MOMENT_ROWS,
        compiler_params=PARAMS,
        cost_estimate=cost(2_000_000_000),
    )(mask, gram, own)


def first_kernel(
    mask_ref, gram_ref, own_ref, before_ref, after_ref, mine_ref, moment_ref, start_a, start_b,
    out_ref, list_ref, geo_ref, pair_ref,
    q_ref, p_ref, a_ref, b_ref, sum_a, sum_b,
):
    own_geo = [own_ref[a] for a in range(4)]
    edge_geo = [edge_rows(before_ref, after_ref, a) for a in range(4)]
    for a in range(4):
        geo_ref[a, 0:INNER, :] = own_geo[a]
        geo_ref[a, INNER:TILES, :] = edge_geo[a]
    prepare_distances(own_geo, edge_geo, INNER, q_ref, p_ref)
    count = list_pairs(mask_ref, list_ref, False)
    sum_a[...] = start_a[...]
    sum_b[...] = start_b[...]
    moment = predict(
        coefficients(gram_ref),
        [edge_rows(before_ref, after_ref, row) for row in range(4, ROWS)],
    )
    prepare_moments(edge_geo, INNER, moment, a_ref, b_ref)
    build_all(list_ref, count, 0, pair_ref, q_ref, p_ref)
    apply_all(list_ref, count, 0, pair_ref, a_ref, b_ref, sum_a, sum_b)

    fields = field_of(own_geo, sum_a, sum_b)
    for c in range(6):
        out_ref[c] = (1.0 - RELAXATION) * moment_ref[c] + mine_ref[0] * (
            mine_ref[1 + c] + fields[c]
        )


def first_field(mask, gram, own, before, after, mine, moment, sums):
    return pl.pallas_call(
        first_kernel,
        name="first_field",
        in_specs=[smem_spec()] + [vmem_spec()] * 8,
        out_specs=[vmem_spec(), smem_spec(), vmem_spec(), vmem_spec()],
        out_shape=[
            jax.ShapeDtypeStruct((6, OWN, SLOTS), jnp.float32),
            jax.ShapeDtypeStruct((LIST,), jnp.int32),
            jax.ShapeDtypeStruct((4, TILES, SLOTS), jnp.float32),
            pair_shape(False),
        ],
        scratch_shapes=DISTANCE_ROWS
        + MOMENT_ROWS
        + [pltpu.VMEM(part.shape, part.dtype) for part in SUMS],
        compiler_params=PARAMS,
        cost_estimate=cost(2_000_000_000),
    )(mask, gram, own, before, after, mine, moment, *sums)


def inner_apply_kernel(
    list_ref, geo_ref, own_ref, pair_ref, sum_a, sum_b, a_ref, b_ref
):
    geo = [geo_ref[a, 0:INNER, :] for a in range(4)]
    prepare_moments(geo, 0, [own_ref[c] for c in range(6)], a_ref, b_ref)
    apply_selves(pair_ref, a_ref, b_ref, sum_a, sum_b)
    apply_all(list_ref, list_ref[COUNT_AT], OWN, pair_ref, a_ref, b_ref, sum_a, sum_b)


def inner_apply(pair_list, geo, own, pairs):
    return pl.pallas_call(
        inner_apply_kernel,
        name="inner_apply",
        in_specs=[smem_spec()] + [vmem_spec()] * 3,
        out_specs=[vmem_spec()] * 2,
        out_shape=SUMS,
        scratch_shapes=MOMENT_ROWS,
        compiler_params=PARAMS,
        cost_estimate=cost(1_000_000_000),
    )(pair_list, geo, own, pairs)


def second_kernel(
    list_ref, geo_ref, own_ref, before_ref, after_ref, mine_ref, pair_ref, start_a, start_b,
    out_ref, size_ref, a_ref, b_ref, sum_a, sum_b,
):
    sum_a[...] = start_a[...]
    sum_b[...] = start_b[...]
    edge_geo = [geo_ref[a, INNER:TILES, :] for a in range(4)]
    moment = [edge_rows(before_ref, after_ref, c) for c in range(6)]
    prepare_moments(edge_geo, INNER, moment, a_ref, b_ref)
    apply_all(list_ref, list_ref[COUNT_AT], 0, pair_ref, a_ref, b_ref, sum_a, sum_b)

    fields = field_of([geo_ref[a, 0:INNER, :] for a in range(4)], sum_a, sum_b)
    moved = jnp.zeros((OWN, SLOTS), jnp.float32)
    size = jnp.zeros((OWN, SLOTS), jnp.float32)
    for c in range(6):
        old = own_part(own_ref[c])
        new = (1.0 - RELAXATION) * old + mine_ref[0] * (mine_ref[1 + c] + fields[c])
        out_ref[c] = new
        moved = moved + (new - old) * (new - old)
        size = size + new * new
    for index, value in enumerate((moved, size)):
        total = jnp.sum(jnp.sum(value, axis=0, keepdims=True), axis=1, keepdims=True)
        size_ref[:, index : index + 1, :] = jnp.broadcast_to(
            total[None], (size_ref.shape[0], 1, SLOTS)
        )


def second_field(pair_list, geo, own, before, after, mine, pairs, sums, copies):
    return pl.pallas_call(
        second_kernel,
        name="second_field",
        in_specs=[smem_spec()] + [vmem_spec()] * 8,
        out_specs=[vmem_spec(), vmem_spec()],
        out_shape=[
            jax.ShapeDtypeStruct((6, OWN, SLOTS), jnp.float32),
            jax.ShapeDtypeStruct((copies, 2, SLOTS), jnp.float32),
        ],
        scratch_shapes=MOMENT_ROWS + [pltpu.VMEM(sums.shape, sums.dtype) for sums in SUMS],
        compiler_params=PARAMS,
        cost_estimate=cost(1_000_000_000),
    )(pair_list, geo, own, before, after, mine, pairs, *sums)


def both_ways(low, high, axis):
    count = lax.axis_size(axis)
    before = lax.ppermute(high, axis, [(i, (i + 1) % count) for i in range(count)])
    after = lax.ppermute(low, axis, [((i + 1) % count, i) for i in range(count)])
    return before, after


def joined(cells, axis, dim):
    size = cells.shape[dim]
    low = lax.slice_in_dim(cells, 0, 1, axis=dim)
    high = lax.slice_in_dim(cells, size - 1, size, axis=dim)
    before, after = both_ways(low, high, axis)
    return jnp.concatenate([before, cells, after], axis=dim)


def z_layers(cells):
    rows = cells.shape[0]
    low = lax.slice_in_dim(cells, 0, 1, axis=3)
    high = lax.slice_in_dim(cells, 1, 2, axis=3)
    before, after = both_ways(low, high, "gz")
    return (
        cells.reshape(rows, INNER, SLOTS),
        before.reshape(rows * LAYER, SLOTS),
        after.reshape(rows * LAYER, SLOTS),
    )


def exchange(parts, axes):
    return lax.all_to_all(parts, axes, 0, 0)


def device_step(fractions, polarizability, occupancy, pair_mask, perm_field, history):
    plane = lax.axis_size("gy") * lax.axis_size("gz")
    line = lax.axis_size("gx")
    stacked, gram, mine, mask = prepare(
        fractions.reshape(3, OWN, SLOTS),
        polarizability.reshape(OWN, SLOTS),
        occupancy.reshape(OWN, SLOTS),
        history.reshape(6, 6, OWN, SLOTS),
        perm_field.reshape(6, OWN, SLOTS),
        pair_mask.reshape(OWN, OFFSETS),
        plane,
    )
    gram = exchange(gram, ("gy", "gz"))
    cells = joined(stacked.reshape(ROWS, 1, 2, 2, SLOTS), "gx", 1)
    cells = joined(cells, "gy", 2)
    gram = sum_parts(gram, line)
    cells, gram = lax.optimization_barrier((cells, gram))
    gram = exchange(gram, "gx")
    own, before, after = z_layers(cells)
    inner_list, inner_pairs, moment, *sums = inner_build(mask, gram, own)
    dipoles, outer_list, geo, outer_pairs = first_field(
        mask, gram, own, before, after, mine, moment, sums
    )
    cells = joined(dipoles.reshape(6, 1, 2, 2, SLOTS), "gx", 1)
    cells = joined(cells, "gy", 2)
    own, before, after = z_layers(cells)
    sums = inner_apply(inner_list, geo, own, inner_pairs)
    induced, sizes = second_field(
        outer_list, geo, own, before, after, mine, outer_pairs, sums, plane
    )
    sizes = exchange(sizes, ("gy", "gz"))
    sizes = exchange(sum_parts(sizes, line), "gx")
    totals = jnp.sum(sizes, axis=0)
    change = jnp.sqrt(totals[0] / (totals[1] + 1.0))
    return induced.reshape(6, 1, 2, 2, SLOTS), change[0]


def solution(mesh):
    from jax.sharding import PartitionSpec as P

    tiles = P("gx", "gy", "gz", None)
    sets = P(None, "gx", "gy", "gz", None)
    return jax.shard_map(
        device_step,
        mesh=mesh,
        in_specs=(
            sets,
            tiles,
            tiles,
            tiles,
            sets,
            P(None, None, "gx", "gy", "gz", None),
        ),
        out_specs=(sets, P()),
        check_vma=False,
    )
```

time: 126 us -> 129 us (1.024)
  blocking collectives: 58.4 us -> 49.2 us
  waiting for transfers between devices: 4.32 us -> 12.7 us
  Pallas kernels: 14.8 us -> 18 us
  other arithmetic: 2.7 us -> 0.99 us
  starting transfers between devices: 41.4 us -> 43.1 us
    all_to_all x0 -> x1, starting transfers between devices: none -> 10.7 us  [exchange(): return lax.all_to_all(parts, axes, 0, 0)]
    ppermute x6, starting transfers between devices: 27.4 us -> 18.1 us  [both_ways(): lax.ppermute(low, axis, [((i + 1) % count, i) for i in range(count)])]
    all_to_all x4 -> x3, blocking collectives: 58.4 us -> 49.2 us  [exchange(): return lax.all_to_all(parts, axes, 0, 0)]
    all_to_all x0 -> x1, waiting for transfers between devices: none -> 6.75 us  [exchange(): return lax.all_to_all(parts, axes, 0, 0)]
    pallas_call x2 -> x4, Pallas kernels: 10.7 us -> 15.6 us  [the longest x1 6.56 us: inner_build(): pl.pallas_call(inner_build_kernel, name='inner_build', in_specs=[smem_spe...]
    ppermute x6, waiting for transfers between devices: 0.02 us -> 2.48 us  [both_ways(): lax.ppermute(high, axis, [(i, (i + 1) % count) for i in range(count)])]
    concatenate x4 -> x2, other arithmetic: 2.04 us -> 0.34 us  [joined(): return jnp.concatenate([before, cells, after], axis=dim)]
    pallas_call x1, Pallas kernels: 4.03 us -> 2.34 us  [second_field(): pl.pallas_call(second_kernel, name='second_field', in_specs=[smem_spec()]...]
  transfers between devices with their start and end apart: 12 -> 13, of which waited for: 4 -> 6; matrix products, arithmetic and copies ran while one was open for 0% -> 1% of each run, Pallas kernels for 0% -> 7%
where the time goes in v5:
time: 129 us
  blocking collectives  49.2 us (38%)
  starting transfers between devices  43.1 us (33%)
  Pallas kernels  18 us (14%)
  waiting for transfers between devices  12.7 us (10%)
  local copies, waits for them, and re-layouts  3.75 us (3%)
    all_to_all x3, blocking collectives, exchange(): return lax.all_to_all(parts, axes, 0, 0)  49.2 us
    ppermute x6, starting transfers between devices, both_ways(): lax.ppermute(low, axis, [((i + 1) % count, i) for i in range(count)])  18.1 us
    ppermute x6, starting transfers between devices, both_ways(): lax.ppermute(high, axis, [(i, (i + 1) % count) for i in range(count)])  14.3 us
    all_to_all x1, starting transfers between devices, exchange(): return lax.all_to_all(parts, axes, 0, 0)  10.7 us
    all_to_all x1, waiting for transfers between devices, exchange(): return lax.all_to_all(parts, axes, 0, 0)  6.75 us
    pallas_call x1, Pallas kernels, inner_build(): pl.pallas_call(inner_build_kernel, name='inner_build', in_specs=[smem_spe...  6.56 us
    pallas_call x1, Pallas kernels, first_field(): pl.pallas_call(first_kernel, name='first_field', in_specs=[smem_spec()] +...  5.12 us
    ppermute x6, waiting for transfers between devices, both_ways(): lax.ppermute(low, axis, [((i + 1) % count, i) for i in range(count)])  3.43 us
  transfers between devices with their start and end apart: 13, of which 6 were waited for; matrix products, arithmetic and copies ran while one was open for 1% of the time, Pallas kernels for 7%

profile of v5, /device:TPU:1, one launch (start us, length us, event | category | flops | bytes accessed | tf_op | source)
XLA Modules:
  0.0 128.6 jit_solution(2238502439789960098)
XLA Ops:
  0.6 1.7 %prepare.1 = (f32[34,4,128]{2,1,0:T(4,128)}, f32[32,1,128]{2,1,0:T(1,128)}, f32[7,4,128]{2,1,0:T(4,128)}, s32[4,27]{1,0:T(4,128)}) custom-call(f32[3,4,128]{2,1,0:T(4,128)} %bitcast.33, f32[4,128]{1,0:T(4,128)} %bitcast.34, s32[4,128]{1,0:T(4,128)} %bitcast.35, f32[6,6,4,128]{3,2,1,0:T(4,128)} %bitcast.31, f32[6,4,128]{2,1,0:T(4,128)} %bitcast.32, ...), custom_call_target="tpu_custom_call" | custom-call | tf_op jit(solution)/shard_map/prepare/pallas_call | solution.py:343
  2.3 0.0 copy-start
  2.3 0.9 copy.26
  3.2 2.7 %collective-permute-start = (f32[34,1,2,2,128]{4,2,1,0,3:T(2,128)S(1)}, f32[34,1,2,2,128]{4,2,1,0,3:T(2,128)S(1)}, u32[]{:S(2)}, u32[]{:S(2)}) collective-permute-start(f32[34,1,2,2,128]{4,2,1,0,3:T(2,128)S(1)} %copy.26), channel_id=1, source_target_pairs={{0,32},{32,64},{64,96},{96,128},{128,160},{160,192},{192,224},{224... | collective-permute-start | bytes 208904 | tf_op jit(solution)/shard_map/ppermute | solution.py:566
  5.9 4.2 %collective-permute-start.1 = (f32[34,1,2,2,128]{4,2,1,0,3:T(2,128)S(1)}, f32[34,1,2,2,128]{4,2,1,0,3:T(2,128)S(1)}, u32[]{:S(2)}, u32[]{:S(2)}) collective-permute-start(f32[34,1,2,2,128]{4,2,1,0,3:T(2,128)S(1)} %copy.26), channel_id=1, source_target_pairs={{32,0},{64,32},{96,64},{128,96},{160,128},{192,160},{224,192},{256... | collective-permute-start | bytes 208904 | tf_op jit(solution)/shard_map/ppermute | solution.py:567
  10.1 0.7 collective-permute-done
  10.9 0.9 constant_dynamic-update-slice_fusion.1
  11.8 0.0 collective-permute-done.1
  11.9 0.2 fusion.2
  12.0 1.9 %collective-permute-start.2 = (f32[34,3,1,2,128]{4,2,1,0,3:T(1,128)S(1)}, f32[34,3,1,2,128]{4,2,1,0,3:T(1,128)S(1)}, u32[]{:S(2)}, u32[]{:S(2)}) collective-permute-start(f32[34,3,1,2,128]{4,2,1,0,3:T(1,128)S(1)} %get-tuple-element.48), channel_id=1, source_target_pairs={{0,8},{8,16},{16,24},{24,0},{1,9},{9,17},{17,25},{25,1},{2,10},{10... | collective-permute-start | bytes 313352 | tf_op jit(solution)/shard_map/ppermute | solution.py:566
  14.0 4.6 %collective-permute-start.3 = (f32[34,3,1,2,128]{4,2,1,0,3:T(1,128)S(1)}, f32[34,3,1,2,128]{4,2,1,0,3:T(1,128)S(1)}, u32[]{:S(2)}, u32[]{:S(2)}) collective-permute-start(f32[34,3,1,2,128]{4,2,1,0,3:T(1,128)S(1)} %get-tuple-element.49), channel_id=1, source_target_pairs={{8,0},{16,8},{24,16},{0,24},{9,1},{17,9},{25,17},{1,25},{10,2},{18... | collective-permute-start | bytes 313352 | tf_op jit(solution)/shard_map/ppermute | solution.py:567
  18.5 18.2 %all_to_all.20 = f32[32,1,128]{2,1,0:T(1,128)S(1)} all-to-all(f32[32,1,128]{2,1,0:T(1,128)} %get-tuple-element.23), channel_id=1, replica_groups=mesh['gx'=16,'gy'=4,'gz'=8] {'gy','gz'}, dimensions={0} | all-to-all | bytes 32768 | tf_op jit(solution)/shard_map/all_to_all | solution.py:592
  36.7 0.1 reduce_sum.27
  36.8 0.0 collective-permute-done.2
  36.8 0.0 collective-permute-done.3
  36.8 0.3 pad_maximum_fusion
  37.1 0.6 broadcast_in_dim.4
  37.7 2.2 %collective-permute-start.5 = (f32[34,3,4,1,128]{4,2,1,0,3:T(4,128)S(1)}, f32[34,3,4,1,128]{4,2,1,0,3:T(4,128)S(1)}, u32[]{:S(2)}, u32[]{:S(2)}) collective-permute-start(f32[34,3,4,1,128]{4,2,1,0,3:T(4,128)S(1)} %get-tuple-element.46), channel_id=1, source_target_pairs={{1,0},{2,1},{3,2},{4,3},{5,4},{6,5},{7,6},{0,7},{9,8},{10,9},{11,1... | collective-permute-start | bytes 626696 | tf_op jit(solution)/shard_map/ppermute | solution.py:567
  39.9 3.1 %collective-permute-start.4 = (f32[34,3,4,1,128]{4,2,1,0,3:T(4,128)S(1)}, f32[34,3,4,1,128]{4,2,1,0,3:T(4,128)S(1)}, u32[]{:S(2)}, u32[]{:S(2)}) collective-permute-start(f32[34,3,4,1,128]{4,2,1,0,3:T(4,128)S(1)} %get-tuple-element.47), channel_id=1, source_target_pairs={{0,1},{1,2},{2,3},{3,4},{4,5},{5,6},{6,7},{7,0},{8,9},{9,10},{10,1... | collective-permute-start | bytes 626696 | tf_op jit(solution)/shard_map/ppermute | solution.py:566
  43.0 10.7 %all-to-all-start.1 = ((f32[16,1,128]{2,1,0:T(1,128)}), f32[16,1,128]{2,1,0:T(1,128)S(1)}, u32[]{:S(2)}, u32[]{:S(2)}) async-start(f32[16,1,128]{2,1,0:T(1,128)} %broadcast_in_dim.4), calls=%async_computation.1 | async-start | bytes 16384 | tf_op jit(solution)/shard_map/all_to_all | solution.py:592
  53.7 0.2 copy.29
  53.9 6.8 %all-to-all-done.1.gram_ref = f32[16,1,128]{2,1,0:T(1,128)S(1)} async-done(((f32[16,1,128]{2,1,0:T(1,128)}), f32[16,1,128]{2,1,0:T(1,128)S(1)}, u32[]{:S(2)}, u32[]{:S(2)}) %all-to-all-start.1) | async-done | bytes 8224 | tf_op jit(solution)/shard_map/all_to_all | solution.py:592
  60.7 0.0 copy-start.1
  60.7 0.7 copy-done.1
  61.3 6.6 %inner_build.1 = (s32[128]{0:T(128)S(1)}, bf16[82,512,128]{2,1,0:T(8,128)(2,1)S(1)}, f32[6,4,128]{2,1,0:T(4,128)S(1)}, f32[4,96,128]{2,1,0:T(8,128)S(1)}, f32[4,24,128]{2,1,0:T(8,128)S(1)}) custom-call(s32[4,27]{1,0:T(4,128)S(1)} %copy-done.1, f32[16,1,128]{2,1,0:T(1,128)S(1)} %all-to-all-done.1.gram_ref, f32[34,24,128]{2,1,0:T(8,128)S(1)} %bitcast.21), custom_call_target="tpu_custom_call" | custom-call | flops 2000000000 | bytes 1000000 | tf_op jit(solution)/shard_map/inner_build/pallas_call | solution.py:433
  67.9 0.0 collective-permute-done.5
  67.9 0.0 collective-permute-done.4
  67.9 0.0 copy-done
  67.9 5.1 %first_field.1 = (f32[6,4,128]{2,1,0:T(4,128)S(1)}, s32[128]{0:T(128)S(1)}, f32[4,48,128]{2,1,0:T(8,128)S(1)}, bf16[39,512,128]{2,1,0:T(8,128)(2,1)S(1)}) custom-call(s32[4,27]{1,0:T(4,128)S(1)} %copy-done.1, f32[16,1,128]{2,1,0:T(1,128)S(1)} %all-to-all-done.1.gram_ref, f32[34,24,128]{2,1,0:T(8,128)S(1)} %bitcast.22, f32[408,128]{1,0:T(8,128)S(1)} %bitcast.28, ...), custom_call_target="tpu_custom_call" | custom-call | flops 2000000000 | bytes 1000000 | tf_op jit(solution)/shard_map/first_field/pallas_call | solution.py:480
  73.1 2.0 %collective-permute-start.6 = (f32[6,1,2,2,128]{4,2,1,0,3:T(2,128)S(1)}, f32[6,1,2,2,128]{4,2,1,0,3:T(2,128)S(1)}, u32[]{:S(2)}, u32[]{:S(2)}) collective-permute-start(f32[6,1,2,2,128]{4,2,1,0,3:T(2,128)S(1)} %copy.30), channel_id=1, source_target_pairs={{0,32},{32,64},{64,96},{96,128},{128,160},{160,192},{192,224},{224... | collective-permute-start | bytes 36872 | tf_op jit(solution)/shard_map/ppermute | solution.py:566
  75.1 0.0 collective-permute-start.7
  75.1 0.8 collective-permute-done.6
  75.9 2.6 %collective-permute-done.7 = f32[6,1,2,2,128]{4,2,1,0,3:T(2,128)S(1)} collective-permute-done((f32[6,1,2,2,128]{4,2,1,0,3:T(2,128)S(1)}, f32[6,1,2,2,128]{4,2,1,0,3:T(2,128)S(1)}, u32[]{:S(2)}, u32[]{:S(2)}) %collective-permute-start.7) | collective-permute-done | bytes 12320 | tf_op jit(solution)/shard_map/ppermute | solution.py:567
  78.5 2.0 %collective-permute-start.8 = (f32[6,3,1,2,128]{4,2,1,0,3:T(1,128)S(1)}, f32[6,3,1,2,128]{4,2,1,0,3:T(1,128)S(1)}, u32[]{:S(2)}, u32[]{:S(2)}) collective-permute-start(f32[6,3,1,2,128]{4,2,1,0,3:T(1,128)S(1)} %get-tuple-element.52), channel_id=1, source_target_pairs={{0,8},{8,16},{16,24},{24,0},{1,9},{9,17},{17,25},{25,1},{2,10},{10... | collective-permute-start | bytes 55304 | tf_op jit(solution)/shard_map/ppermute | solution.py:566
  80.5 4.5 %collective-permute-start.9 = (f32[6,3,1,2,128]{4,2,1,0,3:T(1,128)S(1)}, f32[6,3,1,2,128]{4,2,1,0,3:T(1,128)S(1)}, u32[]{:S(2)}, u32[]{:S(2)}) collective-permute-start(f32[6,3,1,2,128]{4,2,1,0,3:T(1,128)S(1)} %get-tuple-element.53), channel_id=1, source_target_pairs={{8,0},{16,8},{24,16},{0,24},{9,1},{17,9},{25,17},{1,25},{10,2},{18... | collective-permute-start | bytes 55304 | tf_op jit(solution)/shard_map/ppermute | solution.py:567
  85.0 0.0 collective-permute-done.8
  85.0 0.9 collective-permute-done.9
  85.9 0.1 pad_maximum_fusion.1
  86.0 2.6 %collective-permute-start.11 = (f32[6,3,4,1,128]{4,2,1,0,3:T(4,128)S(1)}, f32[6,3,4,1,128]{4,2,1,0,3:T(4,128)S(1)}, u32[]{:S(2)}, u32[]{:S(2)}) collective-permute-start(f32[6,3,4,1,128]{4,2,1,0,3:T(4,128)S(1)} %get-tuple-element.50), channel_id=1, source_target_pairs={{1,0},{2,1},{3,2},{4,3},{5,4},{6,5},{7,6},{0,7},{9,8},{10,9},{11,1... | collective-permute-start | bytes 110600 | tf_op jit(solution)/shard_map/ppermute | solution.py:567
  88.6 2.7 %collective-permute-start.10 = (f32[6,3,4,1,128]{4,2,1,0,3:T(4,128)S(1)}, f32[6,3,4,1,128]{4,2,1,0,3:T(4,128)S(1)}, u32[]{:S(2)}, u32[]{:S(2)}) collective-permute-start(f32[6,3,4,1,128]{4,2,1,0,3:T(4,128)S(1)} %get-tuple-element.51), channel_id=1, source_target_pairs={{0,1},{1,2},{2,3},{3,4},{4,5},{5,6},{6,7},{7,0},{8,9},{9,10},{10,1... | collective-permute-start | bytes 110600 | tf_op jit(solution)/shard_map/ppermute | solution.py:566
  91.3 2.3 %inner_apply.1 = (f32[4,96,128]{2,1,0:T(8,128)S(1)}, f32[4,24,128]{2,1,0:T(8,128)S(1)}) custom-call(s32[128]{0:T(128)S(1)} %get-tuple-element.34.list_ref, f32[4,48,128]{2,1,0:T(8,128)S(1)} %get-tuple-element.31.geo_ref, f32[6,24,128]{2,1,0:T(8,128)S(1)} %bitcast.19, bf16[82,512,128]{2,1,0:T(8,128)(2,1)S(1)} %get-tuple-element.35.pair_ref), custom_call_target="tpu_custom_call" | custom-call | flops 1000000000 | bytes 1000000 | tf_op jit(solution)/shard_map/inner_apply/pallas_call | solution.py:509
  93.6 0.0 collective-permute-done.11
  93.6 0.9 collective-permute-done.10
  94.5 2.3 %second_field.1 = (f32[6,4,128]{2,1,0:T(4,128)}, f32[32,2,128]{2,1,0:T(2,128)S(1)}) custom-call(s32[128]{0:T(128)S(1)} %get-tuple-element.30.list_ref, f32[4,48,128]{2,1,0:T(8,128)S(1)} %get-tuple-element.31.geo_ref, f32[6,24,128]{2,1,0:T(8,128)S(1)} %bitcast.20, f32[72,128]{1,0:T(8,128)S(1)} %bitcast.26, f32[72,128]{1,0:T(8,128)S(1)} %bitcast.25, ...), custom_call_target="tpu_custom_call" | custom-call | flops 1000000000 | bytes 1000000 | tf_op jit(solution)/shard_map/second_field/pallas_call | solution.py:549
  96.9 16.2 %all_to_all.21 = f32[32,2,128]{2,1,0:T(2,128)S(1)} all-to-all(f32[32,2,128]{2,1,0:T(2,128)S(1)} %get-tuple-element.39), channel_id=1, replica_groups=mesh['gx'=16,'gy'=4,'gz'=8] {'gy','gz'}, dimensions={0} | all-to-all | bytes 65536 | tf_op jit(solution)/shard_map/all_to_all | solution.py:592
  113.1 14.9 %all_to_all.22 = f32[16,2,128]{2,1,0:T(2,128)S(1)} all-to-all(f32[16,2,128]{2,1,0:T(2,128)S(1)} %broadcast_in_dim.5), channel_id=1, replica_groups=mesh['gx'=16,'gy'=4,'gz'=8] {'gx'}, dimensions={0} | all-to-all | bytes 32768 | tf_op jit(solution)/shard_map/all_to_all | solution.py:592
  128.0 0.5 fusion
  (13 shorter events, 0.3 us)
Async XLA Ops:
  2.3 65.6 %copy-start = (f32[7,4,128]{2,1,0:T(4,128)S(1)}, f32[7,4,128]{2,1,0:T(4,128)}, u32[]{:S(2)}) copy-start(f32[7,4,128]{2,1,0:T(4,128)} %get-tuple-element.26.mine_ref) | copy-start | bytes 43012
  3.2 7.6 %collective-permute-start = (f32[34,1,2,2,128]{4,2,1,0,3:T(2,128)S(1)}, f32[34,1,2,2,128]{4,2,1,0,3:T(2,128)S(1)}, u32[]{:S(2)}, u32[]{:S(2)}) collective-permute-start(f32[34,1,2,2,128]{4,2,1,0,3:T(2,128)S(1)} %copy.26), channel_id=1, source_target_pairs={{0,32},{32,64},{64,96},{96,128},{128,160},{160,192},{192,224},{224... | collective-permute-start | bytes 208904 | tf_op jit(solution)/shard_map/ppermute | solution.py:566
  5.9 5.9 %collective-permute-start.1 = (f32[34,1,2,2,128]{4,2,1,0,3:T(2,128)S(1)}, f32[34,1,2,2,128]{4,2,1,0,3:T(2,128)S(1)}, u32[]{:S(2)}, u32[]{:S(2)}) collective-permute-start(f32[34,1,2,2,128]{4,2,1,0,3:T(2,128)S(1)} %copy.26), channel_id=1, source_target_pairs={{32,0},{64,32},{96,64},{128,96},{160,128},{192,160},{224,192},{256... | collective-permute-start | bytes 208904 | tf_op jit(solution)/shard_map/ppermute | solution.py:567
  12.0 24.7 %collective-permute-start.2 = (f32[34,3,1,2,128]{4,2,1,0,3:T(1,128)S(1)}, f32[34,3,1,2,128]{4,2,1,0,3:T(1,128)S(1)}, u32[]{:S(2)}, u32[]{:S(2)}) collective-permute-start(f32[34,3,1,2,128]{4,2,1,0,3:T(1,128)S(1)} %get-tuple-element.48), channel_id=1, source_target_pairs={{0,8},{8,16},{16,24},{24,0},{1,9},{9,17},{17,25},{25,1},{2,10},{10... | collective-permute-start | bytes 313352 | tf_op jit(solution)/shard_map/ppermute | solution.py:566
  14.0 22.8 %collective-permute-start.3 = (f32[34,3,1,2,128]{4,2,1,0,3:T(1,128)S(1)}, f32[34,3,1,2,128]{4,2,1,0,3:T(1,128)S(1)}, u32[]{:S(2)}, u32[]{:S(2)}) collective-permute-start(f32[34,3,1,2,128]{4,2,1,0,3:T(1,128)S(1)} %get-tuple-element.49), channel_id=1, source_target_pairs={{8,0},{16,8},{24,16},{0,24},{9,1},{17,9},{25,17},{1,25},{10,2},{18... | collective-permute-start | bytes 313352 | tf_op jit(solution)/shard_map/ppermute | solution.py:567
  37.7 30.2 %collective-permute-start.5 = (f32[34,3,4,1,128]{4,2,1,0,3:T(4,128)S(1)}, f32[34,3,4,1,128]{4,2,1,0,3:T(4,128)S(1)}, u32[]{:S(2)}, u32[]{:S(2)}) collective-permute-start(f32[34,3,4,1,128]{4,2,1,0,3:T(4,128)S(1)} %get-tuple-element.46), channel_id=1, source_target_pairs={{1,0},{2,1},{3,2},{4,3},{5,4},{6,5},{7,6},{0,7},{9,8},{10,9},{11,1... | collective-permute-start | bytes 626696 | tf_op jit(solution)/shard_map/ppermute | solution.py:567
  39.9 28.0 %collective-permute-start.4 = (f32[34,3,4,1,128]{4,2,1,0,3:T(4,128)S(1)}, f32[34,3,4,1,128]{4,2,1,0,3:T(4,128)S(1)}, u32[]{:S(2)}, u32[]{:S(2)}) collective-permute-start(f32[34,3,4,1,128]{4,2,1,0,3:T(4,128)S(1)} %get-tuple-element.47), channel_id=1, source_target_pairs={{0,1},{1,2},{2,3},{3,4},{4,5},{5,6},{6,7},{7,0},{8,9},{9,10},{10,1... | collective-permute-start | bytes 626696 | tf_op jit(solution)/shard_map/ppermute | solution.py:566
  43.0 17.7 %all-to-all-start.1 = ((f32[16,1,128]{2,1,0:T(1,128)}), f32[16,1,128]{2,1,0:T(1,128)S(1)}, u32[]{:S(2)}, u32[]{:S(2)}) async-start(f32[16,1,128]{2,1,0:T(1,128)} %broadcast_in_dim.4), calls=%async_computation.1 | async-start | bytes 16384 | tf_op jit(solution)/shard_map/all_to_all | solution.py:592
  60.7 0.7 copy-start.1
  73.1 2.8 %collective-permute-start.6 = (f32[6,1,2,2,128]{4,2,1,0,3:T(2,128)S(1)}, f32[6,1,2,2,128]{4,2,1,0,3:T(2,128)S(1)}, u32[]{:S(2)}, u32[]{:S(2)}) collective-permute-start(f32[6,1,2,2,128]{4,2,1,0,3:T(2,128)S(1)} %copy.30), channel_id=1, source_target_pairs={{0,32},{32,64},{64,96},{96,128},{128,160},{160,192},{192,224},{224... | collective-permute-start | bytes 36872 | tf_op jit(solution)/shard_map/ppermute | solution.py:566
  75.1 3.4 %collective-permute-start.7 = (f32[6,1,2,2,128]{4,2,1,0,3:T(2,128)S(1)}, f32[6,1,2,2,128]{4,2,1,0,3:T(2,128)S(1)}, u32[]{:S(2)}, u32[]{:S(2)}) collective-permute-start(f32[6,1,2,2,128]{4,2,1,0,3:T(2,128)S(1)} %copy.30), channel_id=1, source_target_pairs={{32,0},{64,32},{96,64},{128,96},{160,128},{192,160},{224,192},{256... | collective-permute-start | bytes 36872 | tf_op jit(solution)/shard_map/ppermute | solution.py:567
  78.5 6.5 %collective-permute-start.8 = (f32[6,3,1,2,128]{4,2,1,0,3:T(1,128)S(1)}, f32[6,3,1,2,128]{4,2,1,0,3:T(1,128)S(1)}, u32[]{:S(2)}, u32[]{:S(2)}) collective-permute-start(f32[6,3,1,2,128]{4,2,1,0,3:T(1,128)S(1)} %get-tuple-element.52), channel_id=1, source_target_pairs={{0,8},{8,16},{16,24},{24,0},{1,9},{9,17},{17,25},{25,1},{2,10},{10... | collective-permute-start | bytes 55304 | tf_op jit(solution)/shard_map/ppermute | solution.py:566
  80.5 5.4 %collective-permute-start.9 = (f32[6,3,1,2,128]{4,2,1,0,3:T(1,128)S(1)}, f32[6,3,1,2,128]{4,2,1,0,3:T(1,128)S(1)}, u32[]{:S(2)}, u32[]{:S(2)}) collective-permute-start(f32[6,3,1,2,128]{4,2,1,0,3:T(1,128)S(1)} %get-tuple-element.53), channel_id=1, source_target_pairs={{8,0},{16,8},{24,16},{0,24},{9,1},{17,9},{25,17},{1,25},{10,2},{18... | collective-permute-start | bytes 55304 | tf_op jit(solution)/shard_map/ppermute | solution.py:567
  86.0 7.6 %collective-permute-start.11 = (f32[6,3,4,1,128]{4,2,1,0,3:T(4,128)S(1)}, f32[6,3,4,1,128]{4,2,1,0,3:T(4,128)S(1)}, u32[]{:S(2)}, u32[]{:S(2)}) collective-permute-start(f32[6,3,4,1,128]{4,2,1,0,3:T(4,128)S(1)} %get-tuple-element.50), channel_id=1, source_target_pairs={{1,0},{2,1},{3,2},{4,3},{5,4},{6,5},{7,6},{0,7},{9,8},{10,9},{11,1... | collective-permute-start | bytes 110600 | tf_op jit(solution)/shard_map/ppermute | solution.py:567
  88.6 5.9 %collective-permute-start.10 = (f32[6,3,4,1,128]{4,2,1,0,3:T(4,128)S(1)}, f32[6,3,4,1,128]{4,2,1,0,3:T(4,128)S(1)}, u32[]{:S(2)}, u32[]{:S(2)}) collective-permute-start(f32[6,3,4,1,128]{4,2,1,0,3:T(4,128)S(1)} %get-tuple-element.51), channel_id=1, source_target_pairs={{0,1},{1,2},{2,3},{3,4},{4,5},{5,6},{6,7},{7,0},{8,9},{9,10},{10,1... | collective-permute-start | bytes 110600 | tf_op jit(solution)/shard_map/ppermute | solution.py:566

commit v6 on v5

--- a/solution.py
+++ b/solution.py
@@ -22,7 +22,9 @@
 BATCH = 13
 LIST = 128
 COUNT_AT = LIST - 1
-ROWS = 34
+ROWS = 36
+LATER = 4
+MASK_ROW = 34
 LAYER = NX * NY
 INNER = 2 * LAYER
 GRAM = tuple((a, b) for a in range(6) for b in range(a + 1))
@@ -33,11 +35,7 @@
     y = tile // 2 + offset // 3 % 3
     z = tile % 2 + offset % 3
     column = x * NY + y
-    if z == 0:
-        return INNER + column
-    if z == NZ - 1:
-        return INNER + LAYER + column
-    return column * 2 + z - 1
+    return (2, 0, 1, 3)[z] * LAYER + column
 
 
 def candidates(inner):
@@ -62,11 +60,9 @@
 def positions(geo, first):
     shape = geo[0].shape
     tile = lax.broadcasted_iota(jnp.int32, shape, 0) + first
-    own = tile < INNER
-    edge = tile - INNER
-    above = edge >= LAYER
-    column = jnp.where(own, tile // 2, jnp.where(above, edge - LAYER, edge))
-    layer = jnp.where(own, tile % 2 + 1, jnp.where(above, NZ - 1, 0))
+    second = tile - first >= LAYER
+    column = tile - first - jnp.where(second, LAYER, 0)
+    layer = jnp.where(second, 2, 1) if first == 0 else jnp.where(second, NZ - 1, 0)
     x = (column // NY).astype(jnp.float32)
     y = (column % NY).astype(jnp.float32)
     z = layer.astype(jnp.float32)
@@ -118,12 +114,24 @@
     q_ref[last : last + TERMS, :] = q_ref[0:TERMS, :]
 
 
+def read_mask(own_ref, mask_ref, sems):
+    copies = []
+    for t in range(OWN):
+        row = MASK_ROW * LAYER + NY + 1 + t // 2
+        copy = pltpu.make_async_copy(
+            own_ref.at[t % 2, pl.ds(row, 1), :], mask_ref.at[pl.ds(t, 1), :], sems.at[t]
+        )
+        copy.start()
+        copies.append(copy)
+    return copies
+
+
 def list_pairs(mask_ref, list_ref, inner):
     first = 0 if inner else INNER
     count = jnp.int32(0)
     for t, k in candidates(inner):
         list_ref[count] = (source_tile(t, k) - first) * OWN + t
-        count = count + (mask_ref[t, k] != 0).astype(jnp.int32)
+        count = count + (mask_ref[t, k] != 0.0).astype(jnp.int32)
     for extra in range(BATCH):
         list_ref[count + extra] = INNER * OWN
     list_ref[COUNT_AT] = count
@@ -303,23 +311,32 @@
     return result
 
 
+def store_layers(ref, rows, row, value):
+    for t in range(OWN):
+        at = ((t % 2) * rows + row) * 2 + t // 2
+        ref[at : at + 1, :] = value[t : t + 1]
+
+
 def prepare_kernel(
     fractions_ref, polar_ref, occupancy_ref, history_ref, perm_ref, mask_ref,
-    stacked_ref, gram_ref, own_ref, mask_copy_ref,
+    stacked_ref, gram_ref, own_ref,
 ):
     filled = occupancy_ref[...].astype(jnp.float32)
-    scaled = RELAXATION * filled * polar_ref[...]
-    own_ref[0] = scaled
+    own_ref[0] = RELAXATION * filled * polar_ref[...]
     for c in range(6):
         own_ref[1 + c] = perm_ref[c]
-    mask_copy_ref[...] = mask_ref[...]
     masked = [[history_ref[h, c] * filled for c in range(6)] for h in range(6)]
     for a in range(3):
-        stacked_ref[a] = fractions_ref[a]
-    stacked_ref[3] = polar_ref[...]
+        store_layers(stacked_ref, ROWS, a, fractions_ref[a])
+    store_layers(stacked_ref, ROWS, 3, polar_ref[...])
     for h in range(1, 6):
         for c in range(6):
-            stacked_ref[4 + 6 * (h - 1) + c] = masked[h][c]
+            store_layers(stacked_ref, ROWS, LATER + 6 * (h - 1) + c, masked[h][c])
+    allowed = jnp.concatenate(
+        [mask_ref[...].astype(jnp.float32), jnp.zeros((OWN, SLOTS - OFFSETS), jnp.float32)], axis=1
+    )
+    store_layers(stacked_ref, ROWS, MASK_ROW, allowed)
+    store_layers(stacked_ref, ROWS, ROWS - 1, jnp.zeros((OWN, SLOTS), jnp.float32))
     lane = lax.broadcasted_iota(jnp.int32, (1, SLOTS), 1)
     row = jnp.zeros((1, SLOTS), jnp.float32)
     for index, (a, b) in enumerate(GRAM):
@@ -344,12 +361,11 @@
         prepare_kernel,
         name="prepare",
         in_specs=[vmem_spec()] * 6,
-        out_specs=[vmem_spec()] * 4,
+        out_specs=[vmem_spec()] * 3,
         out_shape=[
-            jax.ShapeDtypeStruct((ROWS, OWN, SLOTS), jnp.float32),
+            jax.ShapeDtypeStruct((ROWS * OWN, SLOTS), jnp.float32),
             jax.ShapeDtypeStruct((copies, 1, SLOTS), jnp.float32),
             jax.ShapeDtypeStruct((7, OWN, SLOTS), jnp.float32),
-            jax.ShapeDtypeStruct((OWN, OFFSETS), jnp.int32),
         ],
     )(fractions, polarizability, occupancy, history, perm, mask)
 
@@ -392,6 +408,11 @@
     return jnp.concatenate([before_ref[rows, :], after_ref[rows, :]], axis=0)
 
 
+def own_rows_of(own_ref, row):
+    rows = pl.ds(row * LAYER, LAYER)
+    return jnp.concatenate([own_ref[0, rows, :], own_ref[1, rows, :]], axis=0)
+
+
 def coefficients(gram_ref):
     total = jnp.sum(gram_ref[...], axis=0)
     return solve({ab: total[0:1, i : i + 1] for i, ab in enumerate(GRAM)})
@@ -408,14 +429,15 @@
 
 
 def inner_build_kernel(
-    mask_ref, gram_ref, own_ref,
+    gram_ref, own_ref,
     list_ref, pair_ref, moment_ref, sum_a, sum_b,
-    q_ref, p_ref, a_ref, b_ref,
+    mask_ref, q_ref, p_ref, a_ref, b_ref, sems,
 ):
-    geo = [own_ref[a] for a in range(4)]
+    copies = read_mask(own_ref, mask_ref, sems)
+    geo = [own_rows_of(own_ref, a) for a in range(4)]
     prepare_distances(geo, geo, 0, q_ref, p_ref)
-    count = list_pairs(mask_ref, list_ref, True)
-    moment = predict(coefficients(gram_ref), [own_ref[row] for row in range(4, ROWS)])
+    later = [own_rows_of(own_ref, row) for row in range(LATER, MASK_ROW)]
+    moment = predict(coefficients(gram_ref), later)
     prepare_moments(geo, 0, moment, a_ref, b_ref)
     for c in range(6):
         moment_ref[c] = own_part(moment[c])
@@ -424,16 +446,23 @@
     )
     for slot in range(OWN):
         build(slot, OWN_TILES[slot], slot, keep, pair_ref, q_ref, p_ref)
+    for copy in copies:
+        copy.wait()
+    count = list_pairs(mask_ref, list_ref, True)
     build_all(list_ref, count, OWN, pair_ref, q_ref, p_ref)
     apply_selves(pair_ref, a_ref, b_ref, sum_a, sum_b)
     apply_all(list_ref, count, OWN, pair_ref, a_ref, b_ref, sum_a, sum_b)
 
 
-def inner_build(mask, gram, own):
+MASK_SCRATCH = [pltpu.SMEM((OWN, SLOTS), jnp.float32)]
+MASK_SEMS = [pltpu.SemaphoreType.DMA((OWN,))]
+
+
+def inner_build(gram, own):
     return pl.pallas_call(
         inner_build_kernel,
         name="inner_build",
-        in_specs=[smem_spec()] + [vmem_spec()] * 2,
+        in_specs=[vmem_spec()] * 2,
         out_specs=[smem_spec()] + [vmem_spec()] * 4,
         out_shape=[
             jax.ShapeDtypeStruct((LIST,), jnp.int32),
@@ -441,66 +470,70 @@
             jax.ShapeDtypeStruct((6, OWN, SLOTS), jnp.float32),
         ]
         + SUMS,
-        scratch_shapes=DISTANCE_ROWS + MOMENT_ROWS,
+        scratch_shapes=MASK_SCRATCH + DISTANCE_ROWS + MOMENT_ROWS + MASK_SEMS,
         compiler_params=PARAMS,
         cost_estimate=cost(2_000_000_000),
-    )(mask, gram, own)
+    )(gram, own)
 
 
 def first_kernel(
-    mask_ref, gram_ref, own_ref, before_ref, after_ref, mine_ref, moment_ref, start_a, start_b,
+    gram_ref, own_ref, before_ref, after_ref, mine_ref, moment_ref, start_a, start_b,
     out_ref, list_ref, geo_ref, pair_ref,
-    q_ref, p_ref, a_ref, b_ref, sum_a, sum_b,
+    mask_ref, q_ref, p_ref, a_ref, b_ref, sum_a, sum_b, sems,
 ):
-    own_geo = [own_ref[a] for a in range(4)]
+    copies = read_mask(own_ref, mask_ref, sems)
+    own_geo = [own_rows_of(own_ref, a) for a in range(4)]
     edge_geo = [edge_rows(before_ref, after_ref, a) for a in range(4)]
     for a in range(4):
         geo_ref[a, 0:INNER, :] = own_geo[a]
         geo_ref[a, INNER:TILES, :] = edge_geo[a]
     prepare_distances(own_geo, edge_geo, INNER, q_ref, p_ref)
-    count = list_pairs(mask_ref, list_ref, False)
     sum_a[...] = start_a[...]
     sum_b[...] = start_b[...]
     moment = predict(
         coefficients(gram_ref),
-        [edge_rows(before_ref, after_ref, row) for row in range(4, ROWS)],
+        [edge_rows(before_ref, after_ref, row) for row in range(LATER, MASK_ROW)],
     )
     prepare_moments(edge_geo, INNER, moment, a_ref, b_ref)
+    for copy in copies:
+        copy.wait()
+    count = list_pairs(mask_ref, list_ref, False)
     build_all(list_ref, count, 0, pair_ref, q_ref, p_ref)
     apply_all(list_ref, count, 0, pair_ref, a_ref, b_ref, sum_a, sum_b)
 
     fields = field_of(own_geo, sum_a, sum_b)
     for c in range(6):
-        out_ref[c] = (1.0 - RELAXATION) * moment_ref[c] + mine_ref[0] * (
-            mine_ref[1 + c] + fields[c]
-        )
-
-
-def first_field(mask, gram, own, before, after, mine, moment, sums):
+        dipole = (1.0 - RELAXATION) * moment_ref[c] + mine_ref[0] * (mine_ref[1 + c] + fields[c])
+        store_layers(out_ref, 6, c, dipole)
+
+
+def first_field(gram, own, before, after, mine, moment, sums):
     return pl.pallas_call(
         first_kernel,
         name="first_field",
-        in_specs=[smem_spec()] + [vmem_spec()] * 8,
+        in_specs=[vmem_spec()] * 8,
         out_specs=[vmem_spec(), smem_spec(), vmem_spec(), vmem_spec()],
         out_shape=[
-            jax.ShapeDtypeStruct((6, OWN, SLOTS), jnp.float32),
+            jax.ShapeDtypeStruct((6 * OWN, SLOTS), jnp.float32),
             jax.ShapeDtypeStruct((LIST,), jnp.int32),
             jax.ShapeDtypeStruct((4, TILES, SLOTS), jnp.float32),
             pair_shape(False),
         ],
-        scratch_shapes=DISTANCE_ROWS
+        scratch_shapes=MASK_SCRATCH
+        + DISTANCE_ROWS
         + MOMENT_ROWS
-        + [pltpu.VMEM(part.shape, part.dtype) for part in SUMS],
+        + [pltpu.VMEM(part.shape, part.dtype) for part in SUMS]
+        + MASK_SEMS,
         compiler_params=PARAMS,
         cost_estimate=cost(2_000_000_000),
-    )(mask, gram, own, before, after, mine, moment, *sums)
+    )(gram, own, before, after, mine, moment, *sums)
 
 
 def inner_apply_kernel(
     list_ref, geo_ref, own_ref, pair_ref, sum_a, sum_b, a_ref, b_ref
 ):
     geo = [geo_ref[a, 0:INNER, :] for a in range(4)]
-    prepare_moments(geo, 0, [own_ref[c] for c in range(6)], a_ref, b_ref)
+    prepare_moments(geo, 0, [own_rows_of(own_ref, c) for c in range(6)], a_ref, b_ref)
     apply_selves(pair_ref, a_ref, b_ref, sum_a, sum_b)
     apply_all(list_ref, list_ref[COUNT_AT], OWN, pair_ref, a_ref, b_ref, sum_a, sum_b)
 
@@ -533,7 +566,7 @@
     moved = jnp.zeros((OWN, SLOTS), jnp.float32)
     size = jnp.zeros((OWN, SLOTS), jnp.float32)
     for c in range(6):
-        old = own_part(own_ref[c])
+        old = own_part(own_rows_of(own_ref, c))
         new = (1.0 - RELAXATION) * old + mine_ref[0] * (mine_ref[1 + c] + fields[c])
         out_ref[c] = new
         moved = moved + (new - old) * (new - old)
@@ -577,14 +610,14 @@
 
 
 def z_layers(cells):
-    rows = cells.shape[0]
-    low = lax.slice_in_dim(cells, 0, 1, axis=3)
-    high = lax.slice_in_dim(cells, 1, 2, axis=3)
+    rows = cells.shape[1] * LAYER
+    low = lax.slice_in_dim(cells, 0, 1, axis=0)
+    high = lax.slice_in_dim(cells, 1, 2, axis=0)
     before, after = both_ways(low, high, "gz")
     return (
-        cells.reshape(rows, INNER, SLOTS),
-        before.reshape(rows * LAYER, SLOTS),
-        after.reshape(rows * LAYER, SLOTS),
+        cells.reshape(2, rows, SLOTS),
+        before.reshape(rows, SLOTS),
+        after.reshape(rows, SLOTS),
     )
 
 
@@ -595,7 +628,7 @@
 def device_step(fractions, polarizability, occupancy, pair_mask, perm_field, history):
     plane = lax.axis_size("gy") * lax.axis_size("gz")
     line = lax.axis_size("gx")
-    stacked, gram, mine, mask = prepare(
+    stacked, gram, mine = prepare(
         fractions.reshape(3, OWN, SLOTS),
         polarizability.reshape(OWN, SLOTS),
         occupancy.reshape(OWN, SLOTS),
@@ -605,18 +638,17 @@
         plane,
     )
     gram = exchange(gram, ("gy", "gz"))
-    cells = joined(stacked.reshape(ROWS, 1, 2, 2, SLOTS), "gx", 1)
-    cells = joined(cells, "gy", 2)
+    cells = joined(stacked.reshape(2, ROWS, 1, 2, SLOTS), "gx", 2)
+    cells = joined(cells, "gy", 3)
     gram = sum_parts(gram, line)
-    cells, gram = lax.optimization_barrier((cells, gram))
     gram = exchange(gram, "gx")
     own, before, after = z_layers(cells)
-    inner_list, inner_pairs, moment, *sums = inner_build(mask, gram, own)
+    inner_list, inner_pairs, moment, *sums = inner_build(gram, own)
     dipoles, outer_list, geo, outer_pairs = first_field(
-        mask, gram, own, before, after, mine, moment, sums
-    )
-    cells = joined(dipoles.reshape(6, 1, 2, 2, SLOTS), "gx", 1)
-    cells = joined(cells, "gy", 2)
+        gram, own, before, after, mine, moment, sums
+    )
+    cells = joined(dipoles.reshape(2, 6, 1, 2, SLOTS), "gx", 2)
+    cells = joined(cells, "gy", 3)
     own, before, after = z_layers(cells)
     sums = inner_apply(inner_list, geo, own, inner_pairs)
     induced, sizes = second_field(

time: 129 us -> 123 us (0.953)
  waiting for transfers between devices: 12.7 us -> 7.06 us
  local copies, waits for them, and re-layouts: 3.75 us -> 0.99 us
  other arithmetic: 0.99 us -> 2.89 us
    ppermute x6, starting transfers between devices: 18.1 us -> 25 us  [both_ways(): lax.ppermute(low, axis, [((i + 1) % count, i) for i in range(count)])]
    all_to_all x1, waiting for transfers between devices: 6.75 us -> 1.11 us  [exchange(): return lax.all_to_all(parts, axes, 0, 0)]
    ppermute x6, starting transfers between devices: 14.3 us -> 9.13 us  [both_ways(): lax.ppermute(high, axis, [(i, (i + 1) % count) for i in range(count)])]
    all_to_all x1, starting transfers between devices: 10.7 us -> 8.49 us  [exchange(): return lax.all_to_all(parts, axes, 0, 0)]
    concatenate x2 -> x4, other arithmetic: 0.34 us -> 2.24 us  [joined(): return jnp.concatenate([before, cells, after], axis=dim)]
where the time goes in v6:
time: 123 us; the launch traced here: 122 us
  blocking collectives  49.8 us (40%)
  starting transfers between devices  42.6 us (35%)
  Pallas kernels  18 us (15%)
  waiting for transfers between devices  7.06 us (6%)
  other arithmetic  2.89 us (2%)
    all_to_all x3, blocking collectives, exchange(): return lax.all_to_all(parts, axes, 0, 0)  49.8 us
    ppermute x6, starting transfers between devices, both_ways(): lax.ppermute(low, axis, [((i + 1) % count, i) for i in range(count)])  25 us
    ppermute x6, starting transfers between devices, both_ways(): lax.ppermute(high, axis, [(i, (i + 1) % count) for i in range(count)])  9.13 us
    all_to_all x1, starting transfers between devices, exchange(): return lax.all_to_all(parts, axes, 0, 0)  8.49 us
    pallas_call x1, Pallas kernels, inner_build(): pl.pallas_call(inner_build_kernel, name='inner_build', in_specs=[vmem_spe...  6.62 us
    pallas_call x1, Pallas kernels, first_field(): pl.pallas_call(first_kernel, name='first_field', in_specs=[vmem_spec()] *...  5.1 us
    ppermute x6, waiting for transfers between devices, both_ways(): lax.ppermute(low, axis, [((i + 1) % count, i) for i in range(count)])  3.68 us
  transfers between devices with their start and end apart: 13, of which 6 were waited for; matrix products, arithmetic and copies ran while one was open for 1% of the time, Pallas kernels for 7%

profile of v6, /device:TPU:1, one launch (start us, length us, event | category | flops | bytes accessed | tf_op | source)
XLA Modules:
  0.0 122.3 jit_solution(15966575795015664005)
XLA Ops:
  0.6 1.7 %prepare.1 = (f32[144,128]{1,0:T(8,128)}, f32[32,1,128]{2,1,0:T(1,128)}, f32[7,4,128]{2,1,0:T(4,128)}) custom-call(f32[3,4,128]{2,1,0:T(4,128)} %bitcast.41, f32[4,128]{1,0:T(4,128)} %bitcast.42, s32[4,128]{1,0:T(4,128)} %bitcast.43, f32[6,6,4,128]{3,2,1,0:T(4,128)} %bitcast.39, f32[6,4,128]{2,1,0:T(4,128)} %bitcast.40, s32[4,27]{1,0:T(4,128)} %bitcast.44), custom_call_target="tpu_custom_call" | custom-call | tf_op jit(solution)/shard_map/prepare/pallas_call | solution.py:360
  2.3 6.8 %collective-permute-start.1 = (f32[2,36,1,2,128]{4,3,2,1,0:T(2,128)}, f32[2,36,1,2,128]{4,3,2,1,0:T(2,128)S(1)}, u32[]{:S(2)}, u32[]{:S(2)}) collective-permute-start(f32[2,36,1,2,128]{4,3,2,1,0:T(2,128)} %bitcast.35), channel_id=1, source_target_pairs={{32,0},{64,32},{96,64},{128,96},{160,128},{192,160},{224,192},{256... | collective-permute-start | bytes 221192 | tf_op jit(solution)/shard_map/ppermute | solution.py:600
  9.1 0.0 collective-permute-start
  9.1 1.1 collective-permute-done.1
  10.3 0.6 collective-permute-done
  10.9 1.0 pad_maximum_fusion.1
  11.8 0.2 fusion.2
  12.0 1.9 %collective-permute-start.2 = (f32[2,36,3,1,128]{4,3,2,1,0:T(1,128)S(1)}, f32[2,36,3,1,128]{4,3,2,1,0:T(1,128)S(1)}, u32[]{:S(2)}, u32[]{:S(2)}) collective-permute-start(f32[2,36,3,1,128]{4,3,2,1,0:T(1,128)S(1)} %get-tuple-element.42), channel_id=1, source_target_pairs={{0,8},{8,16},{16,24},{24,0},{1,9},{9,17},{17,25},{25,1},{2,10},{10... | collective-permute-start | bytes 331784 | tf_op jit(solution)/shard_map/ppermute | solution.py:599
  14.0 4.6 %collective-permute-start.3 = (f32[2,36,3,1,128]{4,3,2,1,0:T(1,128)S(1)}, f32[2,36,3,1,128]{4,3,2,1,0:T(1,128)S(1)}, u32[]{:S(2)}, u32[]{:S(2)}) collective-permute-start(f32[2,36,3,1,128]{4,3,2,1,0:T(1,128)S(1)} %get-tuple-element.43), channel_id=1, source_target_pairs={{8,0},{16,8},{24,16},{0,24},{9,1},{17,9},{25,17},{1,25},{10,2},{18... | collective-permute-start | bytes 331784 | tf_op jit(solution)/shard_map/ppermute | solution.py:600
  18.5 8.5 %all-to-all-start = ((f32[32,1,128]{2,1,0:T(1,128)}), f32[32,1,128]{2,1,0:T(1,128)S(1)}, u32[]{:S(2)}, u32[]{:S(2)}) async-start(f32[32,1,128]{2,1,0:T(1,128)} %get-tuple-element.18), calls=%async_computation | async-start | bytes 32768 | tf_op jit(solution)/shard_map/all_to_all | solution.py:625
  27.0 0.0 collective-permute-done.2
  27.0 0.0 collective-permute-done.3
  27.1 1.2 pad_maximum_fusion
  28.3 4.4 %collective-permute-start.5 = (f32[1,36,3,4,128]{4,3,2,1,0:T(4,128)S(1)}, f32[1,36,3,4,128]{4,3,2,1,0:T(4,128)S(1)}, u32[]{:S(2)}, u32[]{:S(2)}) collective-permute-start(f32[1,36,3,4,128]{4,3,2,1,0:T(4,128)S(1)} %get-tuple-element.40), channel_id=1, source_target_pairs={{1,0},{2,1},{3,2},{4,3},{5,4},{6,5},{7,6},{0,7},{9,8},{10,9},{11,1... | collective-permute-start | bytes 663560 | tf_op jit(solution)/shard_map/ppermute | solution.py:600
  32.7 1.9 %collective-permute-start.4 = (f32[1,36,3,4,128]{4,3,2,1,0:T(4,128)S(1)}, f32[1,36,3,4,128]{4,3,2,1,0:T(4,128)S(1)}, u32[]{:S(2)}, u32[]{:S(2)}) collective-permute-start(f32[1,36,3,4,128]{4,3,2,1,0:T(4,128)S(1)} %get-tuple-element.41), channel_id=1, source_target_pairs={{0,1},{1,2},{2,3},{3,4},{4,5},{5,6},{6,7},{7,0},{8,9},{9,10},{10,1... | collective-permute-start | bytes 663560 | tf_op jit(solution)/shard_map/ppermute | solution.py:599
  34.6 1.1 all-to-all-done
  35.7 0.1 reduce_sum.27
  35.8 17.3 %all_to_all.20.gram_ref = f32[16,1,128]{2,1,0:T(1,128)S(1)} all-to-all(f32[16,1,128]{2,1,0:T(1,128)S(1)} %broadcast_in_dim.4), channel_id=1, replica_groups=mesh['gx'=16,'gy'=4,'gz'=8] {'gx'}, dimensions={0} | all-to-all | bytes 16384 | tf_op jit(solution)/shard_map/all_to_all | solution.py:625
  53.0 0.0 copy-start.1
  53.0 6.6 %inner_build.1 = (s32[128]{0:T(128)S(1)}, bf16[82,512,128]{2,1,0:T(8,128)(2,1)S(1)}, f32[6,4,128]{2,1,0:T(4,128)S(1)}, f32[4,96,128]{2,1,0:T(8,128)S(1)}, f32[4,24,128]{2,1,0:T(8,128)S(1)}) custom-call(f32[16,1,128]{2,1,0:T(1,128)S(1)} %all_to_all.20.gram_ref, f32[2,432,128]{2,1,0:T(8,128)S(1)} %bitcast.23), custom_call_target="tpu_custom_call" | custom-call | flops 2000000000 | bytes 1000000 | tf_op jit(solution)/shard_map/inner_build/pallas_call | solution.py:462
  59.6 0.0 collective-permute-done.5
  59.7 0.0 collective-permute-done.4
  59.7 0.0 copy-start
  59.7 0.7 copy-done
  60.4 5.1 %first_field.1 = (f32[24,128]{1,0:T(8,128)S(1)}, s32[128]{0:T(128)S(1)}, f32[4,48,128]{2,1,0:T(8,128)S(1)}, bf16[39,512,128]{2,1,0:T(8,128)(2,1)S(1)}) custom-call(f32[16,1,128]{2,1,0:T(1,128)S(1)} %all_to_all.20.gram_ref, f32[2,432,128]{2,1,0:T(8,128)S(1)} %bitcast.24, f32[432,128]{1,0:T(8,128)S(1)} %bitcast.34, f32[432,128]{1,0:T(8,128)S(1)} %bitcast.33, ...), custom_call_target="tpu_custom_call" | custom-call | flops 2000000000 | bytes 1000000 | tf_op jit(solution)/shard_map/first_field/pallas_call | solution.py:511
  65.5 1.9 %collective-permute-start.7 = (f32[2,6,1,2,128]{4,3,2,1,0:T(2,128)S(1)}, f32[2,6,1,2,128]{4,3,2,1,0:T(2,128)S(1)}, u32[]{:S(2)}, u32[]{:S(2)}) collective-permute-start(f32[2,6,1,2,128]{4,3,2,1,0:T(2,128)S(1)} %bitcast.27), channel_id=1, source_target_pairs={{32,0},{64,32},{96,64},{128,96},{160,128},{192,160},{224,192},{256... | collective-permute-start | bytes 36872 | tf_op jit(solution)/shard_map/ppermute | solution.py:600
  67.4 0.2 collective-permute-start.6
  67.5 1.4 %collective-permute-done.7 = f32[2,6,1,2,128]{4,3,2,1,0:T(2,128)S(1)} collective-permute-done((f32[2,6,1,2,128]{4,3,2,1,0:T(2,128)S(1)}, f32[2,6,1,2,128]{4,3,2,1,0:T(2,128)S(1)}, u32[]{:S(2)}, u32[]{:S(2)}) %collective-permute-start.7) | collective-permute-done | bytes 12320 | tf_op jit(solution)/shard_map/ppermute | solution.py:600
  68.9 0.0 collective-permute-done.6
  68.9 3.2 %collective-permute-start.8 = (f32[2,6,3,1,128]{4,3,2,1,0:T(1,128)S(1)}, f32[2,6,3,1,128]{4,3,2,1,0:T(1,128)S(1)}, u32[]{:S(2)}, u32[]{:S(2)}) collective-permute-start(f32[2,6,3,1,128]{4,3,2,1,0:T(1,128)S(1)} %get-tuple-element.46), channel_id=1, source_target_pairs={{0,8},{8,16},{16,24},{24,0},{1,9},{9,17},{17,25},{25,1},{2,10},{10... | collective-permute-start | bytes 55304 | tf_op jit(solution)/shard_map/ppermute | solution.py:599
  72.1 3.3 %collective-permute-start.9 = (f32[2,6,3,1,128]{4,3,2,1,0:T(1,128)S(1)}, f32[2,6,3,1,128]{4,3,2,1,0:T(1,128)S(1)}, u32[]{:S(2)}, u32[]{:S(2)}) collective-permute-start(f32[2,6,3,1,128]{4,3,2,1,0:T(1,128)S(1)} %get-tuple-element.47), channel_id=1, source_target_pairs={{8,0},{16,8},{24,16},{0,24},{9,1},{17,9},{25,17},{1,25},{10,2},{18... | collective-permute-start | bytes 55304 | tf_op jit(solution)/shard_map/ppermute | solution.py:600
  75.4 0.0 collective-permute-done.8
  75.5 1.2 collective-permute-done.9
  76.7 0.1 pad_maximum_fusion.2
  76.7 4.1 %collective-permute-start.11 = (f32[1,6,3,4,128]{4,3,2,1,0:T(4,128)S(1)}, f32[1,6,3,4,128]{4,3,2,1,0:T(4,128)S(1)}, u32[]{:S(2)}, u32[]{:S(2)}) collective-permute-start(f32[1,6,3,4,128]{4,3,2,1,0:T(4,128)S(1)} %get-tuple-element.44), channel_id=1, source_target_pairs={{1,0},{2,1},{3,2},{4,3},{5,4},{6,5},{7,6},{0,7},{9,8},{10,9},{11,1... | collective-permute-start | bytes 110600 | tf_op jit(solution)/shard_map/ppermute | solution.py:600
  80.8 1.9 %collective-permute-start.10 = (f32[1,6,3,4,128]{4,3,2,1,0:T(4,128)S(1)}, f32[1,6,3,4,128]{4,3,2,1,0:T(4,128)S(1)}, u32[]{:S(2)}, u32[]{:S(2)}) collective-permute-start(f32[1,6,3,4,128]{4,3,2,1,0:T(4,128)S(1)} %get-tuple-element.45), channel_id=1, source_target_pairs={{0,1},{1,2},{2,3},{3,4},{4,5},{5,6},{6,7},{7,0},{8,9},{9,10},{10,1... | collective-permute-start | bytes 110600 | tf_op jit(solution)/shard_map/ppermute | solution.py:599
  82.7 2.3 %inner_apply.1 = (f32[4,96,128]{2,1,0:T(8,128)S(1)}, f32[4,24,128]{2,1,0:T(8,128)S(1)}) custom-call(s32[128]{0:T(128)S(1)} %get-tuple-element.28.list_ref, f32[4,48,128]{2,1,0:T(8,128)S(1)} %get-tuple-element.25.geo_ref, f32[2,72,128]{2,1,0:T(8,128)S(1)} %bitcast.25, bf16[82,512,128]{2,1,0:T(8,128)(2,1)S(1)} %get-tuple-element.29.pair_ref), custom_call_target="tpu_custom_call" | custom-call | flops 1000000000 | bytes 1000000 | tf_op jit(solution)/shard_map/inner_apply/pallas_call | solution.py:542
  85.1 0.0 collective-permute-done.11
  85.1 1.7 %collective-permute-done.10 = f32[1,6,3,4,128]{4,3,2,1,0:T(4,128)S(1)} collective-permute-done((f32[1,6,3,4,128]{4,3,2,1,0:T(4,128)S(1)}, f32[1,6,3,4,128]{4,3,2,1,0:T(4,128)S(1)}, u32[]{:S(2)}, u32[]{:S(2)}) %collective-permute-start.10) | collective-permute-done | bytes 36896 | tf_op jit(solution)/shard_map/ppermute | solution.py:599
  86.7 0.0 copy-done.1
  86.7 2.4 %second_field.1 = (f32[6,4,128]{2,1,0:T(4,128)}, f32[32,2,128]{2,1,0:T(2,128)S(1)}) custom-call(s32[128]{0:T(128)S(1)} %get-tuple-element.24.list_ref, f32[4,48,128]{2,1,0:T(8,128)S(1)} %get-tuple-element.25.geo_ref, f32[2,72,128]{2,1,0:T(8,128)S(1)} %bitcast.26, f32[72,128]{1,0:T(8,128)S(1)} %bitcast.32, f32[72,128]{1,0:T(8,128)S(1)} %bitcast.31, ...), custom_call_target="tpu_custom_call" | custom-call | flops 1000000000 | bytes 1000000 | tf_op jit(solution)/shard_map/second_field/pallas_call | solution.py:582
  89.1 14.6 %all_to_all.21 = f32[32,2,128]{2,1,0:T(2,128)S(1)} all-to-all(f32[32,2,128]{2,1,0:T(2,128)S(1)} %get-tuple-element.33), channel_id=1, replica_groups=mesh['gx'=16,'gy'=4,'gz'=8] {'gy','gz'}, dimensions={0} | all-to-all | bytes 65536 | tf_op jit(solution)/shard_map/all_to_all | solution.py:625
  103.8 18.0 %all_to_all.22 = f32[16,2,128]{2,1,0:T(2,128)S(1)} all-to-all(f32[16,2,128]{2,1,0:T(2,128)S(1)} %broadcast_in_dim.5), channel_id=1, replica_groups=mesh['gx'=16,'gy'=4,'gz'=8] {'gx'}, dimensions={0} | all-to-all | bytes 32768 | tf_op jit(solution)/shard_map/all_to_all | solution.py:625
  121.8 0.5 fusion
  (8 shorter events, 0.2 us)
Async XLA Ops:
  2.3 8.0 %collective-permute-start.1 = (f32[2,36,1,2,128]{4,3,2,1,0:T(2,128)}, f32[2,36,1,2,128]{4,3,2,1,0:T(2,128)S(1)}, u32[]{:S(2)}, u32[]{:S(2)}) collective-permute-start(f32[2,36,1,2,128]{4,3,2,1,0:T(2,128)} %bitcast.35), channel_id=1, source_target_pairs={{32,0},{64,32},{96,64},{128,96},{160,128},{192,160},{224,192},{256... | collective-permute-start | bytes 221192 | tf_op jit(solution)/shard_map/ppermute | solution.py:600
  9.1 1.7 %collective-permute-start = (f32[2,36,1,2,128]{4,3,2,1,0:T(2,128)}, f32[2,36,1,2,128]{4,3,2,1,0:T(2,128)S(1)}, u32[]{:S(2)}, u32[]{:S(2)}) collective-permute-start(f32[2,36,1,2,128]{4,3,2,1,0:T(2,128)} %bitcast.36), channel_id=1, source_target_pairs={{0,32},{32,64},{64,96},{96,128},{128,160},{160,192},{192,224},{224... | collective-permute-start | bytes 221192 | tf_op jit(solution)/shard_map/ppermute | solution.py:599
  12.0 15.0 %collective-permute-start.2 = (f32[2,36,3,1,128]{4,3,2,1,0:T(1,128)S(1)}, f32[2,36,3,1,128]{4,3,2,1,0:T(1,128)S(1)}, u32[]{:S(2)}, u32[]{:S(2)}) collective-permute-start(f32[2,36,3,1,128]{4,3,2,1,0:T(1,128)S(1)} %get-tuple-element.42), channel_id=1, source_target_pairs={{0,8},{8,16},{16,24},{24,0},{1,9},{9,17},{17,25},{25,1},{2,10},{10... | collective-permute-start | bytes 331784 | tf_op jit(solution)/shard_map/ppermute | solution.py:599
  14.0 13.1 %collective-permute-start.3 = (f32[2,36,3,1,128]{4,3,2,1,0:T(1,128)S(1)}, f32[2,36,3,1,128]{4,3,2,1,0:T(1,128)S(1)}, u32[]{:S(2)}, u32[]{:S(2)}) collective-permute-start(f32[2,36,3,1,128]{4,3,2,1,0:T(1,128)S(1)} %get-tuple-element.43), channel_id=1, source_target_pairs={{8,0},{16,8},{24,16},{0,24},{9,1},{17,9},{25,17},{1,25},{10,2},{18... | collective-permute-start | bytes 331784 | tf_op jit(solution)/shard_map/ppermute | solution.py:600
  18.5 17.2 %all-to-all-start = ((f32[32,1,128]{2,1,0:T(1,128)}), f32[32,1,128]{2,1,0:T(1,128)S(1)}, u32[]{:S(2)}, u32[]{:S(2)}) async-start(f32[32,1,128]{2,1,0:T(1,128)} %get-tuple-element.18), calls=%async_computation | async-start | bytes 32768 | tf_op jit(solution)/shard_map/all_to_all | solution.py:625
  28.3 31.3 %collective-permute-start.5 = (f32[1,36,3,4,128]{4,3,2,1,0:T(4,128)S(1)}, f32[1,36,3,4,128]{4,3,2,1,0:T(4,128)S(1)}, u32[]{:S(2)}, u32[]{:S(2)}) collective-permute-start(f32[1,36,3,4,128]{4,3,2,1,0:T(4,128)S(1)} %get-tuple-element.40), channel_id=1, source_target_pairs={{1,0},{2,1},{3,2},{4,3},{5,4},{6,5},{7,6},{0,7},{9,8},{10,9},{11,1... | collective-permute-start | bytes 663560 | tf_op jit(solution)/shard_map/ppermute | solution.py:600
  32.7 27.0 %collective-permute-start.4 = (f32[1,36,3,4,128]{4,3,2,1,0:T(4,128)S(1)}, f32[1,36,3,4,128]{4,3,2,1,0:T(4,128)S(1)}, u32[]{:S(2)}, u32[]{:S(2)}) collective-permute-start(f32[1,36,3,4,128]{4,3,2,1,0:T(4,128)S(1)} %get-tuple-element.41), channel_id=1, source_target_pairs={{0,1},{1,2},{2,3},{3,4},{4,5},{5,6},{6,7},{7,0},{8,9},{9,10},{10,1... | collective-permute-start | bytes 663560 | tf_op jit(solution)/shard_map/ppermute | solution.py:599
  53.0 33.7 %copy-start.1 = (f32[7,4,128]{2,1,0:T(4,128)S(1)}, f32[7,4,128]{2,1,0:T(4,128)}, u32[]{:S(2)}) copy-start(f32[7,4,128]{2,1,0:T(4,128)} %get-tuple-element.20.mine_ref) | copy-start | bytes 43012
  59.7 0.7 copy-start
  65.5 3.4 %collective-permute-start.7 = (f32[2,6,1,2,128]{4,3,2,1,0:T(2,128)S(1)}, f32[2,6,1,2,128]{4,3,2,1,0:T(2,128)S(1)}, u32[]{:S(2)}, u32[]{:S(2)}) collective-permute-start(f32[2,6,1,2,128]{4,3,2,1,0:T(2,128)S(1)} %bitcast.27), channel_id=1, source_target_pairs={{32,0},{64,32},{96,64},{128,96},{160,128},{192,160},{224,192},{256... | collective-permute-start | bytes 36872 | tf_op jit(solution)/shard_map/ppermute | solution.py:600
  67.4 1.5 %collective-permute-start.6 = (f32[2,6,1,2,128]{4,3,2,1,0:T(2,128)S(1)}, f32[2,6,1,2,128]{4,3,2,1,0:T(2,128)S(1)}, u32[]{:S(2)}, u32[]{:S(2)}) collective-permute-start(f32[2,6,1,2,128]{4,3,2,1,0:T(2,128)S(1)} %bitcast.28), channel_id=1, source_target_pairs={{0,32},{32,64},{64,96},{96,128},{128,160},{160,192},{192,224},{224... | collective-permute-start | bytes 36872 | tf_op jit(solution)/shard_map/ppermute | solution.py:599
  68.9 6.5 %collective-permute-start.8 = (f32[2,6,3,1,128]{4,3,2,1,0:T(1,128)S(1)}, f32[2,6,3,1,128]{4,3,2,1,0:T(1,128)S(1)}, u32[]{:S(2)}, u32[]{:S(2)}) collective-permute-start(f32[2,6,3,1,128]{4,3,2,1,0:T(1,128)S(1)} %get-tuple-element.46), channel_id=1, source_target_pairs={{0,8},{8,16},{16,24},{24,0},{1,9},{9,17},{17,25},{25,1},{2,10},{10... | collective-permute-start | bytes 55304 | tf_op jit(solution)/shard_map/ppermute | solution.py:599
  72.1 4.5 %collective-permute-start.9 = (f32[2,6,3,1,128]{4,3,2,1,0:T(1,128)S(1)}, f32[2,6,3,1,128]{4,3,2,1,0:T(1,128)S(1)}, u32[]{:S(2)}, u32[]{:S(2)}) collective-permute-start(f32[2,6,3,1,128]{4,3,2,1,0:T(1,128)S(1)} %get-tuple-element.47), channel_id=1, source_target_pairs={{8,0},{16,8},{24,16},{0,24},{9,1},{17,9},{25,17},{1,25},{10,2},{18... | collective-permute-start | bytes 55304 | tf_op jit(solution)/shard_map/ppermute | solution.py:600
  76.7 8.3 %collective-permute-start.11 = (f32[1,6,3,4,128]{4,3,2,1,0:T(4,128)S(1)}, f32[1,6,3,4,128]{4,3,2,1,0:T(4,128)S(1)}, u32[]{:S(2)}, u32[]{:S(2)}) collective-permute-start(f32[1,6,3,4,128]{4,3,2,1,0:T(4,128)S(1)} %get-tuple-element.44), channel_id=1, source_target_pairs={{1,0},{2,1},{3,2},{4,3},{5,4},{6,5},{7,6},{0,7},{9,8},{10,9},{11,1... | collective-permute-start | bytes 110600 | tf_op jit(solution)/shard_map/ppermute | solution.py:600
  80.8 5.9 %collective-permute-start.10 = (f32[1,6,3,4,128]{4,3,2,1,0:T(4,128)S(1)}, f32[1,6,3,4,128]{4,3,2,1,0:T(4,128)S(1)}, u32[]{:S(2)}, u32[]{:S(2)}) collective-permute-start(f32[1,6,3,4,128]{4,3,2,1,0:T(4,128)S(1)} %get-tuple-element.45), channel_id=1, source_target_pairs={{0,1},{1,2},{2,3},{3,4},{4,5},{5,6},{6,7},{7,0},{8,9},{9,10},{10,1... | collective-permute-start | bytes 110600 | tf_op jit(solution)/shard_map/ppermute | solution.py:599

commit v7 on v6

--- a/solution.py
+++ b/solution.py
@@ -296,9 +296,12 @@
     ridge = 0.001 * trace / count + 1.0
     for a in range(count):
         matrix[a][a] = matrix[a][a] + ridge
+    inverse = []
     for c in range(count):
+        inverse.append(1.0 / matrix[c][c])
+        ratios = [matrix[a][c] * inverse[c] for a in range(c + 1, count)]
         for a in range(c + 1, count):
-            ratio = matrix[a][c] / matrix[c][c]
+            ratio = ratios[a - c - 1]
             for b in range(c + 1, a + 1):
                 matrix[a][b] = matrix[a][b] - ratio * matrix[b][c]
             right[a] = right[a] - ratio * right[c]
@@ -307,7 +310,7 @@
         rest = right[a]
         for b in range(a + 1, count):
             rest = rest - matrix[b][a] * result[b]
-        result[a] = rest / matrix[a][a]
+        result[a] = rest * inverse[a]
     return result
 
 
@@ -370,6 +373,11 @@
     )(fractions, polarizability, occupancy, history, perm, mask)
 
 
+def settle(values):
+    lowest = jnp.finfo(jnp.float32).min
+    return lax.optimization_barrier(jnp.maximum(values, lowest))
+
+
 def sum_parts(parts, copies):
     total = jnp.sum(parts, axis=0, keepdims=True)
     return jnp.broadcast_to(total, (copies,) + total.shape[1:])
@@ -415,7 +423,12 @@
 
 def coefficients(gram_ref):
     total = jnp.sum(gram_ref[...], axis=0)
-    return solve({ab: total[0:1, i : i + 1] for i, ab in enumerate(GRAM)})
+    return solve(
+        {
+            ab: jnp.broadcast_to(total[0:1, i : i + 1], (1, SLOTS))
+            for i, ab in enumerate(GRAM)
+        }
+    )
 
 
 def predict(coeffs, later):
@@ -430,14 +443,17 @@
 
 def inner_build_kernel(
     gram_ref, own_ref,
-    list_ref, pair_ref, moment_ref, sum_a, sum_b,
+    list_ref, pair_ref, moment_ref, coeffs_ref, sum_a, sum_b,
     mask_ref, q_ref, p_ref, a_ref, b_ref, sems,
 ):
     copies = read_mask(own_ref, mask_ref, sems)
     geo = [own_rows_of(own_ref, a) for a in range(4)]
     prepare_distances(geo, geo, 0, q_ref, p_ref)
     later = [own_rows_of(own_ref, row) for row in range(LATER, MASK_ROW)]
-    moment = predict(coefficients(gram_ref), later)
+    coeffs = coefficients(gram_ref)
+    for h in range(5):
+        coeffs_ref[h : h + 1, :] = jnp.broadcast_to(coeffs[h], (1, SLOTS))
+    moment = predict(coeffs, later)
     prepare_moments(geo, 0, moment, a_ref, b_ref)
     for c in range(6):
         moment_ref[c] = own_part(moment[c])
@@ -463,11 +479,12 @@
         inner_build_kernel,
         name="inner_build",
         in_specs=[vmem_spec()] * 2,
-        out_specs=[smem_spec()] + [vmem_spec()] * 4,
+        out_specs=[smem_spec()] + [vmem_spec()] * 5,
         out_shape=[
             jax.ShapeDtypeStruct((LIST,), jnp.int32),
             pair_shape(True),
             jax.ShapeDtypeStruct((6, OWN, SLOTS), jnp.float32),
+            jax.ShapeDtypeStruct((5, SLOTS), jnp.float32),
         ]
         + SUMS,
         scratch_shapes=MASK_SCRATCH + DISTANCE_ROWS + MOMENT_ROWS + MASK_SEMS,
@@ -477,7 +494,7 @@
 
 
 def first_kernel(
-    gram_ref, own_ref, before_ref, after_ref, mine_ref, moment_ref, start_a, start_b,
+    coeffs_ref, own_ref, before_ref, after_ref, mine_ref, moment_ref, start_a, start_b,
     out_ref, list_ref, geo_ref, pair_ref,
     mask_ref, q_ref, p_ref, a_ref, b_ref, sum_a, sum_b, sems,
 ):
@@ -491,7 +508,7 @@
     sum_a[...] = start_a[...]
     sum_b[...] = start_b[...]
     moment = predict(
-        coefficients(gram_ref),
+        [coeffs_ref[h : h + 1, :] for h in range(5)],
         [edge_rows(before_ref, after_ref, row) for row in range(LATER, MASK_ROW)],
     )
     prepare_moments(edge_geo, INNER, moment, a_ref, b_ref)
@@ -507,7 +524,7 @@
         store_layers(out_ref, 6, c, dipole)
 
 
-def first_field(gram, own, before, after, mine, moment, sums):
+def first_field(coeffs, own, before, after, mine, moment, sums):
     return pl.pallas_call(
         first_kernel,
         name="first_field",
@@ -526,7 +543,7 @@
         + MASK_SEMS,
         compiler_params=PARAMS,
         cost_estimate=cost(2_000_000_000),
-    )(gram, own, before, after, mine, moment, *sums)
+    )(coeffs, own, before, after, mine, moment, *sums)
 
 
 def inner_apply_kernel(
@@ -601,12 +618,13 @@
     return before, after
 
 
-def joined(cells, axis, dim):
+def joined(cells, axis, dim, middle=None):
     size = cells.shape[dim]
     low = lax.slice_in_dim(cells, 0, 1, axis=dim)
     high = lax.slice_in_dim(cells, size - 1, size, axis=dim)
     before, after = both_ways(low, high, axis)
-    return jnp.concatenate([before, cells, after], axis=dim)
+    middle = cells if middle is None else middle
+    return jnp.concatenate([before, middle, after], axis=dim)
 
 
 def z_layers(cells):
@@ -638,14 +656,21 @@
         plane,
     )
     gram = exchange(gram, ("gy", "gz"))
-    cells = joined(stacked.reshape(2, ROWS, 1, 2, SLOTS), "gx", 2)
+    cells = joined(
+        stacked.reshape(2, ROWS, 1, 2, SLOTS),
+        "gx",
+        2,
+        settle(stacked).reshape(2, ROWS, 1, 2, SLOTS),
+    )
+    mine = settle(mine)
+    cells = lax.optimization_barrier(cells)
     cells = joined(cells, "gy", 3)
     gram = sum_parts(gram, line)
     gram = exchange(gram, "gx")
     own, before, after = z_layers(cells)
-    inner_list, inner_pairs, moment, *sums = inner_build(gram, own)
+    inner_list, inner_pairs, moment, coeffs, *sums = inner_build(gram, own)
     dipoles, outer_list, geo, outer_pairs = first_field(
-        gram, own, before, after, mine, moment, sums
+        coeffs, own, before, after, mine, moment, sums
     )
     cells = joined(dipoles.reshape(2, 6, 1, 2, SLOTS), "gx", 2)
     cells = joined(cells, "gy", 3)

time: 123 us -> 121 us (0.984)
  Pallas kernels: 18 us -> 15.6 us
  waiting for transfers between devices: 7.06 us -> 4.85 us
  blocking collectives: 49.8 us -> 51.7 us
    ppermute x6, starting transfers between devices: 25 us -> 22.5 us  [both_ways(): lax.ppermute(low, axis, [((i + 1) % count, i) for i in range(count)])]
    all_to_all x1, starting transfers between devices: 8.49 us -> 10.4 us  [exchange(): return lax.all_to_all(parts, axes, 0, 0)]
    all_to_all x3, blocking collectives: 49.8 us -> 51.7 us  [exchange(): return lax.all_to_all(parts, axes, 0, 0)]
    concatenate x4, other arithmetic: 2.24 us -> 0.47 us  [joined(): return jnp.concatenate([before, middle, after], axis=dim)]
    max x0 -> x2, other arithmetic: none -> 1.64 us  [settle(): return lax.optimization_barrier(jnp.maximum(values, lowest))]
    ppermute x6, starting transfers between devices: 9.13 us -> 10.7 us  [both_ways(): lax.ppermute(high, axis, [(i, (i + 1) % count) for i in range(count)])]
    pallas_call x1, Pallas kernels: 5.1 us -> 3.66 us  [first_field(): pl.pallas_call(first_kernel, name='first_field', in_specs=[vmem_spec()] *...]
    ppermute x6, waiting for transfers between devices: 3.68 us -> 2.41 us  [both_ways(): lax.ppermute(low, axis, [((i + 1) % count, i) for i in range(count)])]
  transfers between devices with their start and end apart: 13 -> 13, of which waited for: 6 -> 7; matrix products, arithmetic and copies ran while one was open for 1% -> 2% of each run, Pallas kernels for 7% -> 7%
where the time goes in v7:
time: 121 us; the launch traced here: 120 us
  blocking collectives  51.7 us (43%)
  starting transfers between devices  43.7 us (36%)
  Pallas kernels  15.6 us (13%)
  waiting for transfers between devices  4.85 us (4%)
  other arithmetic  2.77 us (2%)
    all_to_all x3, blocking collectives, exchange(): return lax.all_to_all(parts, axes, 0, 0)  51.7 us
    ppermute x6, starting transfers between devices, both_ways(): lax.ppermute(low, axis, [((i + 1) % count, i) for i in range(count)])  22.5 us
    ppermute x6, starting transfers between devices, both_ways(): lax.ppermute(high, axis, [(i, (i + 1) % count) for i in range(count)])  10.7 us
    all_to_all x1, starting transfers between devices, exchange(): return lax.all_to_all(parts, axes, 0, 0)  10.4 us
    pallas_call x1, Pallas kernels, inner_build(): pl.pallas_call(inner_build_kernel, name='inner_build', in_specs=[vmem_spe...  5.59 us
    pallas_call x1, Pallas kernels, first_field(): pl.pallas_call(first_kernel, name='first_field', in_specs=[vmem_spec()] *...  3.66 us
  transfers between devices with their start and end apart: 13, of which 7 were waited for; matrix products, arithmetic and copies ran while one was open for 2% of the time, Pallas kernels for 7%

profile of v7, /device:TPU:1, one launch (start us, length us, event | category | flops | bytes accessed | tf_op | source)
XLA Modules:
  0.0 120.3 jit_solution(11354931749367313709)
XLA Ops:
  0.6 1.7 %prepare.1 = (f32[144,128]{1,0:T(8,128)}, f32[32,1,128]{2,1,0:T(1,128)}, f32[7,4,128]{2,1,0:T(4,128)}) custom-call(f32[3,4,128]{2,1,0:T(4,128)} %bitcast.43, f32[4,128]{1,0:T(4,128)} %bitcast.44, s32[4,128]{1,0:T(4,128)} %bitcast.45, f32[6,6,4,128]{3,2,1,0:T(4,128)} %bitcast.39, f32[6,4,128]{2,1,0:T(4,128)} %bitcast.42, s32[4,27]{1,0:T(4,128)} %bitcast.46), custom_call_target="tpu_custom_call" | custom-call | tf_op jit(solution)/shard_map/prepare/pallas_call | solution.py:363
  2.3 6.8 %collective-permute-start.1 = (f32[2,36,1,2,128]{4,3,2,1,0:T(2,128)}, f32[2,36,1,2,128]{4,3,2,1,0:T(2,128)S(1)}, u32[]{:S(2)}, u32[]{:S(2)}) collective-permute-start(f32[2,36,1,2,128]{4,3,2,1,0:T(2,128)} %bitcast.40), channel_id=1, source_target_pairs={{32,0},{64,32},{96,64},{128,96},{160,128},{192,160},{224,192},{256... | collective-permute-start | bytes 221192 | tf_op jit(solution)/shard_map/ppermute | solution.py:617
  9.1 0.0 collective-permute-start
  9.1 0.9 broadcast_maximum_fusion
  10.1 0.2 collective-permute-done.1
  10.3 0.6 collective-permute-done
  10.9 0.1 pad_maximum_fusion.1
  11.0 0.2 fusion.2
  11.1 1.9 %collective-permute-start.2 = (f32[2,36,3,1,128]{4,3,2,1,0:T(1,128)S(1)}, f32[2,36,3,1,128]{4,3,2,1,0:T(1,128)S(1)}, u32[]{:S(2)}, u32[]{:S(2)}) collective-permute-start(f32[2,36,3,1,128]{4,3,2,1,0:T(1,128)S(1)} %get-tuple-element.44), channel_id=1, source_target_pairs={{0,8},{8,16},{16,24},{24,0},{1,9},{9,17},{17,25},{25,1},{2,10},{10... | collective-permute-start | bytes 331784 | tf_op jit(solution)/shard_map/ppermute | solution.py:616
  13.1 4.6 %collective-permute-start.3 = (f32[2,36,3,1,128]{4,3,2,1,0:T(1,128)S(1)}, f32[2,36,3,1,128]{4,3,2,1,0:T(1,128)S(1)}, u32[]{:S(2)}, u32[]{:S(2)}) collective-permute-start(f32[2,36,3,1,128]{4,3,2,1,0:T(1,128)S(1)} %get-tuple-element.45), channel_id=1, source_target_pairs={{8,0},{16,8},{24,16},{0,24},{9,1},{17,9},{25,17},{1,25},{10,2},{18... | collective-permute-start | bytes 331784 | tf_op jit(solution)/shard_map/ppermute | solution.py:617
  17.7 17.2 %all_to_all.20 = f32[32,1,128]{2,1,0:T(1,128)S(1)} all-to-all(f32[32,1,128]{2,1,0:T(1,128)} %get-tuple-element.19), channel_id=1, replica_groups=mesh['gx'=16,'gy'=4,'gz'=8] {'gy','gz'}, dimensions={0} | all-to-all | bytes 32768 | tf_op jit(solution)/shard_map/all_to_all | solution.py:643
  34.8 0.1 reduce_sum.27
  34.9 0.6 broadcast_in_dim.4
  35.5 10.4 %all-to-all-start.1 = ((f32[16,1,128]{2,1,0:T(1,128)}), f32[16,1,128]{2,1,0:T(1,128)S(1)}, u32[]{:S(2)}, u32[]{:S(2)}) async-start(f32[16,1,128]{2,1,0:T(1,128)} %broadcast_in_dim.4), calls=%async_computation.1 | async-start | bytes 16384 | tf_op jit(solution)/shard_map/all_to_all | solution.py:643
  45.9 0.0 collective-permute-done.2
  45.9 0.0 collective-permute-done.3
  45.9 0.3 pad_maximum_fusion
  46.3 2.2 %collective-permute-start.5 = (f32[1,36,3,4,128]{4,3,2,1,0:T(4,128)S(1)}, f32[1,36,3,4,128]{4,3,2,1,0:T(4,128)S(1)}, u32[]{:S(2)}, u32[]{:S(2)}) collective-permute-start(f32[1,36,3,4,128]{4,3,2,1,0:T(4,128)S(1)} %get-tuple-element.42), channel_id=1, source_target_pairs={{1,0},{2,1},{3,2},{4,3},{5,4},{6,5},{7,6},{0,7},{9,8},{10,9},{11,1... | collective-permute-start | bytes 663560 | tf_op jit(solution)/shard_map/ppermute | solution.py:617
  48.5 3.1 %collective-permute-start.4 = (f32[1,36,3,4,128]{4,3,2,1,0:T(4,128)S(1)}, f32[1,36,3,4,128]{4,3,2,1,0:T(4,128)S(1)}, u32[]{:S(2)}, u32[]{:S(2)}) collective-permute-start(f32[1,36,3,4,128]{4,3,2,1,0:T(4,128)S(1)} %get-tuple-element.43), channel_id=1, source_target_pairs={{0,1},{1,2},{2,3},{3,4},{4,5},{5,6},{6,7},{7,0},{8,9},{9,10},{10,1... | collective-permute-start | bytes 663560 | tf_op jit(solution)/shard_map/ppermute | solution.py:616
  51.6 0.7 broadcast_maximum_fusion.1.mine_ref
  52.3 0.6 all-to-all-done.1.gram_ref
  52.9 5.6 %inner_build.1 = (s32[128]{0:T(128)S(1)}, bf16[82,512,128]{2,1,0:T(8,128)(2,1)S(1)}, f32[6,4,128]{2,1,0:T(4,128)S(1)}, f32[5,128]{1,0:T(8,128)S(1)}, f32[4,96,12...) custom-call(f32[16,1,128]{2,1,0:T(1,128)S(1)} %all-to-all-done.1.gram_ref, f32[2,432,128]{2,1,0:T(8,128)S(1)} %bitcast.26), custom_call_target="tpu_custom_call" | custom-call | flops 2000000000 | bytes 1000000 | tf_op jit(solution)/shard_map/inner_build/pallas_call | solution.py:478
  58.5 0.0 collective-permute-done.5
  58.5 0.0 collective-permute-done.4
  58.5 3.7 %first_field.1 = (f32[24,128]{1,0:T(8,128)S(1)}, s32[128]{0:T(128)S(1)}, f32[4,48,128]{2,1,0:T(8,128)S(1)}, bf16[39,512,128]{2,1,0:T(8,128)(2,1)S(1)}) custom-call(f32[5,128]{1,0:T(8,128)S(1)} %get-tuple-element.21.coeffs_ref, f32[2,432,128]{2,1,0:T(8,128)S(1)} %bitcast.27, f32[432,128]{1,0:T(8,128)S(1)} %bitcast.37, f32[432,128]{1,0:T(8,128)S(1)} %bitcast.36, ...), custom_call_target="tpu_custom_call" | custom-call | flops 2000000000 | bytes 1000000 | tf_op jit(solution)/shard_map/first_field/pallas_call | solution.py:528
  62.1 1.8 %collective-permute-start.7 = (f32[2,6,1,2,128]{4,3,2,1,0:T(2,128)S(1)}, f32[2,6,1,2,128]{4,3,2,1,0:T(2,128)S(1)}, u32[]{:S(2)}, u32[]{:S(2)}) collective-permute-start(f32[2,6,1,2,128]{4,3,2,1,0:T(2,128)S(1)} %bitcast.30), channel_id=1, source_target_pairs={{32,0},{64,32},{96,64},{128,96},{160,128},{192,160},{224,192},{256... | collective-permute-start | bytes 36872 | tf_op jit(solution)/shard_map/ppermute | solution.py:617
  64.0 1.0 collective-permute-start.6
  65.0 1.4 %collective-permute-done.7 = f32[2,6,1,2,128]{4,3,2,1,0:T(2,128)S(1)} collective-permute-done((f32[2,6,1,2,128]{4,3,2,1,0:T(2,128)S(1)}, f32[2,6,1,2,128]{4,3,2,1,0:T(2,128)S(1)}, u32[]{:S(2)}, u32[]{:S(2)}) %collective-permute-start.7) | collective-permute-done | bytes 12320 | tf_op jit(solution)/shard_map/ppermute | solution.py:617
  66.4 0.1 collective-permute-done.6
  66.5 2.3 %collective-permute-start.8 = (f32[2,6,3,1,128]{4,3,2,1,0:T(1,128)S(1)}, f32[2,6,3,1,128]{4,3,2,1,0:T(1,128)S(1)}, u32[]{:S(2)}, u32[]{:S(2)}) collective-permute-start(f32[2,6,3,1,128]{4,3,2,1,0:T(1,128)S(1)} %get-tuple-element.48), channel_id=1, source_target_pairs={{0,8},{8,16},{16,24},{24,0},{1,9},{9,17},{17,25},{25,1},{2,10},{10... | collective-permute-start | bytes 55304 | tf_op jit(solution)/shard_map/ppermute | solution.py:616
  68.8 4.2 %collective-permute-start.9 = (f32[2,6,3,1,128]{4,3,2,1,0:T(1,128)S(1)}, f32[2,6,3,1,128]{4,3,2,1,0:T(1,128)S(1)}, u32[]{:S(2)}, u32[]{:S(2)}) collective-permute-start(f32[2,6,3,1,128]{4,3,2,1,0:T(1,128)S(1)} %get-tuple-element.49), channel_id=1, source_target_pairs={{8,0},{16,8},{24,16},{0,24},{9,1},{17,9},{25,17},{1,25},{10,2},{18... | collective-permute-start | bytes 55304 | tf_op jit(solution)/shard_map/ppermute | solution.py:617
  73.0 0.0 collective-permute-done.8
  73.0 0.9 collective-permute-done.9
  73.9 0.1 pad_maximum_fusion.2
  73.9 2.9 %collective-permute-start.11 = (f32[1,6,3,4,128]{4,3,2,1,0:T(4,128)S(1)}, f32[1,6,3,4,128]{4,3,2,1,0:T(4,128)S(1)}, u32[]{:S(2)}, u32[]{:S(2)}) collective-permute-start(f32[1,6,3,4,128]{4,3,2,1,0:T(4,128)S(1)} %get-tuple-element.46), channel_id=1, source_target_pairs={{1,0},{2,1},{3,2},{4,3},{5,4},{6,5},{7,6},{0,7},{9,8},{10,9},{11,1... | collective-permute-start | bytes 110600 | tf_op jit(solution)/shard_map/ppermute | solution.py:617
  76.8 2.4 %collective-permute-start.10 = (f32[1,6,3,4,128]{4,3,2,1,0:T(4,128)S(1)}, f32[1,6,3,4,128]{4,3,2,1,0:T(4,128)S(1)}, u32[]{:S(2)}, u32[]{:S(2)}) collective-permute-start(f32[1,6,3,4,128]{4,3,2,1,0:T(4,128)S(1)} %get-tuple-element.47), channel_id=1, source_target_pairs={{0,1},{1,2},{2,3},{3,4},{4,5},{5,6},{6,7},{7,0},{8,9},{9,10},{10,1... | collective-permute-start | bytes 110600 | tf_op jit(solution)/shard_map/ppermute | solution.py:616
  79.2 2.3 %inner_apply.1 = (f32[4,96,128]{2,1,0:T(8,128)S(1)}, f32[4,24,128]{2,1,0:T(8,128)S(1)}) custom-call(s32[128]{0:T(128)S(1)} %get-tuple-element.30.list_ref, f32[4,48,128]{2,1,0:T(8,128)S(1)} %get-tuple-element.27.geo_ref, f32[2,72,128]{2,1,0:T(8,128)S(1)} %bitcast.28, bf16[82,512,128]{2,1,0:T(8,128)(2,1)S(1)} %get-tuple-element.31.pair_ref), custom_call_target="tpu_custom_call" | custom-call | flops 1000000000 | bytes 1000000 | tf_op jit(solution)/shard_map/inner_apply/pallas_call | solution.py:559
  81.5 0.0 collective-permute-done.11
  81.6 1.2 collective-permute-done.10
  82.7 2.3 %second_field.1 = (f32[6,4,128]{2,1,0:T(4,128)}, f32[32,2,128]{2,1,0:T(2,128)S(1)}) custom-call(s32[128]{0:T(128)S(1)} %get-tuple-element.26.list_ref, f32[4,48,128]{2,1,0:T(8,128)S(1)} %get-tuple-element.27.geo_ref, f32[2,72,128]{2,1,0:T(8,128)S(1)} %bitcast.29, f32[72,128]{1,0:T(8,128)S(1)} %bitcast.35, f32[72,128]{1,0:T(8,128)S(1)} %bitcast.34, ...), custom_call_target="tpu_custom_call" | custom-call | flops 1000000000 | bytes 1000000 | tf_op jit(solution)/shard_map/second_field/pallas_call | solution.py:599
  85.1 15.9 %all_to_all.21 = f32[32,2,128]{2,1,0:T(2,128)S(1)} all-to-all(f32[32,2,128]{2,1,0:T(2,128)S(1)} %get-tuple-element.35), channel_id=1, replica_groups=mesh['gx'=16,'gy'=4,'gz'=8] {'gy','gz'}, dimensions={0} | all-to-all | bytes 65536 | tf_op jit(solution)/shard_map/all_to_all | solution.py:643
  101.0 18.7 %all_to_all.22 = f32[16,2,128]{2,1,0:T(2,128)S(1)} all-to-all(f32[16,2,128]{2,1,0:T(2,128)S(1)} %broadcast_in_dim.5), channel_id=1, replica_groups=mesh['gx'=16,'gy'=4,'gz'=8] {'gx'}, dimensions={0} | all-to-all | bytes 32768 | tf_op jit(solution)/shard_map/all_to_all | solution.py:643
  119.7 0.5 fusion
  (7 shorter events, 0.2 us)
Async XLA Ops:
  2.3 8.0 %collective-permute-start.1 = (f32[2,36,1,2,128]{4,3,2,1,0:T(2,128)}, f32[2,36,1,2,128]{4,3,2,1,0:T(2,128)S(1)}, u32[]{:S(2)}, u32[]{:S(2)}) collective-permute-start(f32[2,36,1,2,128]{4,3,2,1,0:T(2,128)} %bitcast.40), channel_id=1, source_target_pairs={{32,0},{64,32},{96,64},{128,96},{160,128},{192,160},{224,192},{256... | collective-permute-start | bytes 221192 | tf_op jit(solution)/shard_map/ppermute | solution.py:617
  9.1 1.7 %collective-permute-start = (f32[2,36,1,2,128]{4,3,2,1,0:T(2,128)}, f32[2,36,1,2,128]{4,3,2,1,0:T(2,128)S(1)}, u32[]{:S(2)}, u32[]{:S(2)}) collective-permute-start(f32[2,36,1,2,128]{4,3,2,1,0:T(2,128)} %bitcast.41), channel_id=1, source_target_pairs={{0,32},{32,64},{64,96},{96,128},{128,160},{160,192},{192,224},{224... | collective-permute-start | bytes 221192 | tf_op jit(solution)/shard_map/ppermute | solution.py:616
  11.1 34.7 %collective-permute-start.2 = (f32[2,36,3,1,128]{4,3,2,1,0:T(1,128)S(1)}, f32[2,36,3,1,128]{4,3,2,1,0:T(1,128)S(1)}, u32[]{:S(2)}, u32[]{:S(2)}) collective-permute-start(f32[2,36,3,1,128]{4,3,2,1,0:T(1,128)S(1)} %get-tuple-element.44), channel_id=1, source_target_pairs={{0,8},{8,16},{16,24},{24,0},{1,9},{9,17},{17,25},{25,1},{2,10},{10... | collective-permute-start | bytes 331784 | tf_op jit(solution)/shard_map/ppermute | solution.py:616
  13.1 32.8 %collective-permute-start.3 = (f32[2,36,3,1,128]{4,3,2,1,0:T(1,128)S(1)}, f32[2,36,3,1,128]{4,3,2,1,0:T(1,128)S(1)}, u32[]{:S(2)}, u32[]{:S(2)}) collective-permute-start(f32[2,36,3,1,128]{4,3,2,1,0:T(1,128)S(1)} %get-tuple-element.45), channel_id=1, source_target_pairs={{8,0},{16,8},{24,16},{0,24},{9,1},{17,9},{25,17},{1,25},{10,2},{18... | collective-permute-start | bytes 331784 | tf_op jit(solution)/shard_map/ppermute | solution.py:617
  35.5 17.4 %all-to-all-start.1 = ((f32[16,1,128]{2,1,0:T(1,128)}), f32[16,1,128]{2,1,0:T(1,128)S(1)}, u32[]{:S(2)}, u32[]{:S(2)}) async-start(f32[16,1,128]{2,1,0:T(1,128)} %broadcast_in_dim.4), calls=%async_computation.1 | async-start | bytes 16384 | tf_op jit(solution)/shard_map/all_to_all | solution.py:643
  46.3 12.2 %collective-permute-start.5 = (f32[1,36,3,4,128]{4,3,2,1,0:T(4,128)S(1)}, f32[1,36,3,4,128]{4,3,2,1,0:T(4,128)S(1)}, u32[]{:S(2)}, u32[]{:S(2)}) collective-permute-start(f32[1,36,3,4,128]{4,3,2,1,0:T(4,128)S(1)} %get-tuple-element.42), channel_id=1, source_target_pairs={{1,0},{2,1},{3,2},{4,3},{5,4},{6,5},{7,6},{0,7},{9,8},{10,9},{11,1... | collective-permute-start | bytes 663560 | tf_op jit(solution)/shard_map/ppermute | solution.py:617
  48.5 10.0 %collective-permute-start.4 = (f32[1,36,3,4,128]{4,3,2,1,0:T(4,128)S(1)}, f32[1,36,3,4,128]{4,3,2,1,0:T(4,128)S(1)}, u32[]{:S(2)}, u32[]{:S(2)}) collective-permute-start(f32[1,36,3,4,128]{4,3,2,1,0:T(4,128)S(1)} %get-tuple-element.43), channel_id=1, source_target_pairs={{0,1},{1,2},{2,3},{3,4},{4,5},{5,6},{6,7},{7,0},{8,9},{9,10},{10,1... | collective-permute-start | bytes 663560 | tf_op jit(solution)/shard_map/ppermute | solution.py:616
  62.1 4.2 %collective-permute-start.7 = (f32[2,6,1,2,128]{4,3,2,1,0:T(2,128)S(1)}, f32[2,6,1,2,128]{4,3,2,1,0:T(2,128)S(1)}, u32[]{:S(2)}, u32[]{:S(2)}) collective-permute-start(f32[2,6,1,2,128]{4,3,2,1,0:T(2,128)S(1)} %bitcast.30), channel_id=1, source_target_pairs={{32,0},{64,32},{96,64},{128,96},{160,128},{192,160},{224,192},{256... | collective-permute-start | bytes 36872 | tf_op jit(solution)/shard_map/ppermute | solution.py:617
  64.0 2.4 %collective-permute-start.6 = (f32[2,6,1,2,128]{4,3,2,1,0:T(2,128)S(1)}, f32[2,6,1,2,128]{4,3,2,1,0:T(2,128)S(1)}, u32[]{:S(2)}, u32[]{:S(2)}) collective-permute-start(f32[2,6,1,2,128]{4,3,2,1,0:T(2,128)S(1)} %bitcast.31), channel_id=1, source_target_pairs={{0,32},{32,64},{64,96},{96,128},{128,160},{160,192},{192,224},{224... | collective-permute-start | bytes 36872 | tf_op jit(solution)/shard_map/ppermute | solution.py:616
  66.5 6.5 %collective-permute-start.8 = (f32[2,6,3,1,128]{4,3,2,1,0:T(1,128)S(1)}, f32[2,6,3,1,128]{4,3,2,1,0:T(1,128)S(1)}, u32[]{:S(2)}, u32[]{:S(2)}) collective-permute-start(f32[2,6,3,1,128]{4,3,2,1,0:T(1,128)S(1)} %get-tuple-element.48), channel_id=1, source_target_pairs={{0,8},{8,16},{16,24},{24,0},{1,9},{9,17},{17,25},{25,1},{2,10},{10... | collective-permute-start | bytes 55304 | tf_op jit(solution)/shard_map/ppermute | solution.py:616
  68.8 5.1 %collective-permute-start.9 = (f32[2,6,3,1,128]{4,3,2,1,0:T(1,128)S(1)}, f32[2,6,3,1,128]{4,3,2,1,0:T(1,128)S(1)}, u32[]{:S(2)}, u32[]{:S(2)}) collective-permute-start(f32[2,6,3,1,128]{4,3,2,1,0:T(1,128)S(1)} %get-tuple-element.49), channel_id=1, source_target_pairs={{8,0},{16,8},{24,16},{0,24},{9,1},{17,9},{25,17},{1,25},{10,2},{18... | collective-permute-start | bytes 55304 | tf_op jit(solution)/shard_map/ppermute | solution.py:617
  73.9 7.6 %collective-permute-start.11 = (f32[1,6,3,4,128]{4,3,2,1,0:T(4,128)S(1)}, f32[1,6,3,4,128]{4,3,2,1,0:T(4,128)S(1)}, u32[]{:S(2)}, u32[]{:S(2)}) collective-permute-start(f32[1,6,3,4,128]{4,3,2,1,0:T(4,128)S(1)} %get-tuple-element.46), channel_id=1, source_target_pairs={{1,0},{2,1},{3,2},{4,3},{5,4},{6,5},{7,6},{0,7},{9,8},{10,9},{11,1... | collective-permute-start | bytes 110600 | tf_op jit(solution)/shard_map/ppermute | solution.py:617
  76.8 5.9 %collective-permute-start.10 = (f32[1,6,3,4,128]{4,3,2,1,0:T(4,128)S(1)}, f32[1,6,3,4,128]{4,3,2,1,0:T(4,128)S(1)}, u32[]{:S(2)}, u32[]{:S(2)}) collective-permute-start(f32[1,6,3,4,128]{4,3,2,1,0:T(4,128)S(1)} %get-tuple-element.47), channel_id=1, source_target_pairs={{0,1},{1,2},{2,3},{3,4},{4,5},{5,6},{6,7},{7,0},{8,9},{9,10},{10,1... | collective-permute-start | bytes 110600 | tf_op jit(solution)/shard_map/ppermute | solution.py:616

commit v8 on v7

--- a/solution.py
+++ b/solution.py
@@ -19,7 +19,8 @@
 TERMS = 48
 A_ROWS = 96
 B_ROWS = 24
-BATCH = 13
+INNER_BATCH = 13
+OUTER_BATCH = 15
 LIST = 128
 COUNT_AT = LIST - 1
 ROWS = 36
@@ -132,25 +133,25 @@
     for t, k in candidates(inner):
         list_ref[count] = (source_tile(t, k) - first) * OWN + t
         count = count + (mask_ref[t, k] != 0.0).astype(jnp.int32)
-    for extra in range(BATCH):
+    for extra in range(OUTER_BATCH):
         list_ref[count + extra] = INNER * OWN
     list_ref[COUNT_AT] = count
     return count
 
 
-def trips(count):
-    return (count + BATCH - 1) // BATCH
-
-
-def build_all(list_ref, count, start, pair_ref, q_ref, p_ref):
+def trips(count, batch):
+    return (count + batch - 1) // batch
+
+
+def build_all(list_ref, count, start, size, pair_ref, q_ref, p_ref):
     def batch(b, carry):
-        for u in range(BATCH):
-            slot = b * BATCH + u
+        for u in range(size):
+            slot = b * size + u
             entry = list_ref[slot]
             build(start + slot, entry // OWN, entry % OWN, None, pair_ref, q_ref, p_ref)
         return carry
 
-    lax.fori_loop(0, trips(count), batch, 0)
+    lax.fori_loop(0, trips(count, size), batch, 0)
 
 
 def build(slot, n, t, keep, pair_ref, q_ref, p_ref):
@@ -241,10 +242,10 @@
         sum_a[slot], sum_b[slot] = apply_slot(slot, OWN_TILES[slot], pair_ref, a_ref, b_ref)
 
 
-def apply_all(list_ref, count, start, pair_ref, a_ref, b_ref, sum_a, sum_b):
+def apply_all(list_ref, count, start, size, pair_ref, a_ref, b_ref, sum_a, sum_b):
     def batch(b, carry):
-        for u in range(BATCH):
-            slot = b * BATCH + u
+        for u in range(size):
+            slot = b * size + u
             entry = list_ref[slot]
             t = entry % OWN
             part_a, part_b = apply_slot(start + slot, entry // OWN, pair_ref, a_ref, b_ref)
@@ -252,7 +253,7 @@
             sum_b[t] += part_b
         return carry
 
-    lax.fori_loop(0, trips(count), batch, 0)
+    lax.fori_loop(0, trips(count, size), batch, 0)
 
 
 def field_of(geo, sum_a, sum_b):
@@ -322,12 +323,14 @@
 
 def prepare_kernel(
     fractions_ref, polar_ref, occupancy_ref, history_ref, perm_ref, mask_ref,
-    stacked_ref, gram_ref, own_ref,
+    stacked_ref, gram_ref, both_ref,
 ):
     filled = occupancy_ref[...].astype(jnp.float32)
-    own_ref[0] = RELAXATION * filled * polar_ref[...]
+    start = ROWS * OWN
+    both_ref[start : start + OWN, :] = RELAXATION * filled * polar_ref[...]
     for c in range(6):
-        own_ref[1 + c] = perm_ref[c]
+        at = start + OWN * (1 + c)
+        both_ref[at : at + OWN, :] = perm_ref[c]
     masked = [[history_ref[h, c] * filled for c in range(6)] for h in range(6)]
     for a in range(3):
         store_layers(stacked_ref, ROWS, a, fractions_ref[a])
@@ -340,6 +343,8 @@
     )
     store_layers(stacked_ref, ROWS, MASK_ROW, allowed)
     store_layers(stacked_ref, ROWS, ROWS - 1, jnp.zeros((OWN, SLOTS), jnp.float32))
+    both_ref[0:start, :] = stacked_ref[...]
+    both_ref[start + 7 * OWN :, :] = jnp.zeros((4, SLOTS), jnp.float32)
     lane = lax.broadcasted_iota(jnp.int32, (1, SLOTS), 1)
     row = jnp.zeros((1, SLOTS), jnp.float32)
     for index, (a, b) in enumerate(GRAM):
@@ -368,7 +373,7 @@
         out_shape=[
             jax.ShapeDtypeStruct((ROWS * OWN, SLOTS), jnp.float32),
             jax.ShapeDtypeStruct((copies, 1, SLOTS), jnp.float32),
-            jax.ShapeDtypeStruct((7, OWN, SLOTS), jnp.float32),
+            jax.ShapeDtypeStruct(((ROWS + 7) * OWN + 4, SLOTS), jnp.float32),
         ],
     )(fractions, polarizability, occupancy, history, perm, mask)
 
@@ -399,8 +404,9 @@
 
 
 def slots_for(inner):
-    batches = -(-len(candidates(inner)) // BATCH)
-    return batches * BATCH + (OWN if inner else 0)
+    size = INNER_BATCH if inner else OUTER_BATCH
+    batches = -(-len(candidates(inner)) // size)
+    return batches * size + (OWN if inner else 0)
 
 
 def pair_shape(inner):
@@ -465,9 +471,9 @@
     for copy in copies:
         copy.wait()
     count = list_pairs(mask_ref, list_ref, True)
-    build_all(list_ref, count, OWN, pair_ref, q_ref, p_ref)
+    build_all(list_ref, count, OWN, INNER_BATCH, pair_ref, q_ref, p_ref)
     apply_selves(pair_ref, a_ref, b_ref, sum_a, sum_b)
-    apply_all(list_ref, count, OWN, pair_ref, a_ref, b_ref, sum_a, sum_b)
+    apply_all(list_ref, count, OWN, INNER_BATCH, pair_ref, a_ref, b_ref, sum_a, sum_b)
 
 
 MASK_SCRATCH = [pltpu.SMEM((OWN, SLOTS), jnp.float32)]
@@ -515,8 +521,8 @@
     for copy in copies:
         copy.wait()
     count = list_pairs(mask_ref, list_ref, False)
-    build_all(list_ref, count, 0, pair_ref, q_ref, p_ref)
-    apply_all(list_ref, count, 0, pair_ref, a_ref, b_ref, sum_a, sum_b)
+    build_all(list_ref, count, 0, OUTER_BATCH, pair_ref, q_ref, p_ref)
+    apply_all(list_ref, count, 0, OUTER_BATCH, pair_ref, a_ref, b_ref, sum_a, sum_b)
 
     fields = field_of(own_geo, sum_a, sum_b)
     for c in range(6):
@@ -552,7 +558,7 @@
     geo = [geo_ref[a, 0:INNER, :] for a in range(4)]
     prepare_moments(geo, 0, [own_rows_of(own_ref, c) for c in range(6)], a_ref, b_ref)
     apply_selves(pair_ref, a_ref, b_ref, sum_a, sum_b)
-    apply_all(list_ref, list_ref[COUNT_AT], OWN, pair_ref, a_ref, b_ref, sum_a, sum_b)
+    apply_all(list_ref, list_ref[COUNT_AT], OWN, INNER_BATCH, pair_ref, a_ref, b_ref, sum_a, sum_b)
 
 
 def inner_apply(pair_list, geo, own, pairs):
@@ -577,7 +583,7 @@
     edge_geo = [geo_ref[a, INNER:TILES, :] for a in range(4)]
     moment = [edge_rows(before_ref, after_ref, c) for c in range(6)]
     prepare_moments(edge_geo, INNER, moment, a_ref, b_ref)
-    apply_all(list_ref, list_ref[COUNT_AT], 0, pair_ref, a_ref, b_ref, sum_a, sum_b)
+    apply_all(list_ref, list_ref[COUNT_AT], 0, OUTER_BATCH, pair_ref, a_ref, b_ref, sum_a, sum_b)
 
     fields = field_of([geo_ref[a, 0:INNER, :] for a in range(4)], sum_a, sum_b)
     moved = jnp.zeros((OWN, SLOTS), jnp.float32)
@@ -646,7 +652,7 @@
 def device_step(fractions, polarizability, occupancy, pair_mask, perm_field, history):
     plane = lax.axis_size("gy") * lax.axis_size("gz")
     line = lax.axis_size("gx")
-    stacked, gram, mine = prepare(
+    stacked, gram, both = prepare(
         fractions.reshape(3, OWN, SLOTS),
         polarizability.reshape(OWN, SLOTS),
         occupancy.reshape(OWN, SLOTS),
@@ -655,14 +661,15 @@
         pair_mask.reshape(OWN, OFFSETS),
         plane,
     )
+    both = settle(both)
     gram = exchange(gram, ("gy", "gz"))
     cells = joined(
         stacked.reshape(2, ROWS, 1, 2, SLOTS),
         "gx",
         2,
-        settle(stacked).reshape(2, ROWS, 1, 2, SLOTS),
-    )
-    mine = settle(mine)
+        both[: ROWS * OWN].reshape(2, ROWS, 1, 2, SLOTS),
+    )
+    mine = both[ROWS * OWN : (ROWS + 7) * OWN].reshape(7, OWN, SLOTS)
     cells = lax.optimization_barrier(cells)
     cells = joined(cells, "gy", 3)
     gram = sum_parts(gram, line)

time: 121 us -> 119 us (0.983)
  blocking collectives: 51.7 us -> 32.6 us
  waiting for transfers between devices: 4.85 us -> 13.8 us
  starting transfers between devices: 43.7 us -> 52.3 us
    all_to_all x3 -> x2, blocking collectives: 51.7 us -> 32.6 us  [exchange(): return lax.all_to_all(parts, axes, 0, 0)]
    all_to_all x1 -> x2, starting transfers between devices: 10.4 us -> 18.9 us  [exchange(): return lax.all_to_all(parts, axes, 0, 0)]
    all_to_all x1 -> x2, waiting for transfers between devices: 0.58 us -> 8.94 us  [exchange(): return lax.all_to_all(parts, axes, 0, 0)]
    ppermute x6, starting transfers between devices: 22.5 us -> 24.1 us  [both_ways(): lax.ppermute(low, axis, [((i + 1) % count, i) for i in range(count)])]
    ppermute x6, starting transfers between devices: 10.7 us -> 9.32 us  [both_ways(): lax.ppermute(high, axis, [(i, (i + 1) % count) for i in range(count)])]
  transfers between devices with their start and end apart: 13 -> 14, of which waited for: 7 -> 7; matrix products, arithmetic and copies ran while one was open for 2% -> 2% of each run, Pallas kernels for 7% -> 7%
where the time goes in v8:
time: 119 us; the launch traced here: 118 us
  starting transfers between devices  52.3 us (44%)
  blocking collectives  32.6 us (27%)
  Pallas kernels  16 us (13%)
  waiting for transfers between devices  13.8 us (12%)
  other arithmetic  2.02 us (2%)
    all_to_all x2, blocking collectives, exchange(): return lax.all_to_all(parts, axes, 0, 0)  32.6 us
    ppermute x6, starting transfers between devices, both_ways(): lax.ppermute(low, axis, [((i + 1) % count, i) for i in range(count)])  24.1 us
    all_to_all x2, starting transfers between devices, exchange(): return lax.all_to_all(parts, axes, 0, 0)  18.9 us
    ppermute x6, starting transfers between devices, both_ways(): lax.ppermute(high, axis, [(i, (i + 1) % count) for i in range(count)])  9.32 us
    all_to_all x2, waiting for transfers between devices, exchange(): return lax.all_to_all(parts, axes, 0, 0)  8.94 us
    pallas_call x1, Pallas kernels, inner_build(): pl.pallas_call(inner_build_kernel, name='inner_build', in_specs=[vmem_spe...  5.6 us
    pallas_call x1, Pallas kernels, first_field(): pl.pallas_call(first_kernel, name='first_field', in_specs=[vmem_spec()] *...  3.93 us
    ppermute x6, waiting for transfers between devices, both_ways(): lax.ppermute(low, axis, [((i + 1) % count, i) for i in range(count)])  2.77 us
  transfers between devices with their start and end apart: 14, of which 7 were waited for; matrix products, arithmetic and copies ran while one was open for 2% of the time, Pallas kernels for 7%

profile of v8, /device:TPU:1, one launch (start us, length us, event | category | flops | bytes accessed | tf_op | source)
XLA Modules:
  0.0 118.5 jit_solution(10797628225324124015)
XLA Ops:
  0.6 1.7 %prepare.1 = (f32[144,128]{1,0:T(8,128)}, f32[32,1,128]{2,1,0:T(1,128)}, f32[176,128]{1,0:T(8,128)}) custom-call(f32[3,4,128]{2,1,0:T(4,128)} %bitcast.41, f32[4,128]{1,0:T(4,128)} %bitcast.42, s32[4,128]{1,0:T(4,128)} %bitcast.43, f32[6,6,4,128]{3,2,1,0:T(4,128)} %bitcast.39, f32[6,4,128]{2,1,0:T(4,128)} %bitcast.40, s32[4,27]{1,0:T(4,128)} %bitcast.44), custom_call_target="tpu_custom_call" | custom-call | tf_op jit(solution)/shard_map/prepare/pallas_call | solution.py:368
  2.3 6.8 %collective-permute-start.1 = (f32[2,36,1,2,128]{4,3,2,1,0:T(2,128)}, f32[2,36,1,2,128]{4,3,2,1,0:T(2,128)S(1)}, u32[]{:S(2)}, u32[]{:S(2)}) collective-permute-start(f32[2,36,1,2,128]{4,3,2,1,0:T(2,128)} %bitcast.45), channel_id=1, source_target_pairs={{32,0},{64,32},{96,64},{128,96},{160,128},{192,160},{224,192},{256... | collective-permute-start | bytes 221192 | tf_op jit(solution)/shard_map/ppermute | solution.py:623
  9.2 0.0 collective-permute-start
  9.2 0.9 broadcast_maximum_fusion
  10.1 0.2 collective-permute-done.1
  10.3 0.6 collective-permute-done
  10.9 0.1 pad_maximum_fusion.1
  11.0 0.2 fusion.2
  11.2 1.9 %collective-permute-start.2 = (f32[2,36,3,1,128]{4,3,2,1,0:T(1,128)S(1)}, f32[2,36,3,1,128]{4,3,2,1,0:T(1,128)S(1)}, u32[]{:S(2)}, u32[]{:S(2)}) collective-permute-start(f32[2,36,3,1,128]{4,3,2,1,0:T(1,128)S(1)} %get-tuple-element.44), channel_id=1, source_target_pairs={{0,8},{8,16},{16,24},{24,0},{1,9},{9,17},{17,25},{25,1},{2,10},{10... | collective-permute-start | bytes 331784 | tf_op jit(solution)/shard_map/ppermute | solution.py:622
  13.1 4.6 %collective-permute-start.3 = (f32[2,36,3,1,128]{4,3,2,1,0:T(1,128)S(1)}, f32[2,36,3,1,128]{4,3,2,1,0:T(1,128)S(1)}, u32[]{:S(2)}, u32[]{:S(2)}) collective-permute-start(f32[2,36,3,1,128]{4,3,2,1,0:T(1,128)S(1)} %get-tuple-element.45), channel_id=1, source_target_pairs={{8,0},{16,8},{24,16},{0,24},{9,1},{17,9},{25,17},{1,25},{10,2},{18... | collective-permute-start | bytes 331784 | tf_op jit(solution)/shard_map/ppermute | solution.py:623
  17.7 8.5 %all-to-all-start = ((f32[32,1,128]{2,1,0:T(1,128)}), f32[32,1,128]{2,1,0:T(1,128)S(1)}, u32[]{:S(2)}, u32[]{:S(2)}) async-start(f32[32,1,128]{2,1,0:T(1,128)} %get-tuple-element.19), calls=%async_computation | async-start | bytes 32768 | tf_op jit(solution)/shard_map/all_to_all | solution.py:649
  26.2 0.0 collective-permute-done.2
  26.2 0.0 collective-permute-done.3
  26.2 0.3 pad_maximum_fusion
  26.6 4.4 %collective-permute-start.5 = (f32[1,36,3,4,128]{4,3,2,1,0:T(4,128)S(1)}, f32[1,36,3,4,128]{4,3,2,1,0:T(4,128)S(1)}, u32[]{:S(2)}, u32[]{:S(2)}) collective-permute-start(f32[1,36,3,4,128]{4,3,2,1,0:T(4,128)S(1)} %get-tuple-element.42), channel_id=1, source_target_pairs={{1,0},{2,1},{3,2},{4,3},{5,4},{6,5},{7,6},{0,7},{9,8},{10,9},{11,1... | collective-permute-start | bytes 663560 | tf_op jit(solution)/shard_map/ppermute | solution.py:623
  30.9 1.9 %collective-permute-start.4 = (f32[1,36,3,4,128]{4,3,2,1,0:T(4,128)S(1)}, f32[1,36,3,4,128]{4,3,2,1,0:T(4,128)S(1)}, u32[]{:S(2)}, u32[]{:S(2)}) collective-permute-start(f32[1,36,3,4,128]{4,3,2,1,0:T(4,128)S(1)} %get-tuple-element.43), channel_id=1, source_target_pairs={{0,1},{1,2},{2,3},{3,4},{4,5},{5,6},{6,7},{7,0},{8,9},{9,10},{10,1... | collective-permute-start | bytes 663560 | tf_op jit(solution)/shard_map/ppermute | solution.py:622
  32.9 2.0 %all-to-all-done = f32[32,1,128]{2,1,0:T(1,128)S(1)} async-done(((f32[32,1,128]{2,1,0:T(1,128)}), f32[32,1,128]{2,1,0:T(1,128)S(1)}, u32[]{:S(2)}, u32[]{:S(2)}) %all-to-all-start) | async-done | bytes 16416 | tf_op jit(solution)/shard_map/all_to_all | solution.py:649
  34.9 0.1 reduce_sum.27
  34.9 0.6 broadcast_in_dim.4
  35.5 10.4 %all-to-all-start.1 = ((f32[16,1,128]{2,1,0:T(1,128)}), f32[16,1,128]{2,1,0:T(1,128)S(1)}, u32[]{:S(2)}, u32[]{:S(2)}) async-start(f32[16,1,128]{2,1,0:T(1,128)} %broadcast_in_dim.4), calls=%async_computation.1 | async-start | bytes 16384 | tf_op jit(solution)/shard_map/all_to_all | solution.py:649
  46.0 7.0 %all-to-all-done.1.gram_ref = f32[16,1,128]{2,1,0:T(1,128)S(1)} async-done(((f32[16,1,128]{2,1,0:T(1,128)}), f32[16,1,128]{2,1,0:T(1,128)S(1)}, u32[]{:S(2)}, u32[]{:S(2)}) %all-to-all-start.1) | async-done | bytes 8224 | tf_op jit(solution)/shard_map/all_to_all | solution.py:649
  52.9 5.6 %inner_build.1 = (s32[128]{0:T(128)S(1)}, bf16[82,512,128]{2,1,0:T(8,128)(2,1)S(1)}, f32[6,4,128]{2,1,0:T(4,128)S(1)}, f32[5,128]{1,0:T(8,128)S(1)}, f32[4,96,12...) custom-call(f32[16,1,128]{2,1,0:T(1,128)S(1)} %all-to-all-done.1.gram_ref, f32[2,432,128]{2,1,0:T(8,128)S(1)} %bitcast.26), custom_call_target="tpu_custom_call" | custom-call | flops 2000000000 | bytes 1000000 | tf_op jit(solution)/shard_map/inner_build/pallas_call | solution.py:484
  58.5 0.0 collective-permute-done.5
  58.5 0.0 collective-permute-done.4
  58.5 3.9 %first_field.1 = (f32[24,128]{1,0:T(8,128)S(1)}, s32[128]{0:T(128)S(1)}, f32[4,48,128]{2,1,0:T(8,128)S(1)}, bf16[45,512,128]{2,1,0:T(8,128)(2,1)S(1)}) custom-call(f32[5,128]{1,0:T(8,128)S(1)} %get-tuple-element.22.coeffs_ref, f32[2,432,128]{2,1,0:T(8,128)S(1)} %bitcast.27, f32[432,128]{1,0:T(8,128)S(1)} %bitcast.37, f32[432,128]{1,0:T(8,128)S(1)} %bitcast.36, ...), custom_call_target="tpu_custom_call" | custom-call | flops 2000000000 | bytes 1000000 | tf_op jit(solution)/shard_map/first_field/pallas_call | solution.py:534
  62.5 1.8 %collective-permute-start.7 = (f32[2,6,1,2,128]{4,3,2,1,0:T(2,128)S(1)}, f32[2,6,1,2,128]{4,3,2,1,0:T(2,128)S(1)}, u32[]{:S(2)}, u32[]{:S(2)}) collective-permute-start(f32[2,6,1,2,128]{4,3,2,1,0:T(2,128)S(1)} %bitcast.30), channel_id=1, source_target_pairs={{32,0},{64,32},{96,64},{128,96},{160,128},{192,160},{224,192},{256... | collective-permute-start | bytes 36872 | tf_op jit(solution)/shard_map/ppermute | solution.py:623
  64.3 0.2 collective-permute-start.6
  64.5 1.4 %collective-permute-done.7 = f32[2,6,1,2,128]{4,3,2,1,0:T(2,128)S(1)} collective-permute-done((f32[2,6,1,2,128]{4,3,2,1,0:T(2,128)S(1)}, f32[2,6,1,2,128]{4,3,2,1,0:T(2,128)S(1)}, u32[]{:S(2)}, u32[]{:S(2)}) %collective-permute-start.7) | collective-permute-done | bytes 12320 | tf_op jit(solution)/shard_map/ppermute | solution.py:623
  65.8 0.0 collective-permute-done.6
  65.9 3.2 %collective-permute-start.8 = (f32[2,6,3,1,128]{4,3,2,1,0:T(1,128)S(1)}, f32[2,6,3,1,128]{4,3,2,1,0:T(1,128)S(1)}, u32[]{:S(2)}, u32[]{:S(2)}) collective-permute-start(f32[2,6,3,1,128]{4,3,2,1,0:T(1,128)S(1)} %get-tuple-element.48), channel_id=1, source_target_pairs={{0,8},{8,16},{16,24},{24,0},{1,9},{9,17},{17,25},{25,1},{2,10},{10... | collective-permute-start | bytes 55304 | tf_op jit(solution)/shard_map/ppermute | solution.py:622
  69.1 3.3 %collective-permute-start.9 = (f32[2,6,3,1,128]{4,3,2,1,0:T(1,128)S(1)}, f32[2,6,3,1,128]{4,3,2,1,0:T(1,128)S(1)}, u32[]{:S(2)}, u32[]{:S(2)}) collective-permute-start(f32[2,6,3,1,128]{4,3,2,1,0:T(1,128)S(1)} %get-tuple-element.49), channel_id=1, source_target_pairs={{8,0},{16,8},{24,16},{0,24},{9,1},{17,9},{25,17},{1,25},{10,2},{18... | collective-permute-start | bytes 55304 | tf_op jit(solution)/shard_map/ppermute | solution.py:623
  72.4 0.0 collective-permute-done.8
  72.4 1.2 %collective-permute-done.9 = f32[2,6,3,1,128]{4,3,2,1,0:T(1,128)S(1)} collective-permute-done((f32[2,6,3,1,128]{4,3,2,1,0:T(1,128)S(1)}, f32[2,6,3,1,128]{4,3,2,1,0:T(1,128)S(1)}, u32[]{:S(2)}, u32[]{:S(2)}) %collective-permute-start.9) | collective-permute-done | bytes 18464 | tf_op jit(solution)/shard_map/ppermute | solution.py:623
  73.6 0.1 pad_maximum_fusion.2
  73.7 3.2 %collective-permute-start.11 = (f32[1,6,3,4,128]{4,3,2,1,0:T(4,128)S(1)}, f32[1,6,3,4,128]{4,3,2,1,0:T(4,128)S(1)}, u32[]{:S(2)}, u32[]{:S(2)}) collective-permute-start(f32[1,6,3,4,128]{4,3,2,1,0:T(4,128)S(1)} %get-tuple-element.46), channel_id=1, source_target_pairs={{1,0},{2,1},{3,2},{4,3},{5,4},{6,5},{7,6},{0,7},{9,8},{10,9},{11,1... | collective-permute-start | bytes 110600 | tf_op jit(solution)/shard_map/ppermute | solution.py:623
  76.9 2.1 %collective-permute-start.10 = (f32[1,6,3,4,128]{4,3,2,1,0:T(4,128)S(1)}, f32[1,6,3,4,128]{4,3,2,1,0:T(4,128)S(1)}, u32[]{:S(2)}, u32[]{:S(2)}) collective-permute-start(f32[1,6,3,4,128]{4,3,2,1,0:T(4,128)S(1)} %get-tuple-element.47), channel_id=1, source_target_pairs={{0,1},{1,2},{2,3},{3,4},{4,5},{5,6},{6,7},{7,0},{8,9},{9,10},{10,1... | collective-permute-start | bytes 110600 | tf_op jit(solution)/shard_map/ppermute | solution.py:622
  79.0 2.3 %inner_apply.1 = (f32[4,96,128]{2,1,0:T(8,128)S(1)}, f32[4,24,128]{2,1,0:T(8,128)S(1)}) custom-call(s32[128]{0:T(128)S(1)} %get-tuple-element.30.list_ref, f32[4,48,128]{2,1,0:T(8,128)S(1)} %get-tuple-element.27.geo_ref, f32[2,72,128]{2,1,0:T(8,128)S(1)} %bitcast.28, bf16[82,512,128]{2,1,0:T(8,128)(2,1)S(1)} %get-tuple-element.31.pair_ref), custom_call_target="tpu_custom_call" | custom-call | flops 1000000000 | bytes 1000000 | tf_op jit(solution)/shard_map/inner_apply/pallas_call | solution.py:565
  81.3 0.0 collective-permute-done.11
  81.3 1.5 %collective-permute-done.10 = f32[1,6,3,4,128]{4,3,2,1,0:T(4,128)S(1)} collective-permute-done((f32[1,6,3,4,128]{4,3,2,1,0:T(4,128)S(1)}, f32[1,6,3,4,128]{4,3,2,1,0:T(4,128)S(1)}, u32[]{:S(2)}, u32[]{:S(2)}) %collective-permute-start.10) | collective-permute-done | bytes 36896 | tf_op jit(solution)/shard_map/ppermute | solution.py:622
  82.8 2.4 %second_field.1 = (f32[6,4,128]{2,1,0:T(4,128)}, f32[32,2,128]{2,1,0:T(2,128)S(1)}) custom-call(s32[128]{0:T(128)S(1)} %get-tuple-element.26.list_ref, f32[4,48,128]{2,1,0:T(8,128)S(1)} %get-tuple-element.27.geo_ref, f32[2,72,128]{2,1,0:T(8,128)S(1)} %bitcast.29, f32[72,128]{1,0:T(8,128)S(1)} %bitcast.35, f32[72,128]{1,0:T(8,128)S(1)} %bitcast.34, ...), custom_call_target="tpu_custom_call" | custom-call | flops 1000000000 | bytes 1000000 | tf_op jit(solution)/shard_map/second_field/pallas_call | solution.py:605
  85.3 14.6 %all_to_all.20 = f32[32,2,128]{2,1,0:T(2,128)S(1)} all-to-all(f32[32,2,128]{2,1,0:T(2,128)S(1)} %get-tuple-element.35), channel_id=1, replica_groups=mesh['gx'=16,'gy'=4,'gz'=8] {'gy','gz'}, dimensions={0} | all-to-all | bytes 65536 | tf_op jit(solution)/shard_map/all_to_all | solution.py:649
  99.9 18.0 %all_to_all.21 = f32[16,2,128]{2,1,0:T(2,128)S(1)} all-to-all(f32[16,2,128]{2,1,0:T(2,128)S(1)} %broadcast_in_dim.5), channel_id=1, replica_groups=mesh['gx'=16,'gy'=4,'gz'=8] {'gx'}, dimensions={0} | all-to-all | bytes 32768 | tf_op jit(solution)/shard_map/all_to_all | solution.py:649
  118.0 0.5 fusion
  (10 shorter events, 0.2 us)
Async XLA Ops:
  2.3 8.0 %collective-permute-start.1 = (f32[2,36,1,2,128]{4,3,2,1,0:T(2,128)}, f32[2,36,1,2,128]{4,3,2,1,0:T(2,128)S(1)}, u32[]{:S(2)}, u32[]{:S(2)}) collective-permute-start(f32[2,36,1,2,128]{4,3,2,1,0:T(2,128)} %bitcast.45), channel_id=1, source_target_pairs={{32,0},{64,32},{96,64},{128,96},{160,128},{192,160},{224,192},{256... | collective-permute-start | bytes 221192 | tf_op jit(solution)/shard_map/ppermute | solution.py:623
  9.2 1.7 %collective-permute-start = (f32[2,36,1,2,128]{4,3,2,1,0:T(2,128)}, f32[2,36,1,2,128]{4,3,2,1,0:T(2,128)S(1)}, u32[]{:S(2)}, u32[]{:S(2)}) collective-permute-start(f32[2,36,1,2,128]{4,3,2,1,0:T(2,128)} %bitcast.46), channel_id=1, source_target_pairs={{0,32},{32,64},{64,96},{96,128},{128,160},{160,192},{192,224},{224... | collective-permute-start | bytes 221192 | tf_op jit(solution)/shard_map/ppermute | solution.py:622
  11.2 15.0 %collective-permute-start.2 = (f32[2,36,3,1,128]{4,3,2,1,0:T(1,128)S(1)}, f32[2,36,3,1,128]{4,3,2,1,0:T(1,128)S(1)}, u32[]{:S(2)}, u32[]{:S(2)}) collective-permute-start(f32[2,36,3,1,128]{4,3,2,1,0:T(1,128)S(1)} %get-tuple-element.44), channel_id=1, source_target_pairs={{0,8},{8,16},{16,24},{24,0},{1,9},{9,17},{17,25},{25,1},{2,10},{10... | collective-permute-start | bytes 331784 | tf_op jit(solution)/shard_map/ppermute | solution.py:622
  13.1 13.1 %collective-permute-start.3 = (f32[2,36,3,1,128]{4,3,2,1,0:T(1,128)S(1)}, f32[2,36,3,1,128]{4,3,2,1,0:T(1,128)S(1)}, u32[]{:S(2)}, u32[]{:S(2)}) collective-permute-start(f32[2,36,3,1,128]{4,3,2,1,0:T(1,128)S(1)} %get-tuple-element.45), channel_id=1, source_target_pairs={{8,0},{16,8},{24,16},{0,24},{9,1},{17,9},{25,17},{1,25},{10,2},{18... | collective-permute-start | bytes 331784 | tf_op jit(solution)/shard_map/ppermute | solution.py:623
  17.7 17.2 %all-to-all-start = ((f32[32,1,128]{2,1,0:T(1,128)}), f32[32,1,128]{2,1,0:T(1,128)S(1)}, u32[]{:S(2)}, u32[]{:S(2)}) async-start(f32[32,1,128]{2,1,0:T(1,128)} %get-tuple-element.19), calls=%async_computation | async-start | bytes 32768 | tf_op jit(solution)/shard_map/all_to_all | solution.py:649
  26.6 31.9 %collective-permute-start.5 = (f32[1,36,3,4,128]{4,3,2,1,0:T(4,128)S(1)}, f32[1,36,3,4,128]{4,3,2,1,0:T(4,128)S(1)}, u32[]{:S(2)}, u32[]{:S(2)}) collective-permute-start(f32[1,36,3,4,128]{4,3,2,1,0:T(4,128)S(1)} %get-tuple-element.42), channel_id=1, source_target_pairs={{1,0},{2,1},{3,2},{4,3},{5,4},{6,5},{7,6},{0,7},{9,8},{10,9},{11,1... | collective-permute-start | bytes 663560 | tf_op jit(solution)/shard_map/ppermute | solution.py:623
  30.9 27.6 %collective-permute-start.4 = (f32[1,36,3,4,128]{4,3,2,1,0:T(4,128)S(1)}, f32[1,36,3,4,128]{4,3,2,1,0:T(4,128)S(1)}, u32[]{:S(2)}, u32[]{:S(2)}) collective-permute-start(f32[1,36,3,4,128]{4,3,2,1,0:T(4,128)S(1)} %get-tuple-element.43), channel_id=1, source_target_pairs={{0,1},{1,2},{2,3},{3,4},{4,5},{5,6},{6,7},{7,0},{8,9},{9,10},{10,1... | collective-permute-start | bytes 663560 | tf_op jit(solution)/shard_map/ppermute | solution.py:622
  35.5 17.4 %all-to-all-start.1 = ((f32[16,1,128]{2,1,0:T(1,128)}), f32[16,1,128]{2,1,0:T(1,128)S(1)}, u32[]{:S(2)}, u32[]{:S(2)}) async-start(f32[16,1,128]{2,1,0:T(1,128)} %broadcast_in_dim.4), calls=%async_computation.1 | async-start | bytes 16384 | tf_op jit(solution)/shard_map/all_to_all | solution.py:649
  62.5 3.4 %collective-permute-start.7 = (f32[2,6,1,2,128]{4,3,2,1,0:T(2,128)S(1)}, f32[2,6,1,2,128]{4,3,2,1,0:T(2,128)S(1)}, u32[]{:S(2)}, u32[]{:S(2)}) collective-permute-start(f32[2,6,1,2,128]{4,3,2,1,0:T(2,128)S(1)} %bitcast.30), channel_id=1, source_target_pairs={{32,0},{64,32},{96,64},{128,96},{160,128},{192,160},{224,192},{256... | collective-permute-start | bytes 36872 | tf_op jit(solution)/shard_map/ppermute | solution.py:623
  64.3 1.5 %collective-permute-start.6 = (f32[2,6,1,2,128]{4,3,2,1,0:T(2,128)S(1)}, f32[2,6,1,2,128]{4,3,2,1,0:T(2,128)S(1)}, u32[]{:S(2)}, u32[]{:S(2)}) collective-permute-start(f32[2,6,1,2,128]{4,3,2,1,0:T(2,128)S(1)} %bitcast.31), channel_id=1, source_target_pairs={{0,32},{32,64},{64,96},{96,128},{128,160},{160,192},{192,224},{224... | collective-permute-start | bytes 36872 | tf_op jit(solution)/shard_map/ppermute | solution.py:622
  65.9 6.5 %collective-permute-start.8 = (f32[2,6,3,1,128]{4,3,2,1,0:T(1,128)S(1)}, f32[2,6,3,1,128]{4,3,2,1,0:T(1,128)S(1)}, u32[]{:S(2)}, u32[]{:S(2)}) collective-permute-start(f32[2,6,3,1,128]{4,3,2,1,0:T(1,128)S(1)} %get-tuple-element.48), channel_id=1, source_target_pairs={{0,8},{8,16},{16,24},{24,0},{1,9},{9,17},{17,25},{25,1},{2,10},{10... | collective-permute-start | bytes 55304 | tf_op jit(solution)/shard_map/ppermute | solution.py:622
  69.1 4.5 %collective-permute-start.9 = (f32[2,6,3,1,128]{4,3,2,1,0:T(1,128)S(1)}, f32[2,6,3,1,128]{4,3,2,1,0:T(1,128)S(1)}, u32[]{:S(2)}, u32[]{:S(2)}) collective-permute-start(f32[2,6,3,1,128]{4,3,2,1,0:T(1,128)S(1)} %get-tuple-element.49), channel_id=1, source_target_pairs={{8,0},{16,8},{24,16},{0,24},{9,1},{17,9},{25,17},{1,25},{10,2},{18... | collective-permute-start | bytes 55304 | tf_op jit(solution)/shard_map/ppermute | solution.py:623
  73.7 7.6 %collective-permute-start.11 = (f32[1,6,3,4,128]{4,3,2,1,0:T(4,128)S(1)}, f32[1,6,3,4,128]{4,3,2,1,0:T(4,128)S(1)}, u32[]{:S(2)}, u32[]{:S(2)}) collective-permute-start(f32[1,6,3,4,128]{4,3,2,1,0:T(4,128)S(1)} %get-tuple-element.46), channel_id=1, source_target_pairs={{1,0},{2,1},{3,2},{4,3},{5,4},{6,5},{7,6},{0,7},{9,8},{10,9},{11,1... | collective-permute-start | bytes 110600 | tf_op jit(solution)/shard_map/ppermute | solution.py:623
  76.9 5.9 %collective-permute-start.10 = (f32[1,6,3,4,128]{4,3,2,1,0:T(4,128)S(1)}, f32[1,6,3,4,128]{4,3,2,1,0:T(4,128)S(1)}, u32[]{:S(2)}, u32[]{:S(2)}) collective-permute-start(f32[1,6,3,4,128]{4,3,2,1,0:T(4,128)S(1)} %get-tuple-element.47), channel_id=1, source_target_pairs={{0,1},{1,2},{2,3},{3,4},{4,5},{5,6},{6,7},{7,0},{8,9},{9,10},{10,1... | collective-permute-start | bytes 110600 | tf_op jit(solution)/shard_map/ppermute | solution.py:622
